TPU v7x, 32 devices: a whole 2x2x4 slice. The times are simulated.
32 devices in a mesh: feat: 8 (over y, x, core), rep: 4 (over z).
Axes of the slice: x: 2, y: 2, z: 4, core: 2. Of those that a mesh axis runs over, the one named last changes fastest.
Arguments:
- features: bfloat16 [4, 8, 1024, 512], P('rep', None, 'feat'), may hold values from -6 to 6
- adjacency_one: int32 [4, 8, 5, 16, 512], P('rep'), may hold values from 0 to 65535, as said below
- pre_hidden: bfloat16 [4, 8, 256, 256], P('rep', 'feat'), may hold values from -6 to 6
- adjacency_two: int32 [4, 8, 5, 8, 256], P('rep', 'feat'), may hold values from 0 to 65535, as said below
- weight_two: bfloat16 [6, 256, 256], replicated, may hold values from -0.375 to 0.375
- out_grad: bfloat16 [4, 8, 128, 256], P('rep', 'feat'), may hold values from -6 to 6
Outputs:
- grad_w1: float32 [6, 1024, 256], P(None, 'feat')
- grad_b1: float32 [256], replicated
- grad_w2: float32 [6, 256, 256], replicated
- grad_b2: float32 [256], replicated
Inputs may be any that keep to these rules, and one draw needn't show every extreme that they name: `adjacency_one`: bit k, k below 16, of word (w, n) is the entry of destination row 16 w + k and source column n; higher bits are zero; some rows are empty. `adjacency_two`: bit k, k below 16, of word (w, n) is the entry of seed row 16 w + k and source column n; higher bits are zero; some rows are empty.
All inputs are finite; a program needn't handle non-finite values.
Results may differ from a plain program's by a relative error of at most 0.0041.
Values may be sent and summed in bfloat16 or wider, within the bound.
No kernel may reach another device: no remote copies, remote signals or barrier semaphores. Data moves between devices by JAX's collectives and lax.ppermute only.
A program may use at most 128 MiB of HBM per device.

v0:
```python
import functools

import jax
import jax.numpy as jnp
from jax import lax
from jax.experimental import pallas as pl
from jax.experimental.pallas import tpu as pltpu
from jax.sharding import PartitionSpec as P


BITS = 16
BIAS_ROWS = 16
LOADED = range(6)
F32 = jnp.float32
BF16 = jnp.bfloat16
NT = (((1,), (1,)), ((), ()))
TN = (((0,), (0,)), ((), ()))
VMEM = pl.BlockSpec(memory_space=pltpu.VMEM)


def dot(a, b, dims=(((1,), (0,)), ((), ()))):
    return lax.dot_general(a, b, dims, preferred_element_type=F32)


def reorder(rows):
    words = rows // BITS
    out = lax.broadcasted_iota(jnp.int32, (rows, rows), 0)
    src = lax.broadcasted_iota(jnp.int32, (rows, rows), 1)
    return jnp.where(src == BITS * (out % words) + out // words, 1.0, 0.0).astype(BF16)


def bits_two(words):
    count, cols = words.shape
    shifts = lax.broadcasted_iota(jnp.int32, (BITS, count, cols), 0)
    spread = jnp.bitwise_and(jnp.right_shift(words[None], shifts), 1)
    return spread.astype(F32).reshape(BITS * count, cols)


def split_rows(value):
    high = value.astype(BF16)
    return high.astype(F32), (value - high.astype(F32)).astype(BF16).astype(F32)


def pack_rows(*values):
    row = lax.broadcasted_iota(jnp.int32, (BIAS_ROWS, values[0].shape[1]), 0)
    packed = jnp.zeros(row.shape, F32)
    place = 0
    for value in values:
        for part in split_rows(value):
            packed = jnp.where(row == place, part, packed)
            place += 1
    return packed.astype(BF16)


def read_row(packed, place):
    rows = packed.astype(F32)
    return rows[2 * place : 2 * place + 1] + rows[2 * place + 1 : 2 * place + 2]


def upper_kernel(factor, core_of, *refs):
    count = len(LOADED)
    sources, own_ref, send_ref = refs[:count], refs[count], refs[count + 1]
    targets, (sums, sems) = refs[count + 2 : 2 * count + 2], refs[2 * count + 2 :]
    grad_ref, words_ref, pre_ref = targets[:3]
    copies = [
        pltpu.make_async_copy(source, target, sems.at[n])
        for n, (source, target) in enumerate(zip(sources, targets))
    ]
    for copy in copies:
        copy.start()
    for copy in copies[:3]:
        copy.wait()
    relations = words_ref.shape[0]
    seeds, width = grad_ref.shape
    scaled = grad_ref[...].astype(F32) * factor
    low = scaled.astype(BF16)
    low_bits = dot(reorder(seeds), low).astype(BF16)
    hidden = jnp.maximum(pre_ref[...].astype(F32), 0.0).astype(BF16)
    parts = sums.shape[0]
    rows = sums.shape[1]
    height = hidden.shape[1]
    per = rows // height
    for r in range(relations + 1):
        if r == 0:
            value = dot(hidden[:seeds], low, TN)
        else:
            matrix = bits_two(words_ref[r - 1])
            inverse = 1.0 / jnp.maximum(jnp.sum(matrix, axis=1, keepdims=True), 1.0)
            mixed = (dot(matrix.astype(BF16), hidden) * inverse).astype(BF16)
            value = dot(mixed, low_bits, TN)
        sums[r // per, (r % per) * height : (r % per + 1) * height] = value
    core = core_of()
    own_ref[:rows] = sums[core]
    other = 0 if parts == 1 else 1 - core
    send_ref[:rows] = sums[other]
    bias = jnp.sum(scaled, 0, keepdims=True)
    own_ref[rows:] = jnp.broadcast_to(bias, (BIAS_ROWS, width))
    send_ref[rows:] = jnp.broadcast_to(bias, (BIAS_ROWS, width))
    for copy in copies[3:]:
        copy.wait()


def hidden_kernel(factor, pre_ref, words_ref, weight_ref, grad_ref, hidden_ref):
    relations = words_ref.shape[0]
    seeds = grad_ref.shape[0]
    pre = pre_ref[...]
    low = (grad_ref[...].astype(F32) * factor).astype(BF16)
    low_bits = dot(reorder(seeds), low).astype(BF16)
    total = None
    for r in range(relations):
        matrix = bits_two(words_ref[r])
        inverse = 1.0 / jnp.maximum(jnp.sum(matrix, axis=1, keepdims=True), 1.0)
        back = (dot(low_bits, weight_ref[r + 1], NT) * inverse).astype(BF16)
        part = dot(matrix.astype(BF16), back, TN)
        total = part if total is None else total + part
    own = dot(low, weight_ref[0], NT)
    rest = total.shape[0] - seeds
    total = total + jnp.concatenate([own, jnp.zeros((rest, own.shape[1]), F32)], 0)
    hidden_grad = jnp.where(pre.astype(F32) > 0, total, 0.0).astype(BF16)
    hidden_ref[...] = dot(reorder(total.shape[0]), hidden_grad).astype(BF16)


def pair_kernel(chip_of, own_ref, got_ref, *refs):
    outs, sums = refs[:-1], refs[-1]
    chips, rows, width = sums.shape
    height = chips * rows
    total = own_ref[:height] + got_ref[:height]
    sums[...] = total.reshape(chips, rows, width)
    bias = own_ref[height:] + got_ref[height:]
    packed = pack_rows(bias[0:1])
    chip = chip_of()
    outs[0][:rows] = sums[chip]
    outs[0][rows:] = packed.astype(F32)
    for k in range(1, chips):
        outs[k][:rows] = sums[lax.bitwise_xor(chip, k)].astype(BF16)
        outs[k][rows:] = packed


def gather_kernel(first, count, column_ref, word_ref, out_ref, wide):
    width, nodes = column_ref.shape[1:]
    relations, words = word_ref.shape[1:3]
    rows = words * BITS
    select = reorder(rows)
    wide[width:] = jnp.ones((wide.shape[0] - width, nodes), BF16)
    bit = lax.broadcasted_iota(jnp.int32, (1, rows), 1) // words
    power = lax.shift_left(jnp.int32(1), BITS - 1 - bit).astype(F32) * 2.0 ** (1 - BITS)

    def batch(b):
        column = column_ref[first + b]
        wide[:width] = column
        place = pl.ds(pl.multiple_of(b * rows, rows), rows)
        out_ref[:width, place] = dot(column[:, :rows], select, NT).astype(BF16)
        for r in range(relations):
            word = word_ref[first + b, r]
            matrix = jnp.concatenate(
                [jnp.bitwise_and(word, 1 << k).astype(F32).astype(BF16) for k in range(BITS)], 0
            )
            value = dot(wide[...], matrix, NT)
            total = value[width : width + 1] * power
            scale = power / jnp.maximum(total, 1.0)
            out_ref[(r + 1) * width : (r + 2) * width, place] = (value[:width] * scale).astype(BF16)

    if count <= 4:
        for b in range(count):
            batch(b)
    else:
        lax.fori_loop(0, count, lambda b, unused: (batch(b), unused)[1], 0)


def panel_kernel(taker, order, parts, *refs):
    gathered, refs = refs[:parts], refs[parts:]
    blocks, (bias_ref, own_ref, *outs) = refs[: len(order)], refs[len(order) : -2]
    stack, sums = refs[-2:]
    height = blocks[0].shape[0]
    for block, place in zip(blocks, order):
        start = pl.multiple_of(place() * height, height)
        stack[pl.ds(start, height)] = block[...]
    deep = gathered[0].shape[1]
    total = dot(gathered[0][...], stack[:deep])
    for n in range(1, parts):
        total = total + dot(gathered[n][...], stack[n * deep : (n + 1) * deep])
    sums[...] = total.reshape(sums.shape)
    reps = sums.shape[0]
    bias_ref[...] = jnp.sum(stack[...].astype(F32), 0, keepdims=True)
    own_ref[...] = sums[taker(0)]
    for k in range(1, reps):
        outs[k - 1][...] = sums[taker(k)].astype(BF16)


def call(body, outs, scratch=(), flops=1000000, vmem=8, **keys):
    return pl.pallas_call(
        body,
        out_shape=outs,
        scratch_shapes=list(scratch),
        compiler_params=pltpu.CompilerParams(vmem_limit_bytes=vmem * 1024 * 1024),
        cost_estimate=pl.CostEstimate(flops=flops, bytes_accessed=1000000, transcendentals=0),
        **keys,
    )


def shape(rows, cols, dtype):
    return jax.ShapeDtypeStruct((rows, cols), dtype)


def plane_sum_kernel(chip_of, bias_ref, own_ref, *refs):
    got, out, slots = refs[:-2], refs[-2], refs[-1]
    rows = out.shape[0] - BIAS_ROWS
    chip = chip_of()
    total = own_ref[:rows]
    slots[chip] = own_ref[rows:]
    for k, piece in enumerate(got, 1):
        total = total + piece[:rows].astype(F32)
        slots[lax.bitwise_xor(chip, k)] = piece[rows:].astype(F32)
    out[:rows] = total
    bias = read_row(slots[0], 0)
    for j in range(1, slots.shape[0]):
        bias = bias + read_row(slots[j], 0)
    row = lax.broadcasted_iota(jnp.int32, (BIAS_ROWS, bias.shape[1]), 0)
    out[rows:] = jnp.where(row == 0, bias_ref[...], bias)


def rep_pair_kernel(mine_ref, got_ref, out_ref):
    rows = out_ref.shape[0] - BIAS_ROWS
    out_ref[:rows] = (mine_ref[:rows] + got_ref[:rows]).astype(BF16)
    bias = mine_ref[rows:] + got_ref[rows:]
    out_ref[rows:] = pack_rows(bias[0:1], bias[1:2])


def rep_more_kernel(mine_ref, got_ref, out_ref):
    rows = out_ref.shape[0] - BIAS_ROWS
    out_ref[:rows] = (mine_ref[:rows].astype(F32) + got_ref[:rows].astype(F32)).astype(BF16)
    mine, got = mine_ref[rows:], got_ref[rows:]
    out_ref[rows:] = pack_rows(
        read_row(mine, 0) + read_row(got, 0), read_row(mine, 1) + read_row(got, 1)
    )


def finish_kernel(mine_ref, got_ref, upper_ref, one_ref, two_ref):
    rows = upper_ref.shape[0]
    upper_ref[...] = (mine_ref[:rows].astype(F32) + got_ref[:rows].astype(F32)).astype(BF16)
    mine, got = mine_ref[rows:], got_ref[rows:]
    one_ref[...] = read_row(mine, 0) + read_row(got, 0)
    two_ref[...] = read_row(mine, 1) + read_row(got, 1)


def panel_sum_kernel(own_ref, *refs):
    total = own_ref[...]
    for piece in refs[:-1]:
        total = total + piece[...].astype(F32)
    refs[-1][...] = total.astype(BF16)


def layers(blocks):
    for block in blocks:
        if len(block.shape) == 2:
            yield block[...]
        else:
            for n in range(block.shape[0]):
                yield block[n]


def pack_kernel(*refs):
    for n, value in enumerate(layers(refs[:-1])):
        refs[-1][n] = value


def place_kernel(order, *refs):
    for value, place in zip(layers(refs[:-1]), order):
        refs[-1][place()] = value.astype(F32)


def on_device(features, adjacency_one, pre_hidden, adjacency_two, weight_two, out_grad):
    feat = lax.axis_size("feat")
    reps = lax.axis_size("rep")
    pre, words_two, grad = pre_hidden[0, 0], adjacency_two[0, 0], out_grad[0, 0]
    columns, words_one = features[0], adjacency_one[0]
    batches, width, nodes = columns.shape
    relations, words = words_one.shape[1:3]
    rows_one = words * BITS
    hidden_rows, hidden_width = pre.shape
    seeds = grad.shape[0]
    factor = float(seeds * feat * reps) ** (-0.5)
    sets = relations + 1
    cores = 2
    chips = feat // cores
    direct = feat <= 8 and feat % cores == 0 and chips & (chips - 1) == 0

    def core_of():
        return lax.axis_index("feat") % cores

    def chip_of():
        return lax.axis_index("feat") // cores

    def in_hbm(value):
        return pltpu.with_memory_space_constraint(value, pltpu.HBM)

    loaded = (grad, words_two, pre, weight_two, words_one, columns)
    upper_rows = sets * hidden_width
    half = upper_rows // cores if direct else upper_rows
    own_half, send_half, grad, words_two, pre, weight_two, words_one, columns = call(
        functools.partial(upper_kernel, factor, core_of if direct else lambda: 0),
        (shape(half + BIAS_ROWS, hidden_width, F32),) * 2
        + tuple(jax.ShapeDtypeStruct(v.shape, v.dtype) for v in loaded),
        [
            pltpu.VMEM((upper_rows // half, half, hidden_width), F32),
            pltpu.SemaphoreType.DMA((len(loaded),)),
        ],
        vmem=8 + sum(v.size * v.dtype.itemsize for v in loaded) // 2**20,
        in_specs=[pl.BlockSpec(memory_space=pltpu.HBM)] * len(loaded),
    )(*map(in_hbm, loaded))
    hidden = call(
        functools.partial(hidden_kernel, factor), shape(hidden_rows, hidden_width, BF16)
    )(pre, words_two, weight_two, grad)

    parts = 2 if batches % 2 == 0 else 1
    run = batches // parts
    gathered = []
    for n in range(parts):
        gathered.append(
            call(
                functools.partial(gather_kernel, n * run, run),
                shape(sets * width, run * rows_one, BF16),
                (pltpu.VMEM((width + 16, nodes), BF16),),
                flops=3000000000,
                vmem=12 + 2 * words_one.size * 4 // 2**20,
            )(columns, words_one)
        )

    def to_chip(value, k):
        pairs = [(i, (i // cores ^ k) * cores + i % cores) for i in range(feat)]
        return lax.ppermute(value, "feat", pairs)

    def to_core(value):
        return lax.ppermute(value, "feat", [(i, i ^ 1) for i in range(feat)])

    flip = reps & (reps - 1) == 0

    def giver(k):
        rep = lax.axis_index("rep")
        return lax.bitwise_xor(rep, jnp.int32(k)) if flip else (rep + reps - k) % reps

    def taker(k):
        rep = lax.axis_index("rep")
        return lax.bitwise_xor(rep, jnp.int32(k)) if flip else (rep + k) % reps

    def to_rep(value, k):
        pairs = [(i, (i ^ k) if flip else (i + k) % reps) for i in range(reps)]
        return lax.ppermute(value, "rep", pairs)

    piece = half // chips
    share = sets * width // reps

    if direct:
        blocks = [hidden] + [to_chip(hidden, k) for k in range(1, chips)]
        blocks = blocks + [to_core(block) for block in blocks]
        order = []
        for flip in range(cores):
            for k in range(chips):
                order.append(
                    lambda flip=flip, k=k: lax.bitwise_xor(
                        lax.axis_index("feat"), jnp.int32(k * cores + flip)
                    )
                )
        got_half = to_core(send_half)
        tall = piece + BIAS_ROWS
        pieces = call(
            functools.partial(pair_kernel, chip_of),
            (shape(tall, hidden_width, F32),) + (shape(tall, hidden_width, BF16),) * (chips - 1),
            (pltpu.VMEM((chips, piece, hidden_width), F32),),
        )(own_half, got_half)
        got = [to_chip(pieces[k], k) for k in range(1, chips)]
    else:
        blocks = [lax.all_gather(hidden, "feat", axis=0, tiled=True)]
        order = [lambda: 0]

    stack_bytes = batches * rows_one * (hidden_width + sets * width) * 2
    bias_one, *panels = call(
        functools.partial(panel_kernel, taker, order, parts),
        (shape(1, hidden_width, F32), shape(share, hidden_width, F32))
        + (shape(share, hidden_width, BF16),) * (reps - 1),
        (
            pltpu.VMEM((batches * rows_one, hidden_width), BF16),
            pltpu.VMEM((reps, share, hidden_width), F32),
        ),
        vmem=8 + 2 * stack_bytes // 2**20,
    )(*gathered, *blocks)
    got_panel = [to_rep(panels[k], k) for k in range(1, reps)]
    if direct:
        mine = call(
            functools.partial(plane_sum_kernel, chip_of),
            shape(piece + BIAS_ROWS, hidden_width, F32),
            (pltpu.VMEM((chips, BIAS_ROWS, hidden_width), F32),),
        )(bias_one, pieces[0], *got)
    else:
        summed = lax.psum(own_half, "feat")
        mine = jnp.concatenate([summed[:half], bias_one, summed[half + 1 :]], 0)
    tall = mine.shape[0]
    if flip and reps > 2:
        got_upper = to_rep(mine, 1)
        mine = call(rep_pair_kernel, shape(tall, hidden_width, BF16))(mine, got_upper)
        k = 2
        while k < reps // 2:
            got_upper = to_rep(mine, k)
            mine = call(rep_more_kernel, shape(tall, hidden_width, BF16))(mine, got_upper)
            k *= 2
        got_upper = to_rep(mine, k)
        upper, bias_one, bias_two = call(
            finish_kernel,
            (
                shape(tall - BIAS_ROWS, hidden_width, BF16),
                shape(1, hidden_width, F32),
                shape(1, hidden_width, F32),
            ),
        )(mine, got_upper)
    else:
        mine = lax.psum(mine, "rep")
        upper = mine[:-BIAS_ROWS].astype(BF16)
        bias_one, bias_two = mine[-BIAS_ROWS:][0:1], mine[-BIAS_ROWS:][1:2]
    panel = call(panel_sum_kernel, shape(share, hidden_width, BF16))(panels[0], *got_panel)

    if flip:
        panel_all, near = [panel], [panel]
        held = [0]
        k = reps // 2
        while k:
            if len(panel_all) > 1:
                packed = call(
                    pack_kernel,
                    jax.ShapeDtypeStruct((len(held), share, hidden_width), BF16),
                )(*near)
            else:
                packed = panel[None]
            came = to_rep(packed, k)
            near = near + [came]
            panel_all = near
            held = held + [h ^ k for h in held]
            k //= 2
    else:
        panel_all = [panel] + [to_rep(panel, k) for k in range(1, reps)]
        held = list(range(reps))
    grad_w1 = call(
        functools.partial(place_kernel, [functools.partial(giver, k) for k in held]),
        jax.ShapeDtypeStruct((reps, share, hidden_width), F32),
    )(*panel_all)
    grad_w1 = grad_w1.reshape(sets, width, hidden_width)
    if direct:
        upper_all = [upper] + [to_chip(upper, k) for k in range(1, chips)]
        upper_all = upper_all + [to_core(u) for u in upper_all]
        places = []
        for flip in range(cores):
            for k in range(chips):
                places.append(
                    lambda flip=flip, k=k: lax.bitwise_xor(core_of(), jnp.int32(flip)) * chips
                    + lax.bitwise_xor(chip_of(), jnp.int32(k))
                )
        grad_w2 = call(
            functools.partial(place_kernel, places),
            jax.ShapeDtypeStruct((feat, piece, hidden_width), F32),
        )(*upper_all)
    else:
        grad_w2 = upper.astype(F32)
    grad_w2 = grad_w2.reshape(sets, hidden_width, hidden_width)
    return (grad_w1, bias_one[0], grad_w2, bias_two[0])


def solution(mesh):
    placed = (
        P("rep", None, "feat", None),
        P("rep", None, None, None, None),
        P("rep", "feat", None, None),
        P("rep", "feat", None, None, None),
        P(),
        P("rep", "feat", None, None),
    )
    return jax.shard_map(
        on_device,
        mesh=mesh,
        in_specs=placed,
        out_specs=(P(None, "feat", None), P(), P(), P()),
        check_vma=False,
    )
```

profile of v0, /device:TPU:0, one launch (start us, length us, event | category | flops | bytes accessed | tf_op | source)
XLA Modules:
  0.0 59.8 jit_solution(1796810542521457280)
XLA Ops:
  0.6 2.2 %shard_map.93 = (f32[784,256]{1,0:T(8,128)S(1)}, f32[784,256]{1,0:T(8,128)S(1)}, bf16[128,256]{1,0:T(8,128)(2,1)S(1)}, s32[5,8,256]{2,1,0:T(8,128)S(1)}, bf16[25...) custom-call(bf16[128,256]{1,0:T(8,128)(2,1)} %bitcast.16, ...), custom_call_target="tpu_custom_call" | custom-call | flops 1000000 | bytes 1000000 | tf_op jit(solution)/shard_map/pallas_call | solution.py:300
  2.8 0.6 collective-permute-start.12
  3.4 1.1 %shard_map.96.refs_2_ = bf16[256,256]{1,0:T(8,128)(2,1)S(1)} custom-call(bf16[256,256]{1,0:T(8,128)(2,1)S(1)} %get-tuple-element.26.pre_ref, s32[5,8,256]{2,1,0:T(8,128)S(1)} %get-tuple-element.27.words_ref, bf16[6,256,256]{2,1,0:T(8,128)(2,1)S(1)} %get-tuple-element.28.weight_ref, bf16[128,256]{1,0:T(8,128)(2,1)S(1)} %get-tuple-element.29.grad_ref), custom_call_target="tpu_custom_call" | custom-call | flops 1000000 | bytes 1000000 | tf_op jit(solution)/shard_map/pallas_call | solution.py:311
  4.5 3.5 %collective-permute-start.2 = (bf16[256,256]{1,0:T(8,128)(2,1)S(1)}, bf16[256,256]{1,0:T(8,128)(2,1)S(1)}, u32[]{:S(2)}, u32[]{:S(2)}) collective-permute-start(bf16[256,256]{1,0:T(8,128)(2,1)S(1)} %shard_map.96.refs_2_), channel_id=1, source_target_pairs={{0,24},{4,28},{8,16},{12,20},{16,8},{20,12},{24,0},{28,4},{1,25},{... | collective-permute-start | bytes 393224 | tf_op jit(solution)/shard_map/ppermute | solution.py:331
  8.2 0.5 collective-permute-start.1
  8.7 0.4 collective-permute-start
  9.1 3.1 %collective-permute-done.2.refs_5_ = bf16[256,256]{1,0:T(8,128)(2,1)S(1)} collective-permute-done((bf16[256,256]{1,0:T(8,128)(2,1)S(1)}, bf16[256,256]{1,0:T(8,128)(2,1)S(1)}, u32[]{:S(2)}, u32[]{:S(2)}) %collective-permute-start.2) | collective-permute-done | bytes 131104 | tf_op jit(solution)/shard_map/ppermute | solution.py:331
  12.3 2.1 %shard_map.95.refs_1_ = bf16[768,1024]{1,0:T(8,128)(2,1)S(1)} custom-call(bf16[8,128,512]{2,1,0:T(8,128)(2,1)S(1)} %get-tuple-element.24.column_ref, s32[8,5,16,512]{3,2,1,0:T(8,128)S(1)} %get-tuple-element.25.word_ref), custom_call_target="tpu_custom_call" | custom-call | flops 3000000000 | bytes 1000000 | tf_op jit(solution)/shard_map/pallas_call | solution.py:320
  14.4 0.6 collective-permute-done.1.refs_4_
  15.6 1.7 %collective-permute-start.13 = (bf16[208,256]{1,0:T(8,128)(2,1)S(1)}, bf16[208,256]{1,0:T(8,128)(2,1)S(1)}, u32[]{:S(2)}, u32[]{:S(2)}) collective-permute-start(bf16[208,256]{1,0:T(8,128)(2,1)S(1)} %get-tuple-element.38), channel_id=1, source_target_pairs={{0,8},{4,12},{8,0},{12,4},{16,24},{20,28},{24,16},{28,20},{1,9},{5... | collective-permute-start | bytes 319496 | tf_op jit(solution)/shard_map/ppermute | solution.py:331
  17.4 1.5 %collective-permute-start.14 = (bf16[208,256]{1,0:T(8,128)(2,1)S(1)}, bf16[208,256]{1,0:T(8,128)(2,1)S(1)}, u32[]{:S(2)}, u32[]{:S(2)}) collective-permute-start(bf16[208,256]{1,0:T(8,128)(2,1)S(1)} %get-tuple-element.39), channel_id=1, source_target_pairs={{0,16},{4,20},{8,24},{12,28},{16,0},{20,4},{24,8},{28,12},{1,17},{... | collective-permute-start | bytes 319496 | tf_op jit(solution)/shard_map/ppermute | solution.py:331
  19.2 2.1 %shard_map.94.refs_0_ = bf16[768,1024]{1,0:T(8,128)(2,1)S(1)} custom-call(bf16[8,128,512]{2,1,0:T(8,128)(2,1)S(1)} %get-tuple-element.24.column_ref, s32[8,5,16,512]{3,2,1,0:T(8,128)S(1)} %get-tuple-element.25.word_ref), custom_call_target="tpu_custom_call" | custom-call | flops 3000000000 | bytes 1000000 | tf_op jit(solution)/shard_map/pallas_call | solution.py:320
  21.3 1.1 %shard_map.97 = (f32[1,256]{1,0:T(1,128)S(1)}, f32[192,256]{1,0:T(8,128)S(1)}, bf16[192,256]{1,0:T(8,128)(2,1)S(1)}, bf16[192,256]{1,0:T(8,128)(2,1)S(1)}, bf16[192,256]{1,0:T(8,128)(2,1)S(1)}) custom-call(bf16[768,1024]{1,0:T(8,128)(2,1)S(1)} %shard_map.94.refs_0_, bf16[768,1024]{1,0:T(8,128)(2,1)S(1)} %shard_map.95.refs_1_, ...), custom_call_target="tpu_custom_call" | custom-call | flops 1000000 | bytes 1000000 | tf_op jit(solution)/shard_map/pallas_call | solution.py:377
  22.5 2.2 %collective-permute-done.14.refs_1_ = bf16[208,256]{1,0:T(8,128)(2,1)S(1)} collective-permute-done((bf16[208,256]{1,0:T(8,128)(2,1)S(1)}, bf16[208,256]{1,0:T(8,128)(2,1)S(1)}, u32[]{:S(2)}, u32[]{:S(2)}) %collective-permute-start.14) | collective-permute-done | bytes 106528 | tf_op jit(solution)/shard_map/ppermute | solution.py:331
  24.7 1.6 %collective-permute-start.16 = (f32[208,256]{1,0:T(8,128)S(1)}, f32[208,256]{1,0:T(8,128)S(1)}, u32[]{:S(2)}, u32[]{:S(2)}) collective-permute-start(f32[208,256]{1,0:T(8,128)S(1)} %shard_map.102.mine_ref), channel_id=1, source_target_pairs={{0,1},{1,0},{2,3},{3,2},{4,5},{5,4},{6,7},{7,6},{8,9},{9,8},{10,11... | collective-permute-start | bytes 638984 | tf_op jit(solution)/shard_map/ppermute | solution.py:348
  26.4 0.4 collective-permute-start.7
  26.8 2.6 %collective-permute-start.8 = (bf16[192,256]{1,0:T(8,128)(2,1)S(1)}, bf16[192,256]{1,0:T(8,128)(2,1)S(1)}, u32[]{:S(2)}, u32[]{:S(2)}) collective-permute-start(bf16[192,256]{1,0:T(8,128)(2,1)S(1)} %get-tuple-element.32), channel_id=1, source_target_pairs={{0,2},{1,3},{2,0},{3,1},{4,6},{5,7},{6,4},{7,5},{8,10},{9,11},{10,... | collective-permute-start | bytes 294920 | tf_op jit(solution)/shard_map/ppermute | solution.py:348
  29.4 1.3 %collective-permute-start.9 = (bf16[192,256]{1,0:T(8,128)(2,1)S(1)}, bf16[192,256]{1,0:T(8,128)(2,1)S(1)}, u32[]{:S(2)}, u32[]{:S(2)}) collective-permute-start(bf16[192,256]{1,0:T(8,128)(2,1)S(1)} %get-tuple-element.33), channel_id=1, source_target_pairs={{0,3},{1,2},{2,1},{3,0},{4,7},{5,6},{6,5},{7,4},{8,11},{9,10},{10,... | collective-permute-start | bytes 294920 | tf_op jit(solution)/shard_map/ppermute | solution.py:348
  30.8 3.5 %collective-permute-done.16.got_ref = f32[208,256]{1,0:T(8,128)S(1)} collective-permute-done((f32[208,256]{1,0:T(8,128)S(1)}, f32[208,256]{1,0:T(8,128)S(1)}, u32[]{:S(2)}, u32[]{:S(2)}) %collective-permute-start.16) | collective-permute-done | bytes 213024 | tf_op jit(solution)/shard_map/ppermute | solution.py:348
  34.4 2.9 %collective-permute-start.17 = (bf16[208,256]{1,0:T(8,128)(2,1)S(1)}, bf16[208,256]{1,0:T(8,128)(2,1)S(1)}, u32[]{:S(2)}, u32[]{:S(2)}) collective-permute-start(bf16[208,256]{1,0:T(8,128)(2,1)S(1)} %shard_map.103.mine_ref), channel_id=1, source_target_pairs={{0,2},{1,3},{2,0},{3,1},{4,6},{5,7},{6,4},{7,5},{8,10},{9,11},{10,... | collective-permute-start | bytes 319496 | tf_op jit(solution)/shard_map/ppermute | solution.py:348
  37.3 4.1 %collective-permute-done.9.refs_2_ = bf16[192,256]{1,0:T(8,128)(2,1)S(1)} collective-permute-done((bf16[192,256]{1,0:T(8,128)(2,1)S(1)}, bf16[192,256]{1,0:T(8,128)(2,1)S(1)}, u32[]{:S(2)}, u32[]{:S(2)}) %collective-permute-start.9) | collective-permute-done | bytes 98336 | tf_op jit(solution)/shard_map/ppermute | solution.py:348
  41.4 3.0 %collective-permute-start.10 = (bf16[1,192,256]{2,1,0:T(8,128)(2,1)S(1)}, bf16[1,192,256]{2,1,0:T(8,128)(2,1)S(1)}, u32[]{:S(2)}, u32[]{:S(2)}) collective-permute-start(bf16[1,192,256]{2,1,0:T(8,128)(2,1)S(1)} %bitcast.10), channel_id=1, source_target_pairs={{0,2},{1,3},{2,0},{3,1},{4,6},{5,7},{6,4},{7,5},{8,10},{9,11},{10,... | collective-permute-start | bytes 294920 | tf_op jit(solution)/shard_map/ppermute | solution.py:348
  44.4 2.9 %collective-permute-done.10.refs_1_ = bf16[1,192,256]{2,1,0:T(8,128)(2,1)S(1)} collective-permute-done((bf16[1,192,256]{2,1,0:T(8,128)(2,1)S(1)}, bf16[1,192,256]{2,1,0:T(8,128)(2,1)S(1)}, u32[]{:S(2)}, u32[]{:S(2)}) %collective-permute-start.10) | collective-permute-done | bytes 98336 | tf_op jit(solution)/shard_map/ppermute | solution.py:348
  47.4 2.4 %collective-permute-start.11 = (bf16[2,192,256]{2,1,0:T(8,128)(2,1)S(1)}, bf16[2,192,256]{2,1,0:T(8,128)(2,1)S(1)}, u32[]{:S(2)}, u32[]{:S(2)}) collective-permute-start(bf16[2,192,256]{2,1,0:T(8,128)(2,1)S(1)} %shard_map.99), channel_id=1, source_target_pairs={{0,1},{1,0},{2,3},{3,2},{4,5},{5,4},{6,7},{7,6},{8,9},{9,8},{10,11... | collective-permute-start | bytes 589832 | tf_op jit(solution)/shard_map/ppermute | solution.py:348
  49.7 0.6 shard_map.104
  50.3 1.7 %collective-permute-start.20 = (bf16[192,256]{1,0:T(8,128)(2,1)S(1)}, bf16[192,256]{1,0:T(8,128)(2,1)S(1)}, u32[]{:S(2)}, u32[]{:S(2)}) collective-permute-start(bf16[192,256]{1,0:T(8,128)(2,1)S(1)} %get-tuple-element.42.refs_0_), channel_id=1, source_target_pairs={{0,24},{4,28},{8,16},{12,20},{16,8},{20,12},{24,0},{28,4},{1,25},{... | collective-permute-start | bytes 294920 | tf_op jit(solution)/shard_map/ppermute | solution.py:331
  52.0 1.8 %collective-permute-start.18 = (bf16[192,256]{1,0:T(8,128)(2,1)S(1)}, bf16[192,256]{1,0:T(8,128)(2,1)S(1)}, u32[]{:S(2)}, u32[]{:S(2)}) collective-permute-start(bf16[192,256]{1,0:T(8,128)(2,1)S(1)} %get-tuple-element.42.refs_0_), channel_id=1, source_target_pairs={{0,8},{4,12},{8,0},{12,4},{16,24},{20,28},{24,16},{28,20},{1,9},{5... | collective-permute-start | bytes 294920 | tf_op jit(solution)/shard_map/ppermute | solution.py:331
  53.8 2.0 %collective-permute-done.20.refs_3_ = bf16[192,256]{1,0:T(8,128)(2,1)S(1)} collective-permute-done((bf16[192,256]{1,0:T(8,128)(2,1)S(1)}, bf16[192,256]{1,0:T(8,128)(2,1)S(1)}, u32[]{:S(2)}, u32[]{:S(2)}) %collective-permute-start.20) | collective-permute-done | bytes 98336 | tf_op jit(solution)/shard_map/ppermute | solution.py:331
  55.9 1.0 %collective-permute-done.19.refs_2_ = bf16[192,256]{1,0:T(8,128)(2,1)S(1)} collective-permute-done((bf16[192,256]{1,0:T(8,128)(2,1)S(1)}, bf16[192,256]{1,0:T(8,128)(2,1)S(1)}, u32[]{:S(2)}, u32[]{:S(2)}) %collective-permute-start.19) | collective-permute-done | bytes 98336 | tf_op jit(solution)/shard_map/ppermute | solution.py:331
  56.9 0.3 collective-permute-done.18.refs_1_
  57.4 0.9 %shard_map.100 = f32[4,192,256]{2,1,0:T(8,128)} custom-call(bf16[192,256]{1,0:T(8,128)(2,1)S(1)} %shard_map.98.refs_0_, bf16[1,192,256]{2,1,0:T(8,128)(2,1)S(1)} %collective-permute-done.10.refs_1_, bf16[2,192,256]{2,1,0:T(8,128)(2,1)S(1)} %collective-permute-done.11.refs_2_), custom_call_target="tpu_custom_call" | custom-call | flops 1000000 | bytes 1000000 | tf_op jit(solution)/shard_map/pallas_call | solution.py:441
  58.5 1.3 %shard_map.105 = f32[8,192,256]{2,1,0:T(8,128)} custom-call(bf16[192,256]{1,0:T(8,128)(2,1)S(1)} %get-tuple-element.42.refs_0_, bf16[192,256]{1,0:T(8,128)(2,1)S(1)} %collective-permute-done.18.refs_1_, bf16[192,256]{1,0:T(8,128)(2,1)S(1)} %collective-permute-done.19.refs_2_, bf16[192,256]{1,0:T(8,128)(2,1)S(1)} %collective-permute-done.20.refs_3_, ...), custom_call_target="tpu_custom_call" | custom-call | flops 1000000 | bytes 1000000 | tf_op jit(solution)/shard_map/pallas_call | solution.py:456
  (31 shorter events, 1.7 us)
Async XLA Ops:
  2.8 12.6 %collective-permute-start.12 = (f32[784,256]{1,0:T(8,128)S(1)}, f32[784,256]{1,0:T(8,128)S(1)}, u32[]{:S(2)}, u32[]{:S(2)}) collective-permute-start(f32[784,256]{1,0:T(8,128)S(1)} %get-tuple-element.36), channel_id=1, source_target_pairs={{0,4},{4,0},{8,12},{12,8},{16,20},{20,16},{24,28},{28,24},{1,5},{5... | collective-permute-start | bytes 2408456 | tf_op jit(solution)/shard_map/ppermute | solution.py:334
  4.5 7.8 %collective-permute-start.2 = (bf16[256,256]{1,0:T(8,128)(2,1)S(1)}, bf16[256,256]{1,0:T(8,128)(2,1)S(1)}, u32[]{:S(2)}, u32[]{:S(2)}) collective-permute-start(bf16[256,256]{1,0:T(8,128)(2,1)S(1)} %shard_map.96.refs_2_), channel_id=1, source_target_pairs={{0,24},{4,28},{8,16},{12,20},{16,8},{20,12},{24,0},{28,4},{1,25},{... | collective-permute-start | bytes 393224 | tf_op jit(solution)/shard_map/ppermute | solution.py:331
  8.0 9.4 %collective-permute-start.3 = (bf16[256,256]{1,0:T(8,128)(2,1)S(1)}, bf16[256,256]{1,0:T(8,128)(2,1)S(1)}, u32[]{:S(2)}, u32[]{:S(2)}) collective-permute-start(bf16[256,256]{1,0:T(8,128)(2,1)S(1)} %shard_map.96.refs_2_), channel_id=1, source_target_pairs={{0,4},{4,0},{8,12},{12,8},{16,20},{20,16},{24,28},{28,24},{1,5},{5... | collective-permute-start | bytes 393224 | tf_op jit(solution)/shard_map/ppermute | solution.py:334
  8.2 6.8 %collective-permute-start.1 = (bf16[256,256]{1,0:T(8,128)(2,1)S(1)}, bf16[256,256]{1,0:T(8,128)(2,1)S(1)}, u32[]{:S(2)}, u32[]{:S(2)}) collective-permute-start(bf16[256,256]{1,0:T(8,128)(2,1)S(1)} %shard_map.96.refs_2_), channel_id=1, source_target_pairs={{0,16},{4,20},{8,24},{12,28},{16,0},{20,4},{24,8},{28,12},{1,17},{... | collective-permute-start | bytes 393224 | tf_op jit(solution)/shard_map/ppermute | solution.py:331
  8.7 6.5 %collective-permute-start = (bf16[256,256]{1,0:T(8,128)(2,1)S(1)}, bf16[256,256]{1,0:T(8,128)(2,1)S(1)}, u32[]{:S(2)}, u32[]{:S(2)}) collective-permute-start(bf16[256,256]{1,0:T(8,128)(2,1)S(1)} %shard_map.96.refs_2_), channel_id=1, source_target_pairs={{0,8},{4,12},{8,0},{12,4},{16,24},{20,28},{24,16},{28,20},{1,9},{5... | collective-permute-start | bytes 393224 | tf_op jit(solution)/shard_map/ppermute | solution.py:331
  12.3 6.6 %collective-permute-start.6 = (bf16[256,256]{1,0:T(8,128)(2,1)S(1)}, bf16[256,256]{1,0:T(8,128)(2,1)S(1)}, u32[]{:S(2)}, u32[]{:S(2)}) collective-permute-start(bf16[256,256]{1,0:T(8,128)(2,1)S(1)} %collective-permute-done.2.refs_5_), channel_id=1, source_target_pairs={{0,4},{4,0},{8,12},{12,8},{16,20},{20,16},{24,28},{28,24},{1,5},{5... | collective-permute-start | bytes 393224 | tf_op jit(solution)/shard_map/ppermute | solution.py:334
  15.0 6.4 %collective-permute-start.5 = (bf16[256,256]{1,0:T(8,128)(2,1)S(1)}, bf16[256,256]{1,0:T(8,128)(2,1)S(1)}, u32[]{:S(2)}, u32[]{:S(2)}) collective-permute-start(bf16[256,256]{1,0:T(8,128)(2,1)S(1)} %collective-permute-done.1.refs_4_), channel_id=1, source_target_pairs={{0,4},{4,0},{8,12},{12,8},{16,20},{20,16},{24,28},{28,24},{1,5},{5... | collective-permute-start | bytes 393224 | tf_op jit(solution)/shard_map/ppermute | solution.py:334
  15.3 6.1 %collective-permute-start.4 = (bf16[256,256]{1,0:T(8,128)(2,1)S(1)}, bf16[256,256]{1,0:T(8,128)(2,1)S(1)}, u32[]{:S(2)}, u32[]{:S(2)}) collective-permute-start(bf16[256,256]{1,0:T(8,128)(2,1)S(1)} %collective-permute-done.refs_3_), channel_id=1, source_target_pairs={{0,4},{4,0},{8,12},{12,8},{16,20},{20,16},{24,28},{28,24},{1,5},{5... | collective-permute-start | bytes 393224 | tf_op jit(solution)/shard_map/ppermute | solution.py:334
  15.6 6.9 %collective-permute-start.13 = (bf16[208,256]{1,0:T(8,128)(2,1)S(1)}, bf16[208,256]{1,0:T(8,128)(2,1)S(1)}, u32[]{:S(2)}, u32[]{:S(2)}) collective-permute-start(bf16[208,256]{1,0:T(8,128)(2,1)S(1)} %get-tuple-element.38), channel_id=1, source_target_pairs={{0,8},{4,12},{8,0},{12,4},{16,24},{20,28},{24,16},{28,20},{1,9},{5... | collective-permute-start | bytes 319496 | tf_op jit(solution)/shard_map/ppermute | solution.py:331
  17.4 7.3 %collective-permute-start.14 = (bf16[208,256]{1,0:T(8,128)(2,1)S(1)}, bf16[208,256]{1,0:T(8,128)(2,1)S(1)}, u32[]{:S(2)}, u32[]{:S(2)}) collective-permute-start(bf16[208,256]{1,0:T(8,128)(2,1)S(1)} %get-tuple-element.39), channel_id=1, source_target_pairs={{0,16},{4,20},{8,24},{12,28},{16,0},{20,4},{24,8},{28,12},{1,17},{... | collective-permute-start | bytes 319496 | tf_op jit(solution)/shard_map/ppermute | solution.py:331
  18.9 5.8 %collective-permute-start.15 = (bf16[208,256]{1,0:T(8,128)(2,1)S(1)}, bf16[208,256]{1,0:T(8,128)(2,1)S(1)}, u32[]{:S(2)}, u32[]{:S(2)}) collective-permute-start(bf16[208,256]{1,0:T(8,128)(2,1)S(1)} %get-tuple-element.40), channel_id=1, source_target_pairs={{0,24},{4,28},{8,16},{12,20},{16,8},{20,12},{24,0},{28,4},{1,25},{... | collective-permute-start | bytes 319496 | tf_op jit(solution)/shard_map/ppermute | solution.py:331
  24.7 9.6 %collective-permute-start.16 = (f32[208,256]{1,0:T(8,128)S(1)}, f32[208,256]{1,0:T(8,128)S(1)}, u32[]{:S(2)}, u32[]{:S(2)}) collective-permute-start(f32[208,256]{1,0:T(8,128)S(1)} %shard_map.102.mine_ref), channel_id=1, source_target_pairs={{0,1},{1,0},{2,3},{3,2},{4,5},{5,4},{6,7},{7,6},{8,9},{9,8},{10,11... | collective-permute-start | bytes 638984 | tf_op jit(solution)/shard_map/ppermute | solution.py:348
  26.4 10.9 %collective-permute-start.7 = (bf16[192,256]{1,0:T(8,128)(2,1)S(1)}, bf16[192,256]{1,0:T(8,128)(2,1)S(1)}, u32[]{:S(2)}, u32[]{:S(2)}) collective-permute-start(bf16[192,256]{1,0:T(8,128)(2,1)S(1)} %get-tuple-element.31), channel_id=1, source_target_pairs={{0,1},{1,0},{2,3},{3,2},{4,5},{5,4},{6,7},{7,6},{8,9},{9,8},{10,11... | collective-permute-start | bytes 294920 | tf_op jit(solution)/shard_map/ppermute | solution.py:348
  26.8 10.5 %collective-permute-start.8 = (bf16[192,256]{1,0:T(8,128)(2,1)S(1)}, bf16[192,256]{1,0:T(8,128)(2,1)S(1)}, u32[]{:S(2)}, u32[]{:S(2)}) collective-permute-start(bf16[192,256]{1,0:T(8,128)(2,1)S(1)} %get-tuple-element.32), channel_id=1, source_target_pairs={{0,2},{1,3},{2,0},{3,1},{4,6},{5,7},{6,4},{7,5},{8,10},{9,11},{10,... | collective-permute-start | bytes 294920 | tf_op jit(solution)/shard_map/ppermute | solution.py:348
  29.4 12.0 %collective-permute-start.9 = (bf16[192,256]{1,0:T(8,128)(2,1)S(1)}, bf16[192,256]{1,0:T(8,128)(2,1)S(1)}, u32[]{:S(2)}, u32[]{:S(2)}) collective-permute-start(bf16[192,256]{1,0:T(8,128)(2,1)S(1)} %get-tuple-element.33), channel_id=1, source_target_pairs={{0,3},{1,2},{2,1},{3,0},{4,7},{5,6},{6,5},{7,4},{8,11},{9,10},{10,... | collective-permute-start | bytes 294920 | tf_op jit(solution)/shard_map/ppermute | solution.py:348
  34.4 15.4 %collective-permute-start.17 = (bf16[208,256]{1,0:T(8,128)(2,1)S(1)}, bf16[208,256]{1,0:T(8,128)(2,1)S(1)}, u32[]{:S(2)}, u32[]{:S(2)}) collective-permute-start(bf16[208,256]{1,0:T(8,128)(2,1)S(1)} %shard_map.103.mine_ref), channel_id=1, source_target_pairs={{0,2},{1,3},{2,0},{3,1},{4,6},{5,7},{6,4},{7,5},{8,10},{9,11},{10,... | collective-permute-start | bytes 319496 | tf_op jit(solution)/shard_map/ppermute | solution.py:348
  41.4 5.9 %collective-permute-start.10 = (bf16[1,192,256]{2,1,0:T(8,128)(2,1)S(1)}, bf16[1,192,256]{2,1,0:T(8,128)(2,1)S(1)}, u32[]{:S(2)}, u32[]{:S(2)}) collective-permute-start(bf16[1,192,256]{2,1,0:T(8,128)(2,1)S(1)} %bitcast.10), channel_id=1, source_target_pairs={{0,2},{1,3},{2,0},{3,1},{4,6},{5,7},{6,4},{7,5},{8,10},{9,11},{10,... | collective-permute-start | bytes 294920 | tf_op jit(solution)/shard_map/ppermute | solution.py:348
  47.4 10.0 %collective-permute-start.11 = (bf16[2,192,256]{2,1,0:T(8,128)(2,1)S(1)}, bf16[2,192,256]{2,1,0:T(8,128)(2,1)S(1)}, u32[]{:S(2)}, u32[]{:S(2)}) collective-permute-start(bf16[2,192,256]{2,1,0:T(8,128)(2,1)S(1)} %shard_map.99), channel_id=1, source_target_pairs={{0,1},{1,0},{2,3},{3,2},{4,5},{5,4},{6,7},{7,6},{8,9},{9,8},{10,11... | collective-permute-start | bytes 589832 | tf_op jit(solution)/shard_map/ppermute | solution.py:348
  50.3 5.5 %collective-permute-start.20 = (bf16[192,256]{1,0:T(8,128)(2,1)S(1)}, bf16[192,256]{1,0:T(8,128)(2,1)S(1)}, u32[]{:S(2)}, u32[]{:S(2)}) collective-permute-start(bf16[192,256]{1,0:T(8,128)(2,1)S(1)} %get-tuple-element.42.refs_0_), channel_id=1, source_target_pairs={{0,24},{4,28},{8,16},{12,20},{16,8},{20,12},{24,0},{28,4},{1,25},{... | collective-permute-start | bytes 294920 | tf_op jit(solution)/shard_map/ppermute | solution.py:331
  52.0 4.9 %collective-permute-start.19 = (bf16[192,256]{1,0:T(8,128)(2,1)S(1)}, bf16[192,256]{1,0:T(8,128)(2,1)S(1)}, u32[]{:S(2)}, u32[]{:S(2)}) collective-permute-start(bf16[192,256]{1,0:T(8,128)(2,1)S(1)} %get-tuple-element.42.refs_0_), channel_id=1, source_target_pairs={{0,16},{4,20},{8,24},{12,28},{16,0},{20,4},{24,8},{28,12},{1,17},{... | collective-permute-start | bytes 294920 | tf_op jit(solution)/shard_map/ppermute | solution.py:331
  52.0 5.2 %collective-permute-start.18 = (bf16[192,256]{1,0:T(8,128)(2,1)S(1)}, bf16[192,256]{1,0:T(8,128)(2,1)S(1)}, u32[]{:S(2)}, u32[]{:S(2)}) collective-permute-start(bf16[192,256]{1,0:T(8,128)(2,1)S(1)} %get-tuple-element.42.refs_0_), channel_id=1, source_target_pairs={{0,8},{4,12},{8,0},{12,4},{16,24},{20,28},{24,16},{28,20},{1,9},{5... | collective-permute-start | bytes 294920 | tf_op jit(solution)/shard_map/ppermute | solution.py:331
  53.8 4.5 %collective-permute-start.21 = (bf16[192,256]{1,0:T(8,128)(2,1)S(1)}, bf16[192,256]{1,0:T(8,128)(2,1)S(1)}, u32[]{:S(2)}, u32[]{:S(2)}) collective-permute-start(bf16[192,256]{1,0:T(8,128)(2,1)S(1)} %get-tuple-element.42.refs_0_), channel_id=1, source_target_pairs={{0,4},{4,0},{8,12},{12,8},{16,20},{20,16},{24,28},{28,24},{1,5},{5... | collective-permute-start | bytes 294920 | tf_op jit(solution)/shard_map/ppermute | solution.py:334
  55.9 2.5 %collective-permute-start.24 = (bf16[192,256]{1,0:T(8,128)(2,1)S(1)}, bf16[192,256]{1,0:T(8,128)(2,1)S(1)}, u32[]{:S(2)}, u32[]{:S(2)}) collective-permute-start(bf16[192,256]{1,0:T(8,128)(2,1)S(1)} %collective-permute-done.20.refs_3_), channel_id=1, source_target_pairs={{0,4},{4,0},{8,12},{12,8},{16,20},{20,16},{24,28},{28,24},{1,5},{5... | collective-permute-start | bytes 294920 | tf_op jit(solution)/shard_map/ppermute | solution.py:334
  56.9 1.5 %collective-permute-start.23 = (bf16[192,256]{1,0:T(8,128)(2,1)S(1)}, bf16[192,256]{1,0:T(8,128)(2,1)S(1)}, u32[]{:S(2)}, u32[]{:S(2)}) collective-permute-start(bf16[192,256]{1,0:T(8,128)(2,1)S(1)} %collective-permute-done.19.refs_2_), channel_id=1, source_target_pairs={{0,4},{4,0},{8,12},{12,8},{16,20},{20,16},{24,28},{28,24},{1,5},{5... | collective-permute-start | bytes 294920 | tf_op jit(solution)/shard_map/ppermute | solution.py:334
  57.2 1.3 %collective-permute-start.22 = (bf16[192,256]{1,0:T(8,128)(2,1)S(1)}, bf16[192,256]{1,0:T(8,128)(2,1)S(1)}, u32[]{:S(2)}, u32[]{:S(2)}) collective-permute-start(bf16[192,256]{1,0:T(8,128)(2,1)S(1)} %collective-permute-done.18.refs_1_), channel_id=1, source_target_pairs={{0,4},{4,0},{8,12},{12,8},{16,20},{20,16},{24,28},{28,24},{1,5},{5... | collective-permute-start | bytes 294920 | tf_op jit(solution)/shard_map/ppermute | solution.py:334
where the time goes:
time: 59.9 us; the launch traced here: 59.8 us
  starting transfers between devices  27.1 us (45%)
  waiting for transfers between devices  20.1 us (34%)
  Pallas kernels  11.8 us (20%)
  between operations  0.74 us (1%)
    ppermute x7, starting transfers between devices, to_rep(): return lax.ppermute(value, 'rep', pairs)  14.4 us
    ppermute x9, starting transfers between devices, to_chip(): return lax.ppermute(value, 'feat', pairs)  11.5 us
    ppermute x7, waiting for transfers between devices, to_rep(): return lax.ppermute(value, 'rep', pairs)  10.5 us
    ppermute x9, waiting for transfers between devices, to_chip(): return lax.ppermute(value, 'feat', pairs)  9.46 us
    pallas_call x2, Pallas kernels, on_device(): call(functools.partial(gather_kernel, n * run, run), shape(sets * width,...  4.27 us
    pallas_call x1, Pallas kernels, on_device(): call(functools.partial(upper_kernel, factor, core_of if direct else lambd...  2.21 us
    ppermute x9, starting transfers between devices, to_core(): return lax.ppermute(value, 'feat', [(i, i ^ 1) for i in range(feat)])  1.29 us
    pallas_call x1, Pallas kernels, on_device(): call(functools.partial(place_kernel, places), jax.ShapeDtypeStruct((feat,...  1.26 us
  transfers between devices with their start and end apart: 25, of which 11 were waited for; matrix products, arithmetic and copies ran while one was open for 0% of the time, Pallas kernels for 14%

commit v1 on v0

--- a/solution.py
+++ b/solution.py
@@ -120,14 +120,36 @@
     hidden_ref[...] = dot(reorder(total.shape[0]), hidden_grad).astype(BF16)
 
 
-def pair_kernel(chip_of, own_ref, got_ref, *refs):
+def pair_kernel(taker, own_ref, got_ref, *refs):
     outs, sums = refs[:-1], refs[-1]
-    chips, rows, width = sums.shape
-    height = chips * rows
+    reps, rows, width = sums.shape
+    height = reps * rows
     total = own_ref[:height] + got_ref[:height]
-    sums[...] = total.reshape(chips, rows, width)
+    sums[...] = total.reshape(reps, rows, width)
     bias = own_ref[height:] + got_ref[height:]
     packed = pack_rows(bias[0:1])
+    outs[0][:rows] = sums[taker(0)]
+    outs[0][rows:] = packed.astype(F32)
+    for k in range(1, reps):
+        outs[k][:rows] = sums[taker(k)].astype(BF16)
+        outs[k][rows:] = packed
+
+
+def rep_sum_kernel(giver, chip_of, own_ref, *refs):
+    reps, chips = refs[-1].shape[0], refs[-2].shape[0]
+    got, outs, (sums, slots) = refs[: reps - 1], refs[reps - 1 : -2], refs[-2:]
+    rows = sums.shape[1]
+    height = chips * rows
+    total = own_ref[:height]
+    slots[giver(0)] = own_ref[height:]
+    for k, piece in enumerate(got, 1):
+        total = total + piece[:height].astype(F32)
+        slots[giver(k)] = piece[height:].astype(F32)
+    sums[...] = total.reshape(sums.shape)
+    bias = read_row(slots[0], 0)
+    for j in range(1, reps):
+        bias = bias + read_row(slots[j], 0)
+    packed = pack_rows(bias)
     chip = chip_of()
     outs[0][:rows] = sums[chip]
     outs[0][rows:] = packed.astype(F32)
@@ -169,7 +191,7 @@
 
 def panel_kernel(taker, order, parts, *refs):
     gathered, refs = refs[:parts], refs[parts:]
-    blocks, (bias_ref, own_ref, *outs) = refs[: len(order)], refs[len(order) : -2]
+    blocks, (own_ref, *outs) = refs[: len(order)], refs[len(order) : -2]
     stack, sums = refs[-2:]
     height = blocks[0].shape[0]
     for block, place in zip(blocks, order):
@@ -181,7 +203,6 @@
         total = total + dot(gathered[n][...], stack[n * deep : (n + 1) * deep])
     sums[...] = total.reshape(sums.shape)
     reps = sums.shape[0]
-    bias_ref[...] = jnp.sum(stack[...].astype(F32), 0, keepdims=True)
     own_ref[...] = sums[taker(0)]
     for k in range(1, reps):
         outs[k - 1][...] = sums[taker(k)].astype(BF16)
@@ -202,8 +223,9 @@
     return jax.ShapeDtypeStruct((rows, cols), dtype)
 
 
-def plane_sum_kernel(chip_of, bias_ref, own_ref, *refs):
-    got, out, slots = refs[:-2], refs[-2], refs[-1]
+def plane_sum_kernel(chip_of, order, own_ref, *refs):
+    blocks, got = refs[: len(order)], refs[len(order) : -4]
+    out, two_ref, slots, rows_sum = refs[-4:]
     rows = out.shape[0] - BIAS_ROWS
     chip = chip_of()
     total = own_ref[:rows]
@@ -211,36 +233,29 @@
     for k, piece in enumerate(got, 1):
         total = total + piece[:rows].astype(F32)
         slots[lax.bitwise_xor(chip, k)] = piece[rows:].astype(F32)
-    out[:rows] = total
-    bias = read_row(slots[0], 0)
+    out[:rows] = total.astype(BF16)
+    two = read_row(slots[0], 0)
     for j in range(1, slots.shape[0]):
-        bias = bias + read_row(slots[j], 0)
-    row = lax.broadcasted_iota(jnp.int32, (BIAS_ROWS, bias.shape[1]), 0)
-    out[rows:] = jnp.where(row == 0, bias_ref[...], bias)
-
-
-def rep_pair_kernel(mine_ref, got_ref, out_ref):
-    rows = out_ref.shape[0] - BIAS_ROWS
-    out_ref[:rows] = (mine_ref[:rows] + got_ref[:rows]).astype(BF16)
-    bias = mine_ref[rows:] + got_ref[rows:]
-    out_ref[rows:] = pack_rows(bias[0:1], bias[1:2])
-
-
-def rep_more_kernel(mine_ref, got_ref, out_ref):
-    rows = out_ref.shape[0] - BIAS_ROWS
-    out_ref[:rows] = (mine_ref[:rows].astype(F32) + got_ref[:rows].astype(F32)).astype(BF16)
-    mine, got = mine_ref[rows:], got_ref[rows:]
-    out_ref[rows:] = pack_rows(
-        read_row(mine, 0) + read_row(got, 0), read_row(mine, 1) + read_row(got, 1)
-    )
-
-
-def finish_kernel(mine_ref, got_ref, upper_ref, one_ref, two_ref):
-    rows = upper_ref.shape[0]
-    upper_ref[...] = (mine_ref[:rows].astype(F32) + got_ref[:rows].astype(F32)).astype(BF16)
-    mine, got = mine_ref[rows:], got_ref[rows:]
-    one_ref[...] = read_row(mine, 0) + read_row(got, 0)
-    two_ref[...] = read_row(mine, 1) + read_row(got, 1)
+        two = two + read_row(slots[j], 0)
+    two_ref[...] = jnp.broadcast_to(two, two_ref.shape)
+    for block, place in zip(blocks, order):
+        rows_sum[place()] = jnp.sum(block[...].astype(F32), 0, keepdims=True)
+    one = rows_sum[0]
+    for j in range(1, len(order)):
+        one = one + rows_sum[j]
+    out[rows:] = pack_rows(one)
+
+
+def rep_join_kernel(giver, *refs):
+    parts, (out, one_ref, slots) = refs[:-3], refs[-3:]
+    rows = out.shape[1]
+    for k, part in enumerate(parts):
+        out[giver(k)] = part[:rows]
+        slots[giver(k)] = part[rows:]
+    one = read_row(slots[0], 0)
+    for j in range(1, len(parts)):
+        one = one + read_row(slots[j], 0)
+    one_ref[...] = jnp.broadcast_to(one, one_ref.shape)
 
 
 def panel_sum_kernel(own_ref, *refs):
@@ -250,23 +265,33 @@
     refs[-1][...] = total.astype(BF16)
 
 
-def layers(blocks):
-    for block in blocks:
-        if len(block.shape) == 2:
-            yield block[...]
-        else:
-            for n in range(block.shape[0]):
-                yield block[n]
-
-
-def pack_kernel(*refs):
-    for n, value in enumerate(layers(refs[:-1])):
-        refs[-1][n] = value
-
-
 def place_kernel(order, *refs):
-    for value, place in zip(layers(refs[:-1]), order):
-        refs[-1][place()] = value.astype(F32)
+    blocks, (out, held, sems) = refs[:-3], refs[-3:]
+    copies = []
+    for n, (block, place) in enumerate(zip(blocks, order)):
+        held[n] = block[...].astype(F32)
+        copies.append(pltpu.make_async_copy(held.at[n], out.at[place()], sems.at[n]))
+        copies[-1].start()
+    for copy in copies:
+        copy.wait()
+
+
+def place_two_kernel(order, *refs):
+    blocks, (one_ref, two_ref) = refs[: len(order)], refs[len(order) : len(order) + 2]
+    out, one_out, two_out, held, sems = refs[len(order) + 2 :]
+    copies = [
+        pltpu.make_async_copy(one_ref.at[0], one_out, sems.at[len(order)]),
+        pltpu.make_async_copy(two_ref.at[0], two_out, sems.at[len(order) + 1]),
+    ]
+    for copy in copies:
+        copy.start()
+    for n, (block, place) in enumerate(zip(blocks, order)):
+        core, chip = place()
+        held[n] = block[...].astype(F32)
+        copies.append(pltpu.make_async_copy(held.at[n], out.at[core, :, chip], sems.at[n]))
+        copies[-1].start()
+    for copy in copies:
+        copy.wait()
 
 
 def on_device(features, adjacency_one, pre_hidden, adjacency_two, weight_two, out_grad):
@@ -284,6 +309,7 @@
     cores = 2
     chips = feat // cores
     direct = feat <= 8 and feat % cores == 0 and chips & (chips - 1) == 0
+    direct = direct and sets * hidden_width % (8 * feat * reps) == 0
 
     def core_of():
         return lax.axis_index("feat") % cores
@@ -347,7 +373,7 @@
         pairs = [(i, (i ^ k) if flip else (i + k) % reps) for i in range(reps)]
         return lax.ppermute(value, "rep", pairs)
 
-    piece = half // chips
+    piece = half // (chips * reps)
     share = sets * width // reps
 
     if direct:
@@ -362,22 +388,31 @@
                     )
                 )
         got_half = to_core(send_half)
+        tall = half // reps + BIAS_ROWS
+        thirds = call(
+            functools.partial(pair_kernel, taker),
+            (shape(tall, hidden_width, F32),) + (shape(tall, hidden_width, BF16),) * (reps - 1),
+            (pltpu.VMEM((reps, half // reps, hidden_width), F32),),
+        )(own_half, got_half)
+        got = [to_rep(thirds[k], k) for k in range(1, reps)]
         tall = piece + BIAS_ROWS
         pieces = call(
-            functools.partial(pair_kernel, chip_of),
+            functools.partial(rep_sum_kernel, giver, chip_of),
             (shape(tall, hidden_width, F32),) + (shape(tall, hidden_width, BF16),) * (chips - 1),
-            (pltpu.VMEM((chips, piece, hidden_width), F32),),
-        )(own_half, got_half)
+            (
+                pltpu.VMEM((chips, piece, hidden_width), F32),
+                pltpu.VMEM((reps, BIAS_ROWS, hidden_width), F32),
+            ),
+        )(thirds[0], *got)
         got = [to_chip(pieces[k], k) for k in range(1, chips)]
     else:
         blocks = [lax.all_gather(hidden, "feat", axis=0, tiled=True)]
         order = [lambda: 0]
 
     stack_bytes = batches * rows_one * (hidden_width + sets * width) * 2
-    bias_one, *panels = call(
+    panels = call(
         functools.partial(panel_kernel, taker, order, parts),
-        (shape(1, hidden_width, F32), shape(share, hidden_width, F32))
-        + (shape(share, hidden_width, BF16),) * (reps - 1),
+        (shape(share, hidden_width, F32),) + (shape(share, hidden_width, BF16),) * (reps - 1),
         (
             pltpu.VMEM((batches * rows_one, hidden_width), BF16),
             pltpu.VMEM((reps, share, hidden_width), F32),
@@ -386,81 +421,66 @@
     )(*gathered, *blocks)
     got_panel = [to_rep(panels[k], k) for k in range(1, reps)]
     if direct:
-        mine = call(
-            functools.partial(plane_sum_kernel, chip_of),
-            shape(piece + BIAS_ROWS, hidden_width, F32),
-            (pltpu.VMEM((chips, BIAS_ROWS, hidden_width), F32),),
-        )(bias_one, pieces[0], *got)
+        mine, bias_two = call(
+            functools.partial(plane_sum_kernel, chip_of, order),
+            (shape(tall, hidden_width, BF16), shape(8, hidden_width, F32)),
+            (
+                pltpu.VMEM((chips, BIAS_ROWS, hidden_width), F32),
+                pltpu.VMEM((feat, 1, hidden_width), F32),
+            ),
+        )(pieces[0], *blocks, *got)
+        got = [to_rep(mine, k) for k in range(1, reps)]
+        upper, bias_one = call(
+            functools.partial(rep_join_kernel, giver),
+            (jax.ShapeDtypeStruct((reps, piece, hidden_width), BF16), shape(8, hidden_width, F32)),
+            (pltpu.VMEM((reps, BIAS_ROWS, hidden_width), BF16),),
+        )(mine, *got)
     else:
-        summed = lax.psum(own_half, "feat")
-        mine = jnp.concatenate([summed[:half], bias_one, summed[half + 1 :]], 0)
-    tall = mine.shape[0]
-    if flip and reps > 2:
-        got_upper = to_rep(mine, 1)
-        mine = call(rep_pair_kernel, shape(tall, hidden_width, BF16))(mine, got_upper)
-        k = 2
-        while k < reps // 2:
-            got_upper = to_rep(mine, k)
-            mine = call(rep_more_kernel, shape(tall, hidden_width, BF16))(mine, got_upper)
-            k *= 2
-        got_upper = to_rep(mine, k)
-        upper, bias_one, bias_two = call(
-            finish_kernel,
-            (
-                shape(tall - BIAS_ROWS, hidden_width, BF16),
-                shape(1, hidden_width, F32),
-                shape(1, hidden_width, F32),
-            ),
-        )(mine, got_upper)
-    else:
-        mine = lax.psum(mine, "rep")
-        upper = mine[:-BIAS_ROWS].astype(BF16)
-        bias_one, bias_two = mine[-BIAS_ROWS:][0:1], mine[-BIAS_ROWS:][1:2]
+        summed = lax.psum(own_half, ("feat", "rep"))
+        upper, bias_two = summed[:half], summed[half : half + 1]
+        bias_one = lax.psum(jnp.sum(blocks[0].astype(F32), 0, keepdims=True), "rep")
     panel = call(panel_sum_kernel, shape(share, hidden_width, BF16))(panels[0], *got_panel)
 
-    if flip:
-        panel_all, near = [panel], [panel]
-        held = [0]
-        k = reps // 2
-        while k:
-            if len(panel_all) > 1:
-                packed = call(
-                    pack_kernel,
-                    jax.ShapeDtypeStruct((len(held), share, hidden_width), BF16),
-                )(*near)
-            else:
-                packed = panel[None]
-            came = to_rep(packed, k)
-            near = near + [came]
-            panel_all = near
-            held = held + [h ^ k for h in held]
-            k //= 2
-    else:
-        panel_all = [panel] + [to_rep(panel, k) for k in range(1, reps)]
-        held = list(range(reps))
+    panel_all = [panel] + [to_rep(panel, k) for k in range(1, reps)]
     grad_w1 = call(
-        functools.partial(place_kernel, [functools.partial(giver, k) for k in held]),
+        functools.partial(place_kernel, [functools.partial(giver, k) for k in range(reps)]),
         jax.ShapeDtypeStruct((reps, share, hidden_width), F32),
+        (
+            pltpu.VMEM((reps, share, hidden_width), F32),
+            pltpu.SemaphoreType.DMA((reps,)),
+        ),
+        out_specs=pl.BlockSpec(memory_space=pltpu.HBM),
     )(*panel_all)
     grad_w1 = grad_w1.reshape(sets, width, hidden_width)
     if direct:
         upper_all = [upper] + [to_chip(upper, k) for k in range(1, chips)]
         upper_all = upper_all + [to_core(u) for u in upper_all]
         places = []
-        for flip in range(cores):
+        for turn in range(cores):
             for k in range(chips):
                 places.append(
-                    lambda flip=flip, k=k: lax.bitwise_xor(core_of(), jnp.int32(flip)) * chips
-                    + lax.bitwise_xor(chip_of(), jnp.int32(k))
+                    lambda turn=turn, k=k: (
+                        lax.bitwise_xor(core_of(), jnp.int32(turn)),
+                        lax.bitwise_xor(chip_of(), jnp.int32(k)),
+                    )
                 )
-        grad_w2 = call(
-            functools.partial(place_kernel, places),
-            jax.ShapeDtypeStruct((feat, piece, hidden_width), F32),
-        )(*upper_all)
+        grad_w2, bias_one, bias_two = call(
+            functools.partial(place_two_kernel, places),
+            (
+                jax.ShapeDtypeStruct((cores, reps, chips, piece, hidden_width), F32),
+                jax.ShapeDtypeStruct((hidden_width,), F32),
+                jax.ShapeDtypeStruct((hidden_width,), F32),
+            ),
+            (
+                pltpu.VMEM((feat, reps, piece, hidden_width), F32),
+                pltpu.SemaphoreType.DMA((feat + 2,)),
+            ),
+            out_specs=[pl.BlockSpec(memory_space=pltpu.HBM)] * 3,
+        )(*upper_all, bias_one, bias_two)
     else:
-        grad_w2 = upper.astype(F32)
+        grad_w2, bias_one, bias_two = upper, bias_one[0], bias_two[0]
     grad_w2 = grad_w2.reshape(sets, hidden_width, hidden_width)
-    return (grad_w1, bias_one[0], grad_w2, bias_two[0])
+    return (grad_w1, bias_one, grad_w2, bias_two)
 
 
 def solution(mesh):

time: 59.9 us -> 60.9 us (1.017)
  starting transfers between devices: 27.1 us -> 35.5 us
  waiting for transfers between devices: 20.1 us -> 13.2 us
    ppermute x7 -> x12, starting transfers between devices: 14.4 us -> 22.5 us  [to_rep(): return lax.ppermute(value, 'rep', pairs)]
    ppermute x7 -> x12, waiting for transfers between devices: 10.5 us -> 3.52 us  [to_rep(): return lax.ppermute(value, 'rep', pairs)]
    pallas_call x7 -> x6, Pallas kernels: 3.23 us -> 2.81 us  [the longest x1 1.24 us: on_device(): call(functools.partial(place_two_kernel, places), (jax.ShapeDtypeStruct((...]
  transfers between devices with their start and end apart: 25 -> 30, of which waited for: 11 -> 12; matrix products, arithmetic and copies ran while one was open for 0% -> 0% of each run, Pallas kernels for 14% -> 13%
where the time goes in v1:
time: 60.9 us; the launch traced here: 60.8 us
  starting transfers between devices  35.5 us (58%)
  waiting for transfers between devices  13.2 us (22%)
  Pallas kernels  11.3 us (19%)
  between operations  0.78 us (1%)
    ppermute x12, starting transfers between devices, to_rep(): return lax.ppermute(value, 'rep', pairs)  22.5 us
    ppermute x9, starting transfers between devices, to_chip(): return lax.ppermute(value, 'feat', pairs)  11.6 us
    ppermute x9, waiting for transfers between devices, to_chip(): return lax.ppermute(value, 'feat', pairs)  9.69 us
    pallas_call x2, Pallas kernels, on_device(): call(functools.partial(gather_kernel, n * run, run), shape(sets * width,...  4.25 us
    ppermute x12, waiting for transfers between devices, to_rep(): return lax.ppermute(value, 'rep', pairs)  3.52 us
    pallas_call x1, Pallas kernels, on_device(): call(functools.partial(upper_kernel, factor, core_of if direct else lambd...  2.21 us
    ppermute x9, starting transfers between devices, to_core(): return lax.ppermute(value, 'feat', [(i, i ^ 1) for i in range(feat)])  1.28 us
    pallas_call x1, Pallas kernels, on_device(): call(functools.partial(place_two_kernel, places), (jax.ShapeDtypeStruct((...  1.24 us
  transfers between devices with their start and end apart: 30, of which 12 were waited for; matrix products, arithmetic and copies ran while one was open for 0% of the time, Pallas kernels for 13%

profile of v1, /device:TPU:0, one launch (start us, length us, event | category | flops | bytes accessed | tf_op | source)
XLA Modules:
  0.0 60.8 jit_solution(1521958861176497559)
XLA Ops:
  0.6 2.2 %shard_map.93 = (f32[784,256]{1,0:T(8,128)S(1)}, f32[784,256]{1,0:T(8,128)S(1)}, bf16[128,256]{1,0:T(8,128)(2,1)S(1)}, s32[5,8,256]{2,1,0:T(8,128)S(1)}, bf16[25...) custom-call(bf16[128,256]{1,0:T(8,128)(2,1)} %bitcast.11, ...), custom_call_target="tpu_custom_call" | custom-call | flops 1000000 | bytes 1000000 | tf_op jit(solution)/shard_map/pallas_call | solution.py:326
  2.8 0.6 collective-permute-start.13
  3.4 1.1 %shard_map.96.refs_2_.refs_0_ = bf16[256,256]{1,0:T(8,128)(2,1)S(1)} custom-call(bf16[256,256]{1,0:T(8,128)(2,1)S(1)} %get-tuple-element.33.pre_ref, s32[5,8,256]{2,1,0:T(8,128)S(1)} %get-tuple-element.34.words_ref, bf16[6,256,256]{2,1,0:T(8,128)(2,1)S(1)} %get-tuple-element.35.weight_ref, bf16[128,256]{1,0:T(8,128)(2,1)S(1)} %get-tuple-element.36.grad_ref), custom_call_target="tpu_custom_call" | custom-call | flops 1000000 | bytes 1000000 | tf_op jit(solution)/shard_map/pallas_call | solution.py:337
  4.5 3.5 %collective-permute-start.2 = (bf16[256,256]{1,0:T(8,128)(2,1)S(1)}, bf16[256,256]{1,0:T(8,128)(2,1)S(1)}, u32[]{:S(2)}, u32[]{:S(2)}) collective-permute-start(bf16[256,256]{1,0:T(8,128)(2,1)S(1)} %shard_map.96.refs_2_.refs_0_), channel_id=1, source_target_pairs={{0,24},{4,28},{8,16},{12,20},{16,8},{20,12},{24,0},{28,4},{1,25},{... | collective-permute-start | bytes 393224 | tf_op jit(solution)/shard_map/ppermute | solution.py:357
  9.1 3.1 %collective-permute-done.2.refs_5_.refs_3_ = bf16[256,256]{1,0:T(8,128)(2,1)S(1)} collective-permute-done((bf16[256,256]{1,0:T(8,128)(2,1)S(1)}, bf16[256,256]{1,0:T(8,128)(2,1)S(1)}, u32[]{:S(2)}, u32[]{:S(2)}) %collective-permute-start.2) | collective-permute-done | bytes 131104 | tf_op jit(solution)/shard_map/ppermute | solution.py:357
  12.3 2.1 %shard_map.95.refs_1_ = bf16[768,1024]{1,0:T(8,128)(2,1)S(1)} custom-call(bf16[8,128,512]{2,1,0:T(8,128)(2,1)S(1)} %get-tuple-element.31.column_ref, s32[8,5,16,512]{3,2,1,0:T(8,128)S(1)} %get-tuple-element.32.word_ref), custom_call_target="tpu_custom_call" | custom-call | flops 3000000000 | bytes 1000000 | tf_op jit(solution)/shard_map/pallas_call | solution.py:346
  14.4 0.6 collective-permute-done.1.refs_4_.refs_2_
  15.6 1.8 %collective-permute-start.14 = (bf16[208,256]{1,0:T(8,128)(2,1)S(1)}, bf16[208,256]{1,0:T(8,128)(2,1)S(1)}, u32[]{:S(2)}, u32[]{:S(2)}) collective-permute-start(bf16[208,256]{1,0:T(8,128)(2,1)S(1)} %get-tuple-element.44), channel_id=1, source_target_pairs={{0,1},{1,0},{2,3},{3,2},{4,5},{5,4},{6,7},{7,6},{8,9},{9,8},{10,11... | collective-permute-start | bytes 319496 | tf_op jit(solution)/shard_map/ppermute | solution.py:374
  17.5 2.6 %collective-permute-start.15 = (bf16[208,256]{1,0:T(8,128)(2,1)S(1)}, bf16[208,256]{1,0:T(8,128)(2,1)S(1)}, u32[]{:S(2)}, u32[]{:S(2)}) collective-permute-start(bf16[208,256]{1,0:T(8,128)(2,1)S(1)} %get-tuple-element.45), channel_id=1, source_target_pairs={{0,2},{1,3},{2,0},{3,1},{4,6},{5,7},{6,4},{7,5},{8,10},{9,11},{10,... | collective-permute-start | bytes 319496 | tf_op jit(solution)/shard_map/ppermute | solution.py:374
  20.1 2.1 %shard_map.94.refs_0_ = bf16[768,1024]{1,0:T(8,128)(2,1)S(1)} custom-call(bf16[8,128,512]{2,1,0:T(8,128)(2,1)S(1)} %get-tuple-element.31.column_ref, s32[8,5,16,512]{3,2,1,0:T(8,128)S(1)} %get-tuple-element.32.word_ref), custom_call_target="tpu_custom_call" | custom-call | flops 3000000000 | bytes 1000000 | tf_op jit(solution)/shard_map/pallas_call | solution.py:346
  22.2 1.1 %shard_map.97 = (f32[192,256]{1,0:T(8,128)S(1)}, bf16[192,256]{1,0:T(8,128)(2,1)S(1)}, bf16[192,256]{1,0:T(8,128)(2,1)S(1)}, bf16[192,256]{1,0:T(8,128)(2,1)S(1)}) custom-call(bf16[768,1024]{1,0:T(8,128)(2,1)S(1)} %shard_map.94.refs_0_, bf16[768,1024]{1,0:T(8,128)(2,1)S(1)} %shard_map.95.refs_1_, bf16[256,256]{1,0:T(8,128)(2,1)S(1)} %shard_map.96.refs_2_.refs_0_, ...), custom_call_target="tpu_custom_call" | custom-call | flops 1000000 | bytes 1000000 | tf_op jit(solution)/shard_map/pallas_call | solution.py:413
  23.4 0.9 %collective-permute-start.7 = (bf16[192,256]{1,0:T(8,128)(2,1)S(1)}, bf16[192,256]{1,0:T(8,128)(2,1)S(1)}, u32[]{:S(2)}, u32[]{:S(2)}) collective-permute-start(bf16[192,256]{1,0:T(8,128)(2,1)S(1)} %get-tuple-element.38), channel_id=1, source_target_pairs={{0,1},{1,0},{2,3},{3,2},{4,5},{5,4},{6,7},{7,6},{8,9},{9,8},{10,11... | collective-permute-start | bytes 294920 | tf_op jit(solution)/shard_map/ppermute | solution.py:374
  24.3 3.5 %collective-permute-start.8 = (bf16[192,256]{1,0:T(8,128)(2,1)S(1)}, bf16[192,256]{1,0:T(8,128)(2,1)S(1)}, u32[]{:S(2)}, u32[]{:S(2)}) collective-permute-start(bf16[192,256]{1,0:T(8,128)(2,1)S(1)} %get-tuple-element.39), channel_id=1, source_target_pairs={{0,2},{1,3},{2,0},{3,1},{4,6},{5,7},{6,4},{7,5},{8,10},{9,11},{10,... | collective-permute-start | bytes 294920 | tf_op jit(solution)/shard_map/ppermute | solution.py:374
  27.8 1.3 %collective-permute-done.15.refs_1_ = bf16[208,256]{1,0:T(8,128)(2,1)S(1)} collective-permute-done((bf16[208,256]{1,0:T(8,128)(2,1)S(1)}, bf16[208,256]{1,0:T(8,128)(2,1)S(1)}, u32[]{:S(2)}, u32[]{:S(2)}) %collective-permute-start.15) | collective-permute-done | bytes 106528 | tf_op jit(solution)/shard_map/ppermute | solution.py:374
  29.2 1.2 %collective-permute-start.17 = (bf16[64,256]{1,0:T(8,128)(2,1)S(1)}, bf16[64,256]{1,0:T(8,128)(2,1)S(1)}, u32[]{:S(2)}, u32[]{:S(2)}) collective-permute-start(bf16[64,256]{1,0:T(8,128)(2,1)S(1)} %get-tuple-element.48), channel_id=1, source_target_pairs={{0,8},{4,12},{8,0},{12,4},{16,24},{20,28},{24,16},{28,20},{1,9},{5... | collective-permute-start | bytes 98312 | tf_op jit(solution)/shard_map/ppermute | solution.py:357
  30.5 2.5 %collective-permute-start.9 = (bf16[192,256]{1,0:T(8,128)(2,1)S(1)}, bf16[192,256]{1,0:T(8,128)(2,1)S(1)}, u32[]{:S(2)}, u32[]{:S(2)}) collective-permute-start(bf16[192,256]{1,0:T(8,128)(2,1)S(1)} %get-tuple-element.40), channel_id=1, source_target_pairs={{0,3},{1,2},{2,1},{3,0},{4,7},{5,6},{6,5},{7,4},{8,11},{9,10},{10,... | collective-permute-start | bytes 294920 | tf_op jit(solution)/shard_map/ppermute | solution.py:374
  32.9 1.5 %collective-permute-start.18 = (bf16[64,256]{1,0:T(8,128)(2,1)S(1)}, bf16[64,256]{1,0:T(8,128)(2,1)S(1)}, u32[]{:S(2)}, u32[]{:S(2)}) collective-permute-start(bf16[64,256]{1,0:T(8,128)(2,1)S(1)} %get-tuple-element.49), channel_id=1, source_target_pairs={{0,16},{4,20},{8,24},{12,28},{16,0},{20,4},{24,8},{28,12},{1,17},{... | collective-permute-start | bytes 98312 | tf_op jit(solution)/shard_map/ppermute | solution.py:357
  34.5 0.9 %collective-permute-start.19 = (bf16[64,256]{1,0:T(8,128)(2,1)S(1)}, bf16[64,256]{1,0:T(8,128)(2,1)S(1)}, u32[]{:S(2)}, u32[]{:S(2)}) collective-permute-start(bf16[64,256]{1,0:T(8,128)(2,1)S(1)} %get-tuple-element.50), channel_id=1, source_target_pairs={{0,24},{4,28},{8,16},{12,20},{16,8},{20,12},{24,0},{28,4},{1,25},{... | collective-permute-start | bytes 98312 | tf_op jit(solution)/shard_map/ppermute | solution.py:357
  35.4 1.5 %collective-permute-done.18.refs_9_ = bf16[64,256]{1,0:T(8,128)(2,1)S(1)} collective-permute-done((bf16[64,256]{1,0:T(8,128)(2,1)S(1)}, bf16[64,256]{1,0:T(8,128)(2,1)S(1)}, u32[]{:S(2)}, u32[]{:S(2)}) %collective-permute-start.18) | collective-permute-done | bytes 32800 | tf_op jit(solution)/shard_map/ppermute | solution.py:357
  36.8 2.4 %collective-permute-done.19.refs_10_ = bf16[64,256]{1,0:T(8,128)(2,1)S(1)} collective-permute-done((bf16[64,256]{1,0:T(8,128)(2,1)S(1)}, bf16[64,256]{1,0:T(8,128)(2,1)S(1)}, u32[]{:S(2)}, u32[]{:S(2)}) %collective-permute-start.19) | collective-permute-done | bytes 32800 | tf_op jit(solution)/shard_map/ppermute | solution.py:357
  39.5 1.4 %collective-permute-start.22 = (bf16[64,256]{1,0:T(8,128)(2,1)S(1)}, bf16[64,256]{1,0:T(8,128)(2,1)S(1)}, u32[]{:S(2)}, u32[]{:S(2)}) collective-permute-start(bf16[64,256]{1,0:T(8,128)(2,1)S(1)} %get-tuple-element.51.refs_0_), channel_id=1, source_target_pairs={{0,3},{1,2},{2,1},{3,0},{4,7},{5,6},{6,5},{7,4},{8,11},{9,10},{10,... | collective-permute-start | bytes 98312 | tf_op jit(solution)/shard_map/ppermute | solution.py:374
  40.9 5.2 %collective-permute-start.21 = (bf16[64,256]{1,0:T(8,128)(2,1)S(1)}, bf16[64,256]{1,0:T(8,128)(2,1)S(1)}, u32[]{:S(2)}, u32[]{:S(2)}) collective-permute-start(bf16[64,256]{1,0:T(8,128)(2,1)S(1)} %get-tuple-element.51.refs_0_), channel_id=1, source_target_pairs={{0,2},{1,3},{2,0},{3,1},{4,6},{5,7},{6,4},{7,5},{8,10},{9,11},{10,... | collective-permute-start | bytes 98312 | tf_op jit(solution)/shard_map/ppermute | solution.py:374
  46.2 1.8 %collective-permute-start.12 = (bf16[192,256]{1,0:T(8,128)(2,1)S(1)}, bf16[192,256]{1,0:T(8,128)(2,1)S(1)}, u32[]{:S(2)}, u32[]{:S(2)}) collective-permute-start(bf16[192,256]{1,0:T(8,128)(2,1)S(1)} %shard_map.98.refs_0_), channel_id=1, source_target_pairs={{0,3},{1,2},{2,1},{3,0},{4,7},{5,6},{6,5},{7,4},{8,11},{9,10},{10,... | collective-permute-start | bytes 294920 | tf_op jit(solution)/shard_map/ppermute | solution.py:374
  47.9 1.8 %collective-permute-start.11 = (bf16[192,256]{1,0:T(8,128)(2,1)S(1)}, bf16[192,256]{1,0:T(8,128)(2,1)S(1)}, u32[]{:S(2)}, u32[]{:S(2)}) collective-permute-start(bf16[192,256]{1,0:T(8,128)(2,1)S(1)} %shard_map.98.refs_0_), channel_id=1, source_target_pairs={{0,2},{1,3},{2,0},{3,1},{4,6},{5,7},{6,4},{7,5},{8,10},{9,11},{10,... | collective-permute-start | bytes 294920 | tf_op jit(solution)/shard_map/ppermute | solution.py:374
  49.7 0.6 %collective-permute-done.20.refs_1_ = bf16[64,256]{1,0:T(8,128)(2,1)S(1)} collective-permute-done((bf16[64,256]{1,0:T(8,128)(2,1)S(1)}, bf16[64,256]{1,0:T(8,128)(2,1)S(1)}, u32[]{:S(2)}, u32[]{:S(2)}) %collective-permute-start.20) | collective-permute-done | bytes 32800 | tf_op jit(solution)/shard_map/ppermute | solution.py:374
  50.4 1.8 %collective-permute-start.25 = (bf16[4,48,256]{2,1,0:T(8,128)(2,1)S(1)}, bf16[4,48,256]{2,1,0:T(8,128)(2,1)S(1)}, u32[]{:S(2)}, u32[]{:S(2)}) collective-permute-start(bf16[4,48,256]{2,1,0:T(8,128)(2,1)S(1)} %get-tuple-element.52.refs_0_), channel_id=1, source_target_pairs={{0,24},{4,28},{8,16},{12,20},{16,8},{20,12},{24,0},{28,4},{1,25},{... | collective-permute-start | bytes 294920 | tf_op jit(solution)/shard_map/ppermute | solution.py:357
  52.7 1.2 %collective-permute-start.23 = (bf16[4,48,256]{2,1,0:T(8,128)(2,1)S(1)}, bf16[4,48,256]{2,1,0:T(8,128)(2,1)S(1)}, u32[]{:S(2)}, u32[]{:S(2)}) collective-permute-start(bf16[4,48,256]{2,1,0:T(8,128)(2,1)S(1)} %get-tuple-element.52.refs_0_), channel_id=1, source_target_pairs={{0,8},{4,12},{8,0},{12,4},{16,24},{20,28},{24,16},{28,20},{1,9},{5... | collective-permute-start | bytes 294920 | tf_op jit(solution)/shard_map/ppermute | solution.py:357
  54.0 1.0 %collective-permute-start.10 = (bf16[192,256]{1,0:T(8,128)(2,1)S(1)}, bf16[192,256]{1,0:T(8,128)(2,1)S(1)}, u32[]{:S(2)}, u32[]{:S(2)}) collective-permute-start(bf16[192,256]{1,0:T(8,128)(2,1)S(1)} %shard_map.98.refs_0_), channel_id=1, source_target_pairs={{0,1},{1,0},{2,3},{3,2},{4,5},{5,4},{6,7},{7,6},{8,9},{9,8},{10,11... | collective-permute-start | bytes 294920 | tf_op jit(solution)/shard_map/ppermute | solution.py:374
  56.0 1.0 %collective-permute-done.24.refs_2_ = bf16[4,48,256]{2,1,0:T(8,128)(2,1)S(1)} collective-permute-done((bf16[4,48,256]{2,1,0:T(8,128)(2,1)S(1)}, bf16[4,48,256]{2,1,0:T(8,128)(2,1)S(1)}, u32[]{:S(2)}, u32[]{:S(2)}) %collective-permute-start.24) | collective-permute-done | bytes 98336 | tf_op jit(solution)/shard_map/ppermute | solution.py:357
  57.5 1.0 %collective-permute-done.10.refs_1_ = bf16[192,256]{1,0:T(8,128)(2,1)S(1)} collective-permute-done((bf16[192,256]{1,0:T(8,128)(2,1)S(1)}, bf16[192,256]{1,0:T(8,128)(2,1)S(1)}, u32[]{:S(2)}, u32[]{:S(2)}) %collective-permute-start.10) | collective-permute-done | bytes 98336 | tf_op jit(solution)/shard_map/ppermute | solution.py:374
  58.6 0.9 %shard_map.99 = f32[4,192,256]{2,1,0:T(8,128)} custom-call(bf16[192,256]{1,0:T(8,128)(2,1)S(1)} %shard_map.98.refs_0_, bf16[192,256]{1,0:T(8,128)(2,1)S(1)} %collective-permute-done.10.refs_1_, bf16[192,256]{1,0:T(8,128)(2,1)S(1)} %collective-permute-done.11.refs_2_, bf16[192,256]{1,0:T(8,128)(2,1)S(1)} %collective-permute-done.12.refs_3_), custom_call_target="tpu_custom_call" | custom-call | flops 1000000 | bytes 1000000 | tf_op jit(solution)/shard_map/pallas_call | solution.py:445
  59.5 1.2 %shard_map.104 = (f32[2,4,4,48,256]{4,3,2,1,0:T(8,128)}, f32[256]{0:T(256)}, f32[256]{0:T(256)}) custom-call(bf16[4,48,256]{2,1,0:T(8,128)(2,1)S(1)} %get-tuple-element.52.refs_0_, bf16[4,48,256]{2,1,0:T(8,128)(2,1)S(1)} %collective-permute-done.23.refs_1_, bf16[4,48,256]{2,1,0:T(8,128)(2,1)S(1)} %collective-permute-done.24.refs_2_, ...), custom_call_target="tpu_custom_call" | custom-call | flops 1000000 | bytes 1000000 | tf_op jit(solution)/shard_map/pallas_call | solution.py:467
  (40 shorter events, 4.2 us)
Async XLA Ops:
  2.8 12.6 %collective-permute-start.13 = (f32[784,256]{1,0:T(8,128)S(1)}, f32[784,256]{1,0:T(8,128)S(1)}, u32[]{:S(2)}, u32[]{:S(2)}) collective-permute-start(f32[784,256]{1,0:T(8,128)S(1)} %get-tuple-element.42), channel_id=1, source_target_pairs={{0,4},{4,0},{8,12},{12,8},{16,20},{20,16},{24,28},{28,24},{1,5},{5... | collective-permute-start | bytes 2408456 | tf_op jit(solution)/shard_map/ppermute | solution.py:360
  4.5 7.8 %collective-permute-start.2 = (bf16[256,256]{1,0:T(8,128)(2,1)S(1)}, bf16[256,256]{1,0:T(8,128)(2,1)S(1)}, u32[]{:S(2)}, u32[]{:S(2)}) collective-permute-start(bf16[256,256]{1,0:T(8,128)(2,1)S(1)} %shard_map.96.refs_2_.refs_0_), channel_id=1, source_target_pairs={{0,24},{4,28},{8,16},{12,20},{16,8},{20,12},{24,0},{28,4},{1,25},{... | collective-permute-start | bytes 393224 | tf_op jit(solution)/shard_map/ppermute | solution.py:357
  8.0 9.5 %collective-permute-start.3 = (bf16[256,256]{1,0:T(8,128)(2,1)S(1)}, bf16[256,256]{1,0:T(8,128)(2,1)S(1)}, u32[]{:S(2)}, u32[]{:S(2)}) collective-permute-start(bf16[256,256]{1,0:T(8,128)(2,1)S(1)} %shard_map.96.refs_2_.refs_0_), channel_id=1, source_target_pairs={{0,4},{4,0},{8,12},{12,8},{16,20},{20,16},{24,28},{28,24},{1,5},{5... | collective-permute-start | bytes 393224 | tf_op jit(solution)/shard_map/ppermute | solution.py:360
  8.2 6.8 %collective-permute-start.1 = (bf16[256,256]{1,0:T(8,128)(2,1)S(1)}, bf16[256,256]{1,0:T(8,128)(2,1)S(1)}, u32[]{:S(2)}, u32[]{:S(2)}) collective-permute-start(bf16[256,256]{1,0:T(8,128)(2,1)S(1)} %shard_map.96.refs_2_.refs_0_), channel_id=1, source_target_pairs={{0,16},{4,20},{8,24},{12,28},{16,0},{20,4},{24,8},{28,12},{1,17},{... | collective-permute-start | bytes 393224 | tf_op jit(solution)/shard_map/ppermute | solution.py:357
  8.7 6.5 %collective-permute-start = (bf16[256,256]{1,0:T(8,128)(2,1)S(1)}, bf16[256,256]{1,0:T(8,128)(2,1)S(1)}, u32[]{:S(2)}, u32[]{:S(2)}) collective-permute-start(bf16[256,256]{1,0:T(8,128)(2,1)S(1)} %shard_map.96.refs_2_.refs_0_), channel_id=1, source_target_pairs={{0,8},{4,12},{8,0},{12,4},{16,24},{20,28},{24,16},{28,20},{1,9},{5... | collective-permute-start | bytes 393224 | tf_op jit(solution)/shard_map/ppermute | solution.py:357
  12.3 7.8 %collective-permute-start.6 = (bf16[256,256]{1,0:T(8,128)(2,1)S(1)}, bf16[256,256]{1,0:T(8,128)(2,1)S(1)}, u32[]{:S(2)}, u32[]{:S(2)}) collective-permute-start(bf16[256,256]{1,0:T(8,128)(2,1)S(1)} %collective-permute-done.2.refs_5_.refs_3_), channel_id=1, source_target_pairs={{0,4},{4,0},{8,12},{12,8},{16,20},{20,16},{24,28},{28,24},{1,5},{5... | collective-permute-start | bytes 393224 | tf_op jit(solution)/shard_map/ppermute | solution.py:360
  15.0 7.3 %collective-permute-start.5 = (bf16[256,256]{1,0:T(8,128)(2,1)S(1)}, bf16[256,256]{1,0:T(8,128)(2,1)S(1)}, u32[]{:S(2)}, u32[]{:S(2)}) collective-permute-start(bf16[256,256]{1,0:T(8,128)(2,1)S(1)} %collective-permute-done.1.refs_4_.refs_2_), channel_id=1, source_target_pairs={{0,4},{4,0},{8,12},{12,8},{16,20},{20,16},{24,28},{28,24},{1,5},{5... | collective-permute-start | bytes 393224 | tf_op jit(solution)/shard_map/ppermute | solution.py:360
  15.3 7.0 %collective-permute-start.4 = (bf16[256,256]{1,0:T(8,128)(2,1)S(1)}, bf16[256,256]{1,0:T(8,128)(2,1)S(1)}, u32[]{:S(2)}, u32[]{:S(2)}) collective-permute-start(bf16[256,256]{1,0:T(8,128)(2,1)S(1)} %collective-permute-done.refs_3_.refs_1_), channel_id=1, source_target_pairs={{0,4},{4,0},{8,12},{12,8},{16,20},{20,16},{24,28},{28,24},{1,5},{5... | collective-permute-start | bytes 393224 | tf_op jit(solution)/shard_map/ppermute | solution.py:360
  15.6 12.2 %collective-permute-start.14 = (bf16[208,256]{1,0:T(8,128)(2,1)S(1)}, bf16[208,256]{1,0:T(8,128)(2,1)S(1)}, u32[]{:S(2)}, u32[]{:S(2)}) collective-permute-start(bf16[208,256]{1,0:T(8,128)(2,1)S(1)} %get-tuple-element.44), channel_id=1, source_target_pairs={{0,1},{1,0},{2,3},{3,2},{4,5},{5,4},{6,7},{7,6},{8,9},{9,8},{10,11... | collective-permute-start | bytes 319496 | tf_op jit(solution)/shard_map/ppermute | solution.py:374
  17.5 11.7 %collective-permute-start.15 = (bf16[208,256]{1,0:T(8,128)(2,1)S(1)}, bf16[208,256]{1,0:T(8,128)(2,1)S(1)}, u32[]{:S(2)}, u32[]{:S(2)}) collective-permute-start(bf16[208,256]{1,0:T(8,128)(2,1)S(1)} %get-tuple-element.45), channel_id=1, source_target_pairs={{0,2},{1,3},{2,0},{3,1},{4,6},{5,7},{6,4},{7,5},{8,10},{9,11},{10,... | collective-permute-start | bytes 319496 | tf_op jit(solution)/shard_map/ppermute | solution.py:374
  20.1 9.1 %collective-permute-start.16 = (bf16[208,256]{1,0:T(8,128)(2,1)S(1)}, bf16[208,256]{1,0:T(8,128)(2,1)S(1)}, u32[]{:S(2)}, u32[]{:S(2)}) collective-permute-start(bf16[208,256]{1,0:T(8,128)(2,1)S(1)} %get-tuple-element.46), channel_id=1, source_target_pairs={{0,3},{1,2},{2,1},{3,0},{4,7},{5,6},{6,5},{7,4},{8,11},{9,10},{10,... | collective-permute-start | bytes 319496 | tf_op jit(solution)/shard_map/ppermute | solution.py:374
  23.4 22.7 %collective-permute-start.7 = (bf16[192,256]{1,0:T(8,128)(2,1)S(1)}, bf16[192,256]{1,0:T(8,128)(2,1)S(1)}, u32[]{:S(2)}, u32[]{:S(2)}) collective-permute-start(bf16[192,256]{1,0:T(8,128)(2,1)S(1)} %get-tuple-element.38), channel_id=1, source_target_pairs={{0,1},{1,0},{2,3},{3,2},{4,5},{5,4},{6,7},{7,6},{8,9},{9,8},{10,11... | collective-permute-start | bytes 294920 | tf_op jit(solution)/shard_map/ppermute | solution.py:374
  24.3 21.8 %collective-permute-start.8 = (bf16[192,256]{1,0:T(8,128)(2,1)S(1)}, bf16[192,256]{1,0:T(8,128)(2,1)S(1)}, u32[]{:S(2)}, u32[]{:S(2)}) collective-permute-start(bf16[192,256]{1,0:T(8,128)(2,1)S(1)} %get-tuple-element.39), channel_id=1, source_target_pairs={{0,2},{1,3},{2,0},{3,1},{4,6},{5,7},{6,4},{7,5},{8,10},{9,11},{10,... | collective-permute-start | bytes 294920 | tf_op jit(solution)/shard_map/ppermute | solution.py:374
  29.2 5.2 %collective-permute-start.17 = (bf16[64,256]{1,0:T(8,128)(2,1)S(1)}, bf16[64,256]{1,0:T(8,128)(2,1)S(1)}, u32[]{:S(2)}, u32[]{:S(2)}) collective-permute-start(bf16[64,256]{1,0:T(8,128)(2,1)S(1)} %get-tuple-element.48), channel_id=1, source_target_pairs={{0,8},{4,12},{8,0},{12,4},{16,24},{20,28},{24,16},{28,20},{1,9},{5... | collective-permute-start | bytes 98312 | tf_op jit(solution)/shard_map/ppermute | solution.py:357
  30.5 15.6 %collective-permute-start.9 = (bf16[192,256]{1,0:T(8,128)(2,1)S(1)}, bf16[192,256]{1,0:T(8,128)(2,1)S(1)}, u32[]{:S(2)}, u32[]{:S(2)}) collective-permute-start(bf16[192,256]{1,0:T(8,128)(2,1)S(1)} %get-tuple-element.40), channel_id=1, source_target_pairs={{0,3},{1,2},{2,1},{3,0},{4,7},{5,6},{6,5},{7,4},{8,11},{9,10},{10,... | collective-permute-start | bytes 294920 | tf_op jit(solution)/shard_map/ppermute | solution.py:374
  32.9 3.9 %collective-permute-start.18 = (bf16[64,256]{1,0:T(8,128)(2,1)S(1)}, bf16[64,256]{1,0:T(8,128)(2,1)S(1)}, u32[]{:S(2)}, u32[]{:S(2)}) collective-permute-start(bf16[64,256]{1,0:T(8,128)(2,1)S(1)} %get-tuple-element.49), channel_id=1, source_target_pairs={{0,16},{4,20},{8,24},{12,28},{16,0},{20,4},{24,8},{28,12},{1,17},{... | collective-permute-start | bytes 98312 | tf_op jit(solution)/shard_map/ppermute | solution.py:357
  34.5 4.8 %collective-permute-start.19 = (bf16[64,256]{1,0:T(8,128)(2,1)S(1)}, bf16[64,256]{1,0:T(8,128)(2,1)S(1)}, u32[]{:S(2)}, u32[]{:S(2)}) collective-permute-start(bf16[64,256]{1,0:T(8,128)(2,1)S(1)} %get-tuple-element.50), channel_id=1, source_target_pairs={{0,24},{4,28},{8,16},{12,20},{16,8},{20,12},{24,0},{28,4},{1,25},{... | collective-permute-start | bytes 98312 | tf_op jit(solution)/shard_map/ppermute | solution.py:357
  39.5 10.2 %collective-permute-start.22 = (bf16[64,256]{1,0:T(8,128)(2,1)S(1)}, bf16[64,256]{1,0:T(8,128)(2,1)S(1)}, u32[]{:S(2)}, u32[]{:S(2)}) collective-permute-start(bf16[64,256]{1,0:T(8,128)(2,1)S(1)} %get-tuple-element.51.refs_0_), channel_id=1, source_target_pairs={{0,3},{1,2},{2,1},{3,0},{4,7},{5,6},{6,5},{7,4},{8,11},{9,10},{10,... | collective-permute-start | bytes 98312 | tf_op jit(solution)/shard_map/ppermute | solution.py:374
  40.9 8.8 %collective-permute-start.21 = (bf16[64,256]{1,0:T(8,128)(2,1)S(1)}, bf16[64,256]{1,0:T(8,128)(2,1)S(1)}, u32[]{:S(2)}, u32[]{:S(2)}) collective-permute-start(bf16[64,256]{1,0:T(8,128)(2,1)S(1)} %get-tuple-element.51.refs_0_), channel_id=1, source_target_pairs={{0,2},{1,3},{2,0},{3,1},{4,6},{5,7},{6,4},{7,5},{8,10},{9,11},{10,... | collective-permute-start | bytes 98312 | tf_op jit(solution)/shard_map/ppermute | solution.py:374
  46.1 4.3 %collective-permute-start.20 = (bf16[64,256]{1,0:T(8,128)(2,1)S(1)}, bf16[64,256]{1,0:T(8,128)(2,1)S(1)}, u32[]{:S(2)}, u32[]{:S(2)}) collective-permute-start(bf16[64,256]{1,0:T(8,128)(2,1)S(1)} %get-tuple-element.51.refs_0_), channel_id=1, source_target_pairs={{0,1},{1,0},{2,3},{3,2},{4,5},{5,4},{6,7},{7,6},{8,9},{9,8},{10,11... | collective-permute-start | bytes 98312 | tf_op jit(solution)/shard_map/ppermute | solution.py:374
  46.2 7.8 %collective-permute-start.12 = (bf16[192,256]{1,0:T(8,128)(2,1)S(1)}, bf16[192,256]{1,0:T(8,128)(2,1)S(1)}, u32[]{:S(2)}, u32[]{:S(2)}) collective-permute-start(bf16[192,256]{1,0:T(8,128)(2,1)S(1)} %shard_map.98.refs_0_), channel_id=1, source_target_pairs={{0,3},{1,2},{2,1},{3,0},{4,7},{5,6},{6,5},{7,4},{8,11},{9,10},{10,... | collective-permute-start | bytes 294920 | tf_op jit(solution)/shard_map/ppermute | solution.py:374
  47.9 7.5 %collective-permute-start.11 = (bf16[192,256]{1,0:T(8,128)(2,1)S(1)}, bf16[192,256]{1,0:T(8,128)(2,1)S(1)}, u32[]{:S(2)}, u32[]{:S(2)}) collective-permute-start(bf16[192,256]{1,0:T(8,128)(2,1)S(1)} %shard_map.98.refs_0_), channel_id=1, source_target_pairs={{0,2},{1,3},{2,0},{3,1},{4,6},{5,7},{6,4},{7,5},{8,10},{9,11},{10,... | collective-permute-start | bytes 294920 | tf_op jit(solution)/shard_map/ppermute | solution.py:374
  50.4 5.6 %collective-permute-start.25 = (bf16[4,48,256]{2,1,0:T(8,128)(2,1)S(1)}, bf16[4,48,256]{2,1,0:T(8,128)(2,1)S(1)}, u32[]{:S(2)}, u32[]{:S(2)}) collective-permute-start(bf16[4,48,256]{2,1,0:T(8,128)(2,1)S(1)} %get-tuple-element.52.refs_0_), channel_id=1, source_target_pairs={{0,24},{4,28},{8,16},{12,20},{16,8},{20,12},{24,0},{28,4},{1,25},{... | collective-permute-start | bytes 294920 | tf_op jit(solution)/shard_map/ppermute | solution.py:357
  52.2 4.8 %collective-permute-start.24 = (bf16[4,48,256]{2,1,0:T(8,128)(2,1)S(1)}, bf16[4,48,256]{2,1,0:T(8,128)(2,1)S(1)}, u32[]{:S(2)}, u32[]{:S(2)}) collective-permute-start(bf16[4,48,256]{2,1,0:T(8,128)(2,1)S(1)} %get-tuple-element.52.refs_0_), channel_id=1, source_target_pairs={{0,16},{4,20},{8,24},{12,28},{16,0},{20,4},{24,8},{28,12},{1,17},{... | collective-permute-start | bytes 294920 | tf_op jit(solution)/shard_map/ppermute | solution.py:357
  52.7 4.6 %collective-permute-start.23 = (bf16[4,48,256]{2,1,0:T(8,128)(2,1)S(1)}, bf16[4,48,256]{2,1,0:T(8,128)(2,1)S(1)}, u32[]{:S(2)}, u32[]{:S(2)}) collective-permute-start(bf16[4,48,256]{2,1,0:T(8,128)(2,1)S(1)} %get-tuple-element.52.refs_0_), channel_id=1, source_target_pairs={{0,8},{4,12},{8,0},{12,4},{16,24},{20,28},{24,16},{28,20},{1,9},{5... | collective-permute-start | bytes 294920 | tf_op jit(solution)/shard_map/ppermute | solution.py:357
  54.0 4.6 %collective-permute-start.10 = (bf16[192,256]{1,0:T(8,128)(2,1)S(1)}, bf16[192,256]{1,0:T(8,128)(2,1)S(1)}, u32[]{:S(2)}, u32[]{:S(2)}) collective-permute-start(bf16[192,256]{1,0:T(8,128)(2,1)S(1)} %shard_map.98.refs_0_), channel_id=1, source_target_pairs={{0,1},{1,0},{2,3},{3,2},{4,5},{5,4},{6,7},{7,6},{8,9},{9,8},{10,11... | collective-permute-start | bytes 294920 | tf_op jit(solution)/shard_map/ppermute | solution.py:374
  55.5 4.0 %collective-permute-start.26 = (bf16[4,48,256]{2,1,0:T(8,128)(2,1)S(1)}, bf16[4,48,256]{2,1,0:T(8,128)(2,1)S(1)}, u32[]{:S(2)}, u32[]{:S(2)}) collective-permute-start(bf16[4,48,256]{2,1,0:T(8,128)(2,1)S(1)} %get-tuple-element.52.refs_0_), channel_id=1, source_target_pairs={{0,4},{4,0},{8,12},{12,8},{16,20},{20,16},{24,28},{28,24},{1,5},{5... | collective-permute-start | bytes 294920 | tf_op jit(solution)/shard_map/ppermute | solution.py:360
  56.0 3.5 %collective-permute-start.29 = (bf16[4,48,256]{2,1,0:T(8,128)(2,1)S(1)}, bf16[4,48,256]{2,1,0:T(8,128)(2,1)S(1)}, u32[]{:S(2)}, u32[]{:S(2)}) collective-permute-start(bf16[4,48,256]{2,1,0:T(8,128)(2,1)S(1)} %collective-permute-done.25.refs_3_), channel_id=1, source_target_pairs={{0,4},{4,0},{8,12},{12,8},{16,20},{20,16},{24,28},{28,24},{1,5},{5... | collective-permute-start | bytes 294920 | tf_op jit(solution)/shard_map/ppermute | solution.py:360
  57.0 2.5 %collective-permute-start.28 = (bf16[4,48,256]{2,1,0:T(8,128)(2,1)S(1)}, bf16[4,48,256]{2,1,0:T(8,128)(2,1)S(1)}, u32[]{:S(2)}, u32[]{:S(2)}) collective-permute-start(bf16[4,48,256]{2,1,0:T(8,128)(2,1)S(1)} %collective-permute-done.24.refs_2_), channel_id=1, source_target_pairs={{0,4},{4,0},{8,12},{12,8},{16,20},{20,16},{24,28},{28,24},{1,5},{5... | collective-permute-start | bytes 294920 | tf_op jit(solution)/shard_map/ppermute | solution.py:360
  57.3 2.2 %collective-permute-start.27 = (bf16[4,48,256]{2,1,0:T(8,128)(2,1)S(1)}, bf16[4,48,256]{2,1,0:T(8,128)(2,1)S(1)}, u32[]{:S(2)}, u32[]{:S(2)}) collective-permute-start(bf16[4,48,256]{2,1,0:T(8,128)(2,1)S(1)} %collective-permute-done.23.refs_1_), channel_id=1, source_target_pairs={{0,4},{4,0},{8,12},{12,8},{16,20},{20,16},{24,28},{28,24},{1,5},{5... | collective-permute-start | bytes 294920 | tf_op jit(solution)/shard_map/ppermute | solution.py:360

commit v2 on v1

--- a/solution.py
+++ b/solution.py
@@ -11,6 +11,7 @@
 BITS = 16
 BIAS_ROWS = 16
 LOADED = range(6)
+FIRST_SHARE = 5
 F32 = jnp.float32
 BF16 = jnp.bfloat16
 NT = (((1,), (1,)), ((), ()))
@@ -59,8 +60,9 @@
 
 def upper_kernel(factor, core_of, *refs):
     count = len(LOADED)
-    sources, own_ref, send_ref = refs[:count], refs[count], refs[count + 1]
-    targets, (sums, sems) = refs[count + 2 : 2 * count + 2], refs[2 * count + 2 :]
+    sources, (hidden_ref, own_ref, send_ref) = refs[:count], refs[count : count + 3]
+    targets, (sums, sems) = refs[count + 5 : -2] + refs[count + 3 : count + 5], refs[-2:]
+    weight_ref = targets[3]
     grad_ref, words_ref, pre_ref = targets[:3]
     copies = [
         pltpu.make_async_copy(source, target, sems.at[n])
@@ -68,27 +70,32 @@
     ]
     for copy in copies:
         copy.start()
-    for copy in copies[:3]:
+    for copy in copies[:4]:
         copy.wait()
     relations = words_ref.shape[0]
     seeds, width = grad_ref.shape
     scaled = grad_ref[...].astype(F32) * factor
     low = scaled.astype(BF16)
     low_bits = dot(reorder(seeds), low).astype(BF16)
-    hidden = jnp.maximum(pre_ref[...].astype(F32), 0.0).astype(BF16)
+    pre = pre_ref[...].astype(F32)
+    hidden = jnp.maximum(pre, 0.0).astype(BF16)
     parts = sums.shape[0]
     rows = sums.shape[1]
     height = hidden.shape[1]
     per = rows // height
-    for r in range(relations + 1):
-        if r == 0:
-            value = dot(hidden[:seeds], low, TN)
-        else:
-            matrix = bits_two(words_ref[r - 1])
-            inverse = 1.0 / jnp.maximum(jnp.sum(matrix, axis=1, keepdims=True), 1.0)
-            mixed = (dot(matrix.astype(BF16), hidden) * inverse).astype(BF16)
-            value = dot(mixed, low_bits, TN)
-        sums[r // per, (r % per) * height : (r % per + 1) * height] = value
+    own = dot(low, weight_ref[0], NT)
+    total = jnp.concatenate([own, jnp.zeros((pre.shape[0] - seeds, own.shape[1]), F32)], 0)
+    sums[0, :height] = dot(hidden[:seeds], low, TN)
+    for r in range(1, relations + 1):
+        spread = bits_two(words_ref[r - 1])
+        inverse = 1.0 / jnp.maximum(jnp.sum(spread, axis=1, keepdims=True), 1.0)
+        matrix = spread.astype(BF16)
+        back = (dot(low_bits, weight_ref[r], NT) * inverse).astype(BF16)
+        total = total + dot(matrix, back, TN)
+        mixed = (dot(matrix, hidden) * inverse).astype(BF16)
+        sums[r // per, (r % per) * height : (r % per + 1) * height] = dot(mixed, low_bits, TN)
+    hidden_grad = jnp.where(pre > 0, total, 0.0).astype(BF16)
+    hidden_ref[...] = dot(reorder(total.shape[0]), hidden_grad).astype(BF16)
     core = core_of()
     own_ref[:rows] = sums[core]
     other = 0 if parts == 1 else 1 - core
@@ -96,28 +103,8 @@
     bias = jnp.sum(scaled, 0, keepdims=True)
     own_ref[rows:] = jnp.broadcast_to(bias, (BIAS_ROWS, width))
     send_ref[rows:] = jnp.broadcast_to(bias, (BIAS_ROWS, width))
-    for copy in copies[3:]:
+    for copy in copies[4:]:
         copy.wait()
-
-
-def hidden_kernel(factor, pre_ref, words_ref, weight_ref, grad_ref, hidden_ref):
-    relations = words_ref.shape[0]
-    seeds = grad_ref.shape[0]
-    pre = pre_ref[...]
-    low = (grad_ref[...].astype(F32) * factor).astype(BF16)
-    low_bits = dot(reorder(seeds), low).astype(BF16)
-    total = None
-    for r in range(relations):
-        matrix = bits_two(words_ref[r])
-        inverse = 1.0 / jnp.maximum(jnp.sum(matrix, axis=1, keepdims=True), 1.0)
-        back = (dot(low_bits, weight_ref[r + 1], NT) * inverse).astype(BF16)
-        part = dot(matrix.astype(BF16), back, TN)
-        total = part if total is None else total + part
-    own = dot(low, weight_ref[0], NT)
-    rest = total.shape[0] - seeds
-    total = total + jnp.concatenate([own, jnp.zeros((rest, own.shape[1]), F32)], 0)
-    hidden_grad = jnp.where(pre.astype(F32) > 0, total, 0.0).astype(BF16)
-    hidden_ref[...] = dot(reorder(total.shape[0]), hidden_grad).astype(BF16)
 
 
 def pair_kernel(taker, own_ref, got_ref, *refs):
@@ -182,7 +169,7 @@
             scale = power / jnp.maximum(total, 1.0)
             out_ref[(r + 1) * width : (r + 2) * width, place] = (value[:width] * scale).astype(BF16)
 
-    if count <= 4:
+    if count <= 8:
         for b in range(count):
             batch(b)
     else:
@@ -197,10 +184,12 @@
     for block, place in zip(blocks, order):
         start = pl.multiple_of(place() * height, height)
         stack[pl.ds(start, height)] = block[...]
-    deep = gathered[0].shape[1]
-    total = dot(gathered[0][...], stack[:deep])
-    for n in range(1, parts):
-        total = total + dot(gathered[n][...], stack[n * deep : (n + 1) * deep])
+    total, place = None, 0
+    for part in gathered:
+        deep = part.shape[1]
+        value = dot(part[...], stack[place : place + deep])
+        total = value if total is None else total + value
+        place += deep
     sums[...] = total.reshape(sums.shape)
     reps = sums.shape[0]
     own_ref[...] = sums[taker(0)]
@@ -323,28 +312,28 @@
     loaded = (grad, words_two, pre, weight_two, words_one, columns)
     upper_rows = sets * hidden_width
     half = upper_rows // cores if direct else upper_rows
-    own_half, send_half, grad, words_two, pre, weight_two, words_one, columns = call(
+    kept = (words_one, columns)
+    hidden, own_half, send_half, words_one, columns = call(
         functools.partial(upper_kernel, factor, core_of if direct else lambda: 0),
-        (shape(half + BIAS_ROWS, hidden_width, F32),) * 2
-        + tuple(jax.ShapeDtypeStruct(v.shape, v.dtype) for v in loaded),
-        [
+        (shape(hidden_rows, hidden_width, BF16),)
+        + (shape(half + BIAS_ROWS, hidden_width, F32),) * 2
+        + tuple(jax.ShapeDtypeStruct(v.shape, v.dtype) for v in kept),
+        [pltpu.VMEM(v.shape, v.dtype) for v in loaded[:4]]
+        + [
             pltpu.VMEM((upper_rows // half, half, hidden_width), F32),
             pltpu.SemaphoreType.DMA((len(loaded),)),
         ],
         vmem=8 + sum(v.size * v.dtype.itemsize for v in loaded) // 2**20,
         in_specs=[pl.BlockSpec(memory_space=pltpu.HBM)] * len(loaded),
     )(*map(in_hbm, loaded))
-    hidden = call(
-        functools.partial(hidden_kernel, factor), shape(hidden_rows, hidden_width, BF16)
-    )(pre, words_two, weight_two, grad)
-
-    parts = 2 if batches % 2 == 0 else 1
-    run = batches // parts
+
+    first = batches * FIRST_SHARE // 8
+    runs = [(0, first), (first, batches - first)]
     gathered = []
-    for n in range(parts):
+    for start, run in runs:
         gathered.append(
             call(
-                functools.partial(gather_kernel, n * run, run),
+                functools.partial(gather_kernel, start, run),
                 shape(sets * width, run * rows_one, BF16),
                 (pltpu.VMEM((width + 16, nodes), BF16),),
                 flops=3000000000,
@@ -411,7 +400,7 @@
 
     stack_bytes = batches * rows_one * (hidden_width + sets * width) * 2
     panels = call(
-        functools.partial(panel_kernel, taker, order, parts),
+        functools.partial(panel_kernel, taker, order, len(runs)),
         (shape(share, hidden_width, F32),) + (shape(share, hidden_width, BF16),) * (reps - 1),
         (
             pltpu.VMEM((batches * rows_one, hidden_width), BF16),

time: 60.9 us -> 63 us (1.034)
  waiting for transfers between devices: 13.2 us -> 14.5 us
  starting transfers between devices: 35.5 us -> 36.6 us
    ppermute x12, waiting for transfers between devices: 3.52 us -> 4.66 us  [to_rep(): return lax.ppermute(value, 'rep', pairs)]
    pallas_call x4 -> x3, Pallas kernels: 6.45 us -> 5.35 us  [the longest x2 4.24 us: on_device(): call(functools.partial(gather_kernel, start, run), shape(sets * width, ru...]
    pallas_call x1, Pallas kernels: 2.21 us -> 3.01 us  [on_device(): call(functools.partial(upper_kernel, factor, core_of if direct else lambd...]
  transfers between devices with their start and end apart: 30 -> 30, of which waited for: 12 -> 9; matrix products, arithmetic and copies ran while one was open for 0% -> 0% of each run, Pallas kernels for 13% -> 11%
where the time goes in v2:
time: 63 us; the launch traced here: 62.9 us
  starting transfers between devices  36.6 us (58%)
  waiting for transfers between devices  14.5 us (23%)
  Pallas kernels  11 us (17%)
  between operations  0.77 us (1%)
    ppermute x12, starting transfers between devices, to_rep(): return lax.ppermute(value, 'rep', pairs)  23.1 us
    ppermute x9, starting transfers between devices, to_chip(): return lax.ppermute(value, 'feat', pairs)  11.9 us
    ppermute x9, waiting for transfers between devices, to_chip(): return lax.ppermute(value, 'feat', pairs)  9.79 us
    ppermute x12, waiting for transfers between devices, to_rep(): return lax.ppermute(value, 'rep', pairs)  4.66 us
    pallas_call x2, Pallas kernels, on_device(): call(functools.partial(gather_kernel, start, run), shape(sets * width, ru...  4.24 us
    pallas_call x1, Pallas kernels, on_device(): call(functools.partial(upper_kernel, factor, core_of if direct else lambd...  3.01 us
    ppermute x9, starting transfers between devices, to_core(): return lax.ppermute(value, 'feat', [(i, i ^ 1) for i in range(feat)])  1.6 us
  transfers between devices with their start and end apart: 30, of which 9 were waited for; matrix products, arithmetic and copies ran while one was open for 0% of the time, Pallas kernels for 11%

profile of v2, /device:TPU:0, one launch (start us, length us, event | category | flops | bytes accessed | tf_op | source)
XLA Modules:
  0.0 62.9 jit_solution(17422423188141160406)
XLA Ops:
  0.6 3.0 %shard_map.93 = (bf16[256,256]{1,0:T(8,128)(2,1)S(1)}, f32[784,256]{1,0:T(8,128)S(1)}, f32[784,256]{1,0:T(8,128)S(1)}, s32[8,5,16,512]{3,2,1,0:T(8,128)S(1)}, bf16[8,128,512]{2,1,0:T(8,128)(2,1)S(1)}) custom-call(bf16[128,256]{1,0:T(8,128)(2,1)} %bitcast.11, s32[5,8,256]{2,1,0:T(8,128)} %bitcast.12, bf16[256,256]{1,0:T(8,128)(2,1)} %bitcast.10, ...), custom_call_target="tpu_custom_call" | custom-call | flops 1000000 | bytes 1000000 | tf_op jit(solution)/shard_map/pallas_call | solution.py:316
  4.2 2.5 %collective-permute-start = (bf16[256,256]{1,0:T(8,128)(2,1)S(1)}, bf16[256,256]{1,0:T(8,128)(2,1)S(1)}, u32[]{:S(2)}, u32[]{:S(2)}) collective-permute-start(bf16[256,256]{1,0:T(8,128)(2,1)S(1)} %get-tuple-element.30.refs_2_.refs_0_), channel_id=1, source_target_pairs={{0,8},{4,12},{8,0},{12,4},{16,24},{20,28},{24,16},{28,20},{1,9},{5... | collective-permute-start | bytes 393224 | tf_op jit(solution)/shard_map/ppermute | solution.py:346
  6.8 1.5 %collective-permute-start.1 = (bf16[256,256]{1,0:T(8,128)(2,1)S(1)}, bf16[256,256]{1,0:T(8,128)(2,1)S(1)}, u32[]{:S(2)}, u32[]{:S(2)}) collective-permute-start(bf16[256,256]{1,0:T(8,128)(2,1)S(1)} %get-tuple-element.30.refs_2_.refs_0_), channel_id=1, source_target_pairs={{0,16},{4,20},{8,24},{12,28},{16,0},{20,4},{24,8},{28,12},{1,17},{... | collective-permute-start | bytes 393224 | tf_op jit(solution)/shard_map/ppermute | solution.py:346
  8.3 2.7 %collective-permute-done.refs_3_.refs_1_ = bf16[256,256]{1,0:T(8,128)(2,1)S(1)} collective-permute-done((bf16[256,256]{1,0:T(8,128)(2,1)S(1)}, bf16[256,256]{1,0:T(8,128)(2,1)S(1)}, u32[]{:S(2)}, u32[]{:S(2)}) %collective-permute-start) | collective-permute-done | bytes 131104 | tf_op jit(solution)/shard_map/ppermute | solution.py:346
  11.0 2.6 %shard_map.94.refs_0_ = bf16[768,1280]{1,0:T(8,128)(2,1)S(1)} custom-call(bf16[8,128,512]{2,1,0:T(8,128)(2,1)S(1)} %get-tuple-element.28.column_ref, s32[8,5,16,512]{3,2,1,0:T(8,128)S(1)} %get-tuple-element.29.word_ref), custom_call_target="tpu_custom_call" | custom-call | flops 3000000000 | bytes 1000000 | tf_op jit(solution)/shard_map/pallas_call | solution.py:335
  13.6 1.5 %collective-permute-done.1.refs_4_.refs_2_ = bf16[256,256]{1,0:T(8,128)(2,1)S(1)} collective-permute-done((bf16[256,256]{1,0:T(8,128)(2,1)S(1)}, bf16[256,256]{1,0:T(8,128)(2,1)S(1)}, u32[]{:S(2)}, u32[]{:S(2)}) %collective-permute-start.1) | collective-permute-done | bytes 131104 | tf_op jit(solution)/shard_map/ppermute | solution.py:346
  15.8 1.6 %collective-permute-start.14 = (bf16[208,256]{1,0:T(8,128)(2,1)S(1)}, bf16[208,256]{1,0:T(8,128)(2,1)S(1)}, u32[]{:S(2)}, u32[]{:S(2)}) collective-permute-start(bf16[208,256]{1,0:T(8,128)(2,1)S(1)} %get-tuple-element.38), channel_id=1, source_target_pairs={{0,1},{1,0},{2,3},{3,2},{4,5},{5,4},{6,7},{7,6},{8,9},{9,8},{10,11... | collective-permute-start | bytes 319496 | tf_op jit(solution)/shard_map/ppermute | solution.py:363
  17.4 2.6 %collective-permute-start.15 = (bf16[208,256]{1,0:T(8,128)(2,1)S(1)}, bf16[208,256]{1,0:T(8,128)(2,1)S(1)}, u32[]{:S(2)}, u32[]{:S(2)}) collective-permute-start(bf16[208,256]{1,0:T(8,128)(2,1)S(1)} %get-tuple-element.39), channel_id=1, source_target_pairs={{0,2},{1,3},{2,0},{3,1},{4,6},{5,7},{6,4},{7,5},{8,10},{9,11},{10,... | collective-permute-start | bytes 319496 | tf_op jit(solution)/shard_map/ppermute | solution.py:363
  20.2 1.6 %shard_map.95.refs_1_ = bf16[768,768]{1,0:T(8,128)(2,1)S(1)} custom-call(bf16[8,128,512]{2,1,0:T(8,128)(2,1)S(1)} %get-tuple-element.28.column_ref, s32[8,5,16,512]{3,2,1,0:T(8,128)S(1)} %get-tuple-element.29.word_ref), custom_call_target="tpu_custom_call" | custom-call | flops 3000000000 | bytes 1000000 | tf_op jit(solution)/shard_map/pallas_call | solution.py:335
  21.9 1.1 %shard_map.96 = (f32[192,256]{1,0:T(8,128)S(1)}, bf16[192,256]{1,0:T(8,128)(2,1)S(1)}, bf16[192,256]{1,0:T(8,128)(2,1)S(1)}, bf16[192,256]{1,0:T(8,128)(2,1)S(1)}) custom-call(bf16[768,1280]{1,0:T(8,128)(2,1)S(1)} %shard_map.94.refs_0_, bf16[768,768]{1,0:T(8,128)(2,1)S(1)} %shard_map.95.refs_1_, bf16[256,256]{1,0:T(8,128)(2,1)S(1)} %get-tuple-element.30.refs_2_.refs_0_, ...), custom_call_target="tpu_custom_call" | custom-call | flops 1000000 | bytes 1000000 | tf_op jit(solution)/shard_map/pallas_call | solution.py:402
  23.0 0.7 %collective-permute-start.7 = (bf16[192,256]{1,0:T(8,128)(2,1)S(1)}, bf16[192,256]{1,0:T(8,128)(2,1)S(1)}, u32[]{:S(2)}, u32[]{:S(2)}) collective-permute-start(bf16[192,256]{1,0:T(8,128)(2,1)S(1)} %get-tuple-element.32), channel_id=1, source_target_pairs={{0,1},{1,0},{2,3},{3,2},{4,5},{5,4},{6,7},{7,6},{8,9},{9,8},{10,11... | collective-permute-start | bytes 294920 | tf_op jit(solution)/shard_map/ppermute | solution.py:363
  23.8 3.5 %collective-permute-start.8 = (bf16[192,256]{1,0:T(8,128)(2,1)S(1)}, bf16[192,256]{1,0:T(8,128)(2,1)S(1)}, u32[]{:S(2)}, u32[]{:S(2)}) collective-permute-start(bf16[192,256]{1,0:T(8,128)(2,1)S(1)} %get-tuple-element.33), channel_id=1, source_target_pairs={{0,2},{1,3},{2,0},{3,1},{4,6},{5,7},{6,4},{7,5},{8,10},{9,11},{10,... | collective-permute-start | bytes 294920 | tf_op jit(solution)/shard_map/ppermute | solution.py:363
  27.3 1.4 %collective-permute-done.15.refs_1_ = bf16[208,256]{1,0:T(8,128)(2,1)S(1)} collective-permute-done((bf16[208,256]{1,0:T(8,128)(2,1)S(1)}, bf16[208,256]{1,0:T(8,128)(2,1)S(1)}, u32[]{:S(2)}, u32[]{:S(2)}) %collective-permute-start.15) | collective-permute-done | bytes 106528 | tf_op jit(solution)/shard_map/ppermute | solution.py:363
  28.8 0.9 %collective-permute-start.17 = (bf16[64,256]{1,0:T(8,128)(2,1)S(1)}, bf16[64,256]{1,0:T(8,128)(2,1)S(1)}, u32[]{:S(2)}, u32[]{:S(2)}) collective-permute-start(bf16[64,256]{1,0:T(8,128)(2,1)S(1)} %get-tuple-element.42), channel_id=1, source_target_pairs={{0,8},{4,12},{8,0},{12,4},{16,24},{20,28},{24,16},{28,20},{1,9},{5... | collective-permute-start | bytes 98312 | tf_op jit(solution)/shard_map/ppermute | solution.py:346
  29.7 2.7 %collective-permute-start.9 = (bf16[192,256]{1,0:T(8,128)(2,1)S(1)}, bf16[192,256]{1,0:T(8,128)(2,1)S(1)}, u32[]{:S(2)}, u32[]{:S(2)}) collective-permute-start(bf16[192,256]{1,0:T(8,128)(2,1)S(1)} %get-tuple-element.34), channel_id=1, source_target_pairs={{0,3},{1,2},{2,1},{3,0},{4,7},{5,6},{6,5},{7,4},{8,11},{9,10},{10,... | collective-permute-start | bytes 294920 | tf_op jit(solution)/shard_map/ppermute | solution.py:363
  32.4 1.5 %collective-permute-start.18 = (bf16[64,256]{1,0:T(8,128)(2,1)S(1)}, bf16[64,256]{1,0:T(8,128)(2,1)S(1)}, u32[]{:S(2)}, u32[]{:S(2)}) collective-permute-start(bf16[64,256]{1,0:T(8,128)(2,1)S(1)} %get-tuple-element.43), channel_id=1, source_target_pairs={{0,16},{4,20},{8,24},{12,28},{16,0},{20,4},{24,8},{28,12},{1,17},{... | collective-permute-start | bytes 98312 | tf_op jit(solution)/shard_map/ppermute | solution.py:346
  34.0 1.8 %collective-permute-start.19 = (bf16[64,256]{1,0:T(8,128)(2,1)S(1)}, bf16[64,256]{1,0:T(8,128)(2,1)S(1)}, u32[]{:S(2)}, u32[]{:S(2)}) collective-permute-start(bf16[64,256]{1,0:T(8,128)(2,1)S(1)} %get-tuple-element.44), channel_id=1, source_target_pairs={{0,24},{4,28},{8,16},{12,20},{16,8},{20,12},{24,0},{28,4},{1,25},{... | collective-permute-start | bytes 98312 | tf_op jit(solution)/shard_map/ppermute | solution.py:346
  36.3 2.4 %collective-permute-done.19.refs_10_ = bf16[64,256]{1,0:T(8,128)(2,1)S(1)} collective-permute-done((bf16[64,256]{1,0:T(8,128)(2,1)S(1)}, bf16[64,256]{1,0:T(8,128)(2,1)S(1)}, u32[]{:S(2)}, u32[]{:S(2)}) %collective-permute-start.19) | collective-permute-done | bytes 32800 | tf_op jit(solution)/shard_map/ppermute | solution.py:346
  39.0 4.9 %collective-permute-start.20 = (bf16[64,256]{1,0:T(8,128)(2,1)S(1)}, bf16[64,256]{1,0:T(8,128)(2,1)S(1)}, u32[]{:S(2)}, u32[]{:S(2)}) collective-permute-start(bf16[64,256]{1,0:T(8,128)(2,1)S(1)} %get-tuple-element.45.refs_0_), channel_id=1, source_target_pairs={{0,1},{1,0},{2,3},{3,2},{4,5},{5,4},{6,7},{7,6},{8,9},{9,8},{10,11... | collective-permute-start | bytes 98312 | tf_op jit(solution)/shard_map/ppermute | solution.py:363
  43.9 0.9 %collective-permute-start.21 = (bf16[64,256]{1,0:T(8,128)(2,1)S(1)}, bf16[64,256]{1,0:T(8,128)(2,1)S(1)}, u32[]{:S(2)}, u32[]{:S(2)}) collective-permute-start(bf16[64,256]{1,0:T(8,128)(2,1)S(1)} %get-tuple-element.45.refs_0_), channel_id=1, source_target_pairs={{0,2},{1,3},{2,0},{3,1},{4,6},{5,7},{6,4},{7,5},{8,10},{9,11},{10,... | collective-permute-start | bytes 98312 | tf_op jit(solution)/shard_map/ppermute | solution.py:363
  44.8 1.5 %collective-permute-start.22 = (bf16[64,256]{1,0:T(8,128)(2,1)S(1)}, bf16[64,256]{1,0:T(8,128)(2,1)S(1)}, u32[]{:S(2)}, u32[]{:S(2)}) collective-permute-start(bf16[64,256]{1,0:T(8,128)(2,1)S(1)} %get-tuple-element.45.refs_0_), channel_id=1, source_target_pairs={{0,3},{1,2},{2,1},{3,0},{4,7},{5,6},{6,5},{7,4},{8,11},{9,10},{10,... | collective-permute-start | bytes 98312 | tf_op jit(solution)/shard_map/ppermute | solution.py:363
  46.4 1.1 %collective-permute-start.10 = (bf16[192,256]{1,0:T(8,128)(2,1)S(1)}, bf16[192,256]{1,0:T(8,128)(2,1)S(1)}, u32[]{:S(2)}, u32[]{:S(2)}) collective-permute-start(bf16[192,256]{1,0:T(8,128)(2,1)S(1)} %shard_map.97.refs_0_), channel_id=1, source_target_pairs={{0,1},{1,0},{2,3},{3,2},{4,5},{5,4},{6,7},{7,6},{8,9},{9,8},{10,11... | collective-permute-start | bytes 294920 | tf_op jit(solution)/shard_map/ppermute | solution.py:363
  47.5 1.8 %collective-permute-start.11 = (bf16[192,256]{1,0:T(8,128)(2,1)S(1)}, bf16[192,256]{1,0:T(8,128)(2,1)S(1)}, u32[]{:S(2)}, u32[]{:S(2)}) collective-permute-start(bf16[192,256]{1,0:T(8,128)(2,1)S(1)} %shard_map.97.refs_0_), channel_id=1, source_target_pairs={{0,2},{1,3},{2,0},{3,1},{4,6},{5,7},{6,4},{7,5},{8,10},{9,11},{10,... | collective-permute-start | bytes 294920 | tf_op jit(solution)/shard_map/ppermute | solution.py:363
  49.4 1.3 %collective-permute-done.22.refs_3_ = bf16[64,256]{1,0:T(8,128)(2,1)S(1)} collective-permute-done((bf16[64,256]{1,0:T(8,128)(2,1)S(1)}, bf16[64,256]{1,0:T(8,128)(2,1)S(1)}, u32[]{:S(2)}, u32[]{:S(2)}) %collective-permute-start.22) | collective-permute-done | bytes 32800 | tf_op jit(solution)/shard_map/ppermute | solution.py:363
  50.7 1.1 %collective-permute-start.23 = (bf16[4,48,256]{2,1,0:T(8,128)(2,1)S(1)}, bf16[4,48,256]{2,1,0:T(8,128)(2,1)S(1)}, u32[]{:S(2)}, u32[]{:S(2)}) collective-permute-start(bf16[4,48,256]{2,1,0:T(8,128)(2,1)S(1)} %get-tuple-element.46.refs_0_), channel_id=1, source_target_pairs={{0,8},{4,12},{8,0},{12,4},{16,24},{20,28},{24,16},{28,20},{1,9},{5... | collective-permute-start | bytes 294920 | tf_op jit(solution)/shard_map/ppermute | solution.py:346
  51.8 1.4 %collective-permute-start.24 = (bf16[4,48,256]{2,1,0:T(8,128)(2,1)S(1)}, bf16[4,48,256]{2,1,0:T(8,128)(2,1)S(1)}, u32[]{:S(2)}, u32[]{:S(2)}) collective-permute-start(bf16[4,48,256]{2,1,0:T(8,128)(2,1)S(1)} %get-tuple-element.46.refs_0_), channel_id=1, source_target_pairs={{0,16},{4,20},{8,24},{12,28},{16,0},{20,4},{24,8},{28,12},{1,17},{... | collective-permute-start | bytes 294920 | tf_op jit(solution)/shard_map/ppermute | solution.py:346
  53.2 1.0 %collective-permute-start.25 = (bf16[4,48,256]{2,1,0:T(8,128)(2,1)S(1)}, bf16[4,48,256]{2,1,0:T(8,128)(2,1)S(1)}, u32[]{:S(2)}, u32[]{:S(2)}) collective-permute-start(bf16[4,48,256]{2,1,0:T(8,128)(2,1)S(1)} %get-tuple-element.46.refs_0_), channel_id=1, source_target_pairs={{0,24},{4,28},{8,16},{12,20},{16,8},{20,12},{24,0},{28,4},{1,25},{... | collective-permute-start | bytes 294920 | tf_op jit(solution)/shard_map/ppermute | solution.py:346
  54.2 1.4 %collective-permute-start.12 = (bf16[192,256]{1,0:T(8,128)(2,1)S(1)}, bf16[192,256]{1,0:T(8,128)(2,1)S(1)}, u32[]{:S(2)}, u32[]{:S(2)}) collective-permute-start(bf16[192,256]{1,0:T(8,128)(2,1)S(1)} %shard_map.97.refs_0_), channel_id=1, source_target_pairs={{0,3},{1,2},{2,1},{3,0},{4,7},{5,6},{6,5},{7,4},{8,11},{9,10},{10,... | collective-permute-start | bytes 294920 | tf_op jit(solution)/shard_map/ppermute | solution.py:363
  56.4 2.3 %collective-permute-done.25.refs_3_ = bf16[4,48,256]{2,1,0:T(8,128)(2,1)S(1)} collective-permute-done((bf16[4,48,256]{2,1,0:T(8,128)(2,1)S(1)}, bf16[4,48,256]{2,1,0:T(8,128)(2,1)S(1)}, u32[]{:S(2)}, u32[]{:S(2)}) %collective-permute-start.25) | collective-permute-done | bytes 98336 | tf_op jit(solution)/shard_map/ppermute | solution.py:346
  58.8 1.9 %collective-permute-done.12.refs_3_ = bf16[192,256]{1,0:T(8,128)(2,1)S(1)} collective-permute-done((bf16[192,256]{1,0:T(8,128)(2,1)S(1)}, bf16[192,256]{1,0:T(8,128)(2,1)S(1)}, u32[]{:S(2)}, u32[]{:S(2)}) %collective-permute-start.12) | collective-permute-done | bytes 98336 | tf_op jit(solution)/shard_map/ppermute | solution.py:363
  60.7 0.9 %shard_map.98 = f32[4,192,256]{2,1,0:T(8,128)} custom-call(bf16[192,256]{1,0:T(8,128)(2,1)S(1)} %shard_map.97.refs_0_, bf16[192,256]{1,0:T(8,128)(2,1)S(1)} %collective-permute-done.10.refs_1_, bf16[192,256]{1,0:T(8,128)(2,1)S(1)} %collective-permute-done.11.refs_2_, bf16[192,256]{1,0:T(8,128)(2,1)S(1)} %collective-permute-done.12.refs_3_), custom_call_target="tpu_custom_call" | custom-call | flops 1000000 | bytes 1000000 | tf_op jit(solution)/shard_map/pallas_call | solution.py:434
  61.6 1.2 %shard_map.103 = (f32[2,4,4,48,256]{4,3,2,1,0:T(8,128)}, f32[256]{0:T(256)}, f32[256]{0:T(256)}) custom-call(bf16[4,48,256]{2,1,0:T(8,128)(2,1)S(1)} %get-tuple-element.46.refs_0_, bf16[4,48,256]{2,1,0:T(8,128)(2,1)S(1)} %collective-permute-done.23.refs_1_, bf16[4,48,256]{2,1,0:T(8,128)(2,1)S(1)} %collective-permute-done.24.refs_2_, ...), custom_call_target="tpu_custom_call" | custom-call | flops 1000000 | bytes 1000000 | tf_op jit(solution)/shard_map/pallas_call | solution.py:456
  (39 shorter events, 3.2 us)
Async XLA Ops:
  3.7 12.0 %collective-permute-start.13 = (f32[784,256]{1,0:T(8,128)S(1)}, f32[784,256]{1,0:T(8,128)S(1)}, u32[]{:S(2)}, u32[]{:S(2)}) collective-permute-start(f32[784,256]{1,0:T(8,128)S(1)} %get-tuple-element.36), channel_id=1, source_target_pairs={{0,4},{4,0},{8,12},{12,8},{16,20},{20,16},{24,28},{28,24},{1,5},{5... | collective-permute-start | bytes 2408456 | tf_op jit(solution)/shard_map/ppermute | solution.py:349
  4.2 6.8 %collective-permute-start = (bf16[256,256]{1,0:T(8,128)(2,1)S(1)}, bf16[256,256]{1,0:T(8,128)(2,1)S(1)}, u32[]{:S(2)}, u32[]{:S(2)}) collective-permute-start(bf16[256,256]{1,0:T(8,128)(2,1)S(1)} %get-tuple-element.30.refs_2_.refs_0_), channel_id=1, source_target_pairs={{0,8},{4,12},{8,0},{12,4},{16,24},{20,28},{24,16},{28,20},{1,9},{5... | collective-permute-start | bytes 393224 | tf_op jit(solution)/shard_map/ppermute | solution.py:346
  6.8 8.4 %collective-permute-start.1 = (bf16[256,256]{1,0:T(8,128)(2,1)S(1)}, bf16[256,256]{1,0:T(8,128)(2,1)S(1)}, u32[]{:S(2)}, u32[]{:S(2)}) collective-permute-start(bf16[256,256]{1,0:T(8,128)(2,1)S(1)} %get-tuple-element.30.refs_2_.refs_0_), channel_id=1, source_target_pairs={{0,16},{4,20},{8,24},{12,28},{16,0},{20,4},{24,8},{28,12},{1,17},{... | collective-permute-start | bytes 393224 | tf_op jit(solution)/shard_map/ppermute | solution.py:346
  8.3 6.8 %collective-permute-start.2 = (bf16[256,256]{1,0:T(8,128)(2,1)S(1)}, bf16[256,256]{1,0:T(8,128)(2,1)S(1)}, u32[]{:S(2)}, u32[]{:S(2)}) collective-permute-start(bf16[256,256]{1,0:T(8,128)(2,1)S(1)} %get-tuple-element.30.refs_2_.refs_0_), channel_id=1, source_target_pairs={{0,24},{4,28},{8,16},{12,20},{16,8},{20,12},{24,0},{28,4},{1,25},{... | collective-permute-start | bytes 393224 | tf_op jit(solution)/shard_map/ppermute | solution.py:346
  8.3 9.1 %collective-permute-start.3 = (bf16[256,256]{1,0:T(8,128)(2,1)S(1)}, bf16[256,256]{1,0:T(8,128)(2,1)S(1)}, u32[]{:S(2)}, u32[]{:S(2)}) collective-permute-start(bf16[256,256]{1,0:T(8,128)(2,1)S(1)} %get-tuple-element.30.refs_2_.refs_0_), channel_id=1, source_target_pairs={{0,4},{4,0},{8,12},{12,8},{16,20},{20,16},{24,28},{28,24},{1,5},{5... | collective-permute-start | bytes 393224 | tf_op jit(solution)/shard_map/ppermute | solution.py:349
  11.0 9.0 %collective-permute-start.4 = (bf16[256,256]{1,0:T(8,128)(2,1)S(1)}, bf16[256,256]{1,0:T(8,128)(2,1)S(1)}, u32[]{:S(2)}, u32[]{:S(2)}) collective-permute-start(bf16[256,256]{1,0:T(8,128)(2,1)S(1)} %collective-permute-done.refs_3_.refs_1_), channel_id=1, source_target_pairs={{0,4},{4,0},{8,12},{12,8},{16,20},{20,16},{24,28},{28,24},{1,5},{5... | collective-permute-start | bytes 393224 | tf_op jit(solution)/shard_map/ppermute | solution.py:349
  15.1 6.8 %collective-permute-start.5 = (bf16[256,256]{1,0:T(8,128)(2,1)S(1)}, bf16[256,256]{1,0:T(8,128)(2,1)S(1)}, u32[]{:S(2)}, u32[]{:S(2)}) collective-permute-start(bf16[256,256]{1,0:T(8,128)(2,1)S(1)} %collective-permute-done.1.refs_4_.refs_2_), channel_id=1, source_target_pairs={{0,4},{4,0},{8,12},{12,8},{16,20},{20,16},{24,28},{28,24},{1,5},{5... | collective-permute-start | bytes 393224 | tf_op jit(solution)/shard_map/ppermute | solution.py:349
  15.1 6.8 %collective-permute-start.6 = (bf16[256,256]{1,0:T(8,128)(2,1)S(1)}, bf16[256,256]{1,0:T(8,128)(2,1)S(1)}, u32[]{:S(2)}, u32[]{:S(2)}) collective-permute-start(bf16[256,256]{1,0:T(8,128)(2,1)S(1)} %collective-permute-done.2.refs_5_.refs_3_), channel_id=1, source_target_pairs={{0,4},{4,0},{8,12},{12,8},{16,20},{20,16},{24,28},{28,24},{1,5},{5... | collective-permute-start | bytes 393224 | tf_op jit(solution)/shard_map/ppermute | solution.py:349
  15.8 11.5 %collective-permute-start.14 = (bf16[208,256]{1,0:T(8,128)(2,1)S(1)}, bf16[208,256]{1,0:T(8,128)(2,1)S(1)}, u32[]{:S(2)}, u32[]{:S(2)}) collective-permute-start(bf16[208,256]{1,0:T(8,128)(2,1)S(1)} %get-tuple-element.38), channel_id=1, source_target_pairs={{0,1},{1,0},{2,3},{3,2},{4,5},{5,4},{6,7},{7,6},{8,9},{9,8},{10,11... | collective-permute-start | bytes 319496 | tf_op jit(solution)/shard_map/ppermute | solution.py:363
  17.4 11.3 %collective-permute-start.15 = (bf16[208,256]{1,0:T(8,128)(2,1)S(1)}, bf16[208,256]{1,0:T(8,128)(2,1)S(1)}, u32[]{:S(2)}, u32[]{:S(2)}) collective-permute-start(bf16[208,256]{1,0:T(8,128)(2,1)S(1)} %get-tuple-element.39), channel_id=1, source_target_pairs={{0,2},{1,3},{2,0},{3,1},{4,6},{5,7},{6,4},{7,5},{8,10},{9,11},{10,... | collective-permute-start | bytes 319496 | tf_op jit(solution)/shard_map/ppermute | solution.py:363
  20.0 8.7 %collective-permute-start.16 = (bf16[208,256]{1,0:T(8,128)(2,1)S(1)}, bf16[208,256]{1,0:T(8,128)(2,1)S(1)}, u32[]{:S(2)}, u32[]{:S(2)}) collective-permute-start(bf16[208,256]{1,0:T(8,128)(2,1)S(1)} %get-tuple-element.40), channel_id=1, source_target_pairs={{0,3},{1,2},{2,1},{3,0},{4,7},{5,6},{6,5},{7,4},{8,11},{9,10},{10,... | collective-permute-start | bytes 319496 | tf_op jit(solution)/shard_map/ppermute | solution.py:363
  23.0 21.8 %collective-permute-start.7 = (bf16[192,256]{1,0:T(8,128)(2,1)S(1)}, bf16[192,256]{1,0:T(8,128)(2,1)S(1)}, u32[]{:S(2)}, u32[]{:S(2)}) collective-permute-start(bf16[192,256]{1,0:T(8,128)(2,1)S(1)} %get-tuple-element.32), channel_id=1, source_target_pairs={{0,1},{1,0},{2,3},{3,2},{4,5},{5,4},{6,7},{7,6},{8,9},{9,8},{10,11... | collective-permute-start | bytes 294920 | tf_op jit(solution)/shard_map/ppermute | solution.py:363
  23.8 22.6 %collective-permute-start.8 = (bf16[192,256]{1,0:T(8,128)(2,1)S(1)}, bf16[192,256]{1,0:T(8,128)(2,1)S(1)}, u32[]{:S(2)}, u32[]{:S(2)}) collective-permute-start(bf16[192,256]{1,0:T(8,128)(2,1)S(1)} %get-tuple-element.33), channel_id=1, source_target_pairs={{0,2},{1,3},{2,0},{3,1},{4,6},{5,7},{6,4},{7,5},{8,10},{9,11},{10,... | collective-permute-start | bytes 294920 | tf_op jit(solution)/shard_map/ppermute | solution.py:363
  28.8 5.2 %collective-permute-start.17 = (bf16[64,256]{1,0:T(8,128)(2,1)S(1)}, bf16[64,256]{1,0:T(8,128)(2,1)S(1)}, u32[]{:S(2)}, u32[]{:S(2)}) collective-permute-start(bf16[64,256]{1,0:T(8,128)(2,1)S(1)} %get-tuple-element.42), channel_id=1, source_target_pairs={{0,8},{4,12},{8,0},{12,4},{16,24},{20,28},{24,16},{28,20},{1,9},{5... | collective-permute-start | bytes 98312 | tf_op jit(solution)/shard_map/ppermute | solution.py:346
  29.7 16.6 %collective-permute-start.9 = (bf16[192,256]{1,0:T(8,128)(2,1)S(1)}, bf16[192,256]{1,0:T(8,128)(2,1)S(1)}, u32[]{:S(2)}, u32[]{:S(2)}) collective-permute-start(bf16[192,256]{1,0:T(8,128)(2,1)S(1)} %get-tuple-element.34), channel_id=1, source_target_pairs={{0,3},{1,2},{2,1},{3,0},{4,7},{5,6},{6,5},{7,4},{8,11},{9,10},{10,... | collective-permute-start | bytes 294920 | tf_op jit(solution)/shard_map/ppermute | solution.py:363
  32.4 3.9 %collective-permute-start.18 = (bf16[64,256]{1,0:T(8,128)(2,1)S(1)}, bf16[64,256]{1,0:T(8,128)(2,1)S(1)}, u32[]{:S(2)}, u32[]{:S(2)}) collective-permute-start(bf16[64,256]{1,0:T(8,128)(2,1)S(1)} %get-tuple-element.43), channel_id=1, source_target_pairs={{0,16},{4,20},{8,24},{12,28},{16,0},{20,4},{24,8},{28,12},{1,17},{... | collective-permute-start | bytes 98312 | tf_op jit(solution)/shard_map/ppermute | solution.py:346
  34.0 4.8 %collective-permute-start.19 = (bf16[64,256]{1,0:T(8,128)(2,1)S(1)}, bf16[64,256]{1,0:T(8,128)(2,1)S(1)}, u32[]{:S(2)}, u32[]{:S(2)}) collective-permute-start(bf16[64,256]{1,0:T(8,128)(2,1)S(1)} %get-tuple-element.44), channel_id=1, source_target_pairs={{0,24},{4,28},{8,16},{12,20},{16,8},{20,12},{24,0},{28,4},{1,25},{... | collective-permute-start | bytes 98312 | tf_op jit(solution)/shard_map/ppermute | solution.py:346
  39.0 10.4 %collective-permute-start.20 = (bf16[64,256]{1,0:T(8,128)(2,1)S(1)}, bf16[64,256]{1,0:T(8,128)(2,1)S(1)}, u32[]{:S(2)}, u32[]{:S(2)}) collective-permute-start(bf16[64,256]{1,0:T(8,128)(2,1)S(1)} %get-tuple-element.45.refs_0_), channel_id=1, source_target_pairs={{0,1},{1,0},{2,3},{3,2},{4,5},{5,4},{6,7},{7,6},{8,9},{9,8},{10,11... | collective-permute-start | bytes 98312 | tf_op jit(solution)/shard_map/ppermute | solution.py:363
  43.9 5.5 %collective-permute-start.21 = (bf16[64,256]{1,0:T(8,128)(2,1)S(1)}, bf16[64,256]{1,0:T(8,128)(2,1)S(1)}, u32[]{:S(2)}, u32[]{:S(2)}) collective-permute-start(bf16[64,256]{1,0:T(8,128)(2,1)S(1)} %get-tuple-element.45.refs_0_), channel_id=1, source_target_pairs={{0,2},{1,3},{2,0},{3,1},{4,6},{5,7},{6,4},{7,5},{8,10},{9,11},{10,... | collective-permute-start | bytes 98312 | tf_op jit(solution)/shard_map/ppermute | solution.py:363
  44.8 5.8 %collective-permute-start.22 = (bf16[64,256]{1,0:T(8,128)(2,1)S(1)}, bf16[64,256]{1,0:T(8,128)(2,1)S(1)}, u32[]{:S(2)}, u32[]{:S(2)}) collective-permute-start(bf16[64,256]{1,0:T(8,128)(2,1)S(1)} %get-tuple-element.45.refs_0_), channel_id=1, source_target_pairs={{0,3},{1,2},{2,1},{3,0},{4,7},{5,6},{6,5},{7,4},{8,11},{9,10},{10,... | collective-permute-start | bytes 98312 | tf_op jit(solution)/shard_map/ppermute | solution.py:363
  46.4 7.8 %collective-permute-start.10 = (bf16[192,256]{1,0:T(8,128)(2,1)S(1)}, bf16[192,256]{1,0:T(8,128)(2,1)S(1)}, u32[]{:S(2)}, u32[]{:S(2)}) collective-permute-start(bf16[192,256]{1,0:T(8,128)(2,1)S(1)} %shard_map.97.refs_0_), channel_id=1, source_target_pairs={{0,1},{1,0},{2,3},{3,2},{4,5},{5,4},{6,7},{7,6},{8,9},{9,8},{10,11... | collective-permute-start | bytes 294920 | tf_op jit(solution)/shard_map/ppermute | solution.py:363
  47.5 8.2 %collective-permute-start.11 = (bf16[192,256]{1,0:T(8,128)(2,1)S(1)}, bf16[192,256]{1,0:T(8,128)(2,1)S(1)}, u32[]{:S(2)}, u32[]{:S(2)}) collective-permute-start(bf16[192,256]{1,0:T(8,128)(2,1)S(1)} %shard_map.97.refs_0_), channel_id=1, source_target_pairs={{0,2},{1,3},{2,0},{3,1},{4,6},{5,7},{6,4},{7,5},{8,10},{9,11},{10,... | collective-permute-start | bytes 294920 | tf_op jit(solution)/shard_map/ppermute | solution.py:363
  50.7 5.0 %collective-permute-start.23 = (bf16[4,48,256]{2,1,0:T(8,128)(2,1)S(1)}, bf16[4,48,256]{2,1,0:T(8,128)(2,1)S(1)}, u32[]{:S(2)}, u32[]{:S(2)}) collective-permute-start(bf16[4,48,256]{2,1,0:T(8,128)(2,1)S(1)} %get-tuple-element.46.refs_0_), channel_id=1, source_target_pairs={{0,8},{4,12},{8,0},{12,4},{16,24},{20,28},{24,16},{28,20},{1,9},{5... | collective-permute-start | bytes 294920 | tf_op jit(solution)/shard_map/ppermute | solution.py:346
  51.8 4.6 %collective-permute-start.24 = (bf16[4,48,256]{2,1,0:T(8,128)(2,1)S(1)}, bf16[4,48,256]{2,1,0:T(8,128)(2,1)S(1)}, u32[]{:S(2)}, u32[]{:S(2)}) collective-permute-start(bf16[4,48,256]{2,1,0:T(8,128)(2,1)S(1)} %get-tuple-element.46.refs_0_), channel_id=1, source_target_pairs={{0,16},{4,20},{8,24},{12,28},{16,0},{20,4},{24,8},{28,12},{1,17},{... | collective-permute-start | bytes 294920 | tf_op jit(solution)/shard_map/ppermute | solution.py:346
  53.2 5.5 %collective-permute-start.25 = (bf16[4,48,256]{2,1,0:T(8,128)(2,1)S(1)}, bf16[4,48,256]{2,1,0:T(8,128)(2,1)S(1)}, u32[]{:S(2)}, u32[]{:S(2)}) collective-permute-start(bf16[4,48,256]{2,1,0:T(8,128)(2,1)S(1)} %get-tuple-element.46.refs_0_), channel_id=1, source_target_pairs={{0,24},{4,28},{8,16},{12,20},{16,8},{20,12},{24,0},{28,4},{1,25},{... | collective-permute-start | bytes 294920 | tf_op jit(solution)/shard_map/ppermute | solution.py:346
  54.2 6.4 %collective-permute-start.12 = (bf16[192,256]{1,0:T(8,128)(2,1)S(1)}, bf16[192,256]{1,0:T(8,128)(2,1)S(1)}, u32[]{:S(2)}, u32[]{:S(2)}) collective-permute-start(bf16[192,256]{1,0:T(8,128)(2,1)S(1)} %shard_map.97.refs_0_), channel_id=1, source_target_pairs={{0,3},{1,2},{2,1},{3,0},{4,7},{5,6},{6,5},{7,4},{8,11},{9,10},{10,... | collective-permute-start | bytes 294920 | tf_op jit(solution)/shard_map/ppermute | solution.py:363
  55.7 5.9 %collective-permute-start.26 = (bf16[4,48,256]{2,1,0:T(8,128)(2,1)S(1)}, bf16[4,48,256]{2,1,0:T(8,128)(2,1)S(1)}, u32[]{:S(2)}, u32[]{:S(2)}) collective-permute-start(bf16[4,48,256]{2,1,0:T(8,128)(2,1)S(1)} %get-tuple-element.46.refs_0_), channel_id=1, source_target_pairs={{0,4},{4,0},{8,12},{12,8},{16,20},{20,16},{24,28},{28,24},{1,5},{5... | collective-permute-start | bytes 294920 | tf_op jit(solution)/shard_map/ppermute | solution.py:349
  55.7 5.9 %collective-permute-start.27 = (bf16[4,48,256]{2,1,0:T(8,128)(2,1)S(1)}, bf16[4,48,256]{2,1,0:T(8,128)(2,1)S(1)}, u32[]{:S(2)}, u32[]{:S(2)}) collective-permute-start(bf16[4,48,256]{2,1,0:T(8,128)(2,1)S(1)} %collective-permute-done.23.refs_1_), channel_id=1, source_target_pairs={{0,4},{4,0},{8,12},{12,8},{16,20},{20,16},{24,28},{28,24},{1,5},{5... | collective-permute-start | bytes 294920 | tf_op jit(solution)/shard_map/ppermute | solution.py:349
  56.4 5.2 %collective-permute-start.28 = (bf16[4,48,256]{2,1,0:T(8,128)(2,1)S(1)}, bf16[4,48,256]{2,1,0:T(8,128)(2,1)S(1)}, u32[]{:S(2)}, u32[]{:S(2)}) collective-permute-start(bf16[4,48,256]{2,1,0:T(8,128)(2,1)S(1)} %collective-permute-done.24.refs_2_), channel_id=1, source_target_pairs={{0,4},{4,0},{8,12},{12,8},{16,20},{20,16},{24,28},{28,24},{1,5},{5... | collective-permute-start | bytes 294920 | tf_op jit(solution)/shard_map/ppermute | solution.py:349
  58.8 2.9 %collective-permute-start.29 = (bf16[4,48,256]{2,1,0:T(8,128)(2,1)S(1)}, bf16[4,48,256]{2,1,0:T(8,128)(2,1)S(1)}, u32[]{:S(2)}, u32[]{:S(2)}) collective-permute-start(bf16[4,48,256]{2,1,0:T(8,128)(2,1)S(1)} %collective-permute-done.25.refs_3_), channel_id=1, source_target_pairs={{0,4},{4,0},{8,12},{12,8},{16,20},{20,16},{24,28},{28,24},{1,5},{5... | collective-permute-start | bytes 294920 | tf_op jit(solution)/shard_map/ppermute | solution.py:349

commit v3 on v2

--- a/solution.py
+++ b/solution.py
@@ -70,7 +70,7 @@
     ]
     for copy in copies:
         copy.start()
-    for copy in copies[:4]:
+    for copy in copies[:3]:
         copy.wait()
     relations = words_ref.shape[0]
     seeds, width = grad_ref.shape
@@ -83,17 +83,21 @@
     rows = sums.shape[1]
     height = hidden.shape[1]
     per = rows // height
-    own = dot(low, weight_ref[0], NT)
-    total = jnp.concatenate([own, jnp.zeros((pre.shape[0] - seeds, own.shape[1]), F32)], 0)
     sums[0, :height] = dot(hidden[:seeds], low, TN)
+    matrices = []
     for r in range(1, relations + 1):
         spread = bits_two(words_ref[r - 1])
         inverse = 1.0 / jnp.maximum(jnp.sum(spread, axis=1, keepdims=True), 1.0)
         matrix = spread.astype(BF16)
+        matrices.append((matrix, inverse))
+        mixed = (dot(matrix, hidden) * inverse).astype(BF16)
+        sums[r // per, (r % per) * height : (r % per + 1) * height] = dot(mixed, low_bits, TN)
+    copies[3].wait()
+    own = dot(low, weight_ref[0], NT)
+    total = jnp.concatenate([own, jnp.zeros((pre.shape[0] - seeds, own.shape[1]), F32)], 0)
+    for r, (matrix, inverse) in enumerate(matrices, 1):
         back = (dot(low_bits, weight_ref[r], NT) * inverse).astype(BF16)
         total = total + dot(matrix, back, TN)
-        mixed = (dot(matrix, hidden) * inverse).astype(BF16)
-        sums[r // per, (r % per) * height : (r % per + 1) * height] = dot(mixed, low_bits, TN)
     hidden_grad = jnp.where(pre > 0, total, 0.0).astype(BF16)
     hidden_ref[...] = dot(reorder(total.shape[0]), hidden_grad).astype(BF16)
     core = core_of()
@@ -369,11 +373,11 @@
         blocks = [hidden] + [to_chip(hidden, k) for k in range(1, chips)]
         blocks = blocks + [to_core(block) for block in blocks]
         order = []
-        for flip in range(cores):
+        for turn in range(cores):
             for k in range(chips):
                 order.append(
-                    lambda flip=flip, k=k: lax.bitwise_xor(
-                        lax.axis_index("feat"), jnp.int32(k * cores + flip)
+                    lambda turn=turn, k=k: lax.bitwise_xor(
+                        lax.axis_index("feat"), jnp.int32(k * cores + turn)
                     )
                 )
         got_half = to_core(send_half)

time: 63 us -> 63 us (level)
  no operation moved by 1% of the time
where the time goes in v3:
time: 63 us; the launch traced here: 62.9 us
  starting transfers between devices  36.6 us (58%)
  waiting for transfers between devices  14.5 us (23%)
  Pallas kernels  11 us (17%)
  between operations  0.77 us (1%)
    ppermute x12, starting transfers between devices, to_rep(): return lax.ppermute(value, 'rep', pairs)  23.1 us
    ppermute x9, starting transfers between devices, to_chip(): return lax.ppermute(value, 'feat', pairs)  11.9 us
    ppermute x9, waiting for transfers between devices, to_chip(): return lax.ppermute(value, 'feat', pairs)  9.89 us
    ppermute x12, waiting for transfers between devices, to_rep(): return lax.ppermute(value, 'rep', pairs)  4.56 us
    pallas_call x2, Pallas kernels, on_device(): call(functools.partial(gather_kernel, start, run), shape(sets * width, ru...  4.24 us
    pallas_call x1, Pallas kernels, on_device(): call(functools.partial(upper_kernel, factor, core_of if direct else lambd...  3.03 us
    ppermute x9, starting transfers between devices, to_core(): return lax.ppermute(value, 'feat', [(i, i ^ 1) for i in range(feat)])  1.59 us
  transfers between devices with their start and end apart: 30, of which 9 were waited for; matrix products, arithmetic and copies ran while one was open for 0% of the time, Pallas kernels for 11%

profile of v3, /device:TPU:0, one launch (start us, length us, event | category | flops | bytes accessed | tf_op | source)
XLA Modules:
  0.0 62.9 jit_solution(9057977157726173945)
XLA Ops:
  0.6 3.0 %shard_map.93 = (bf16[256,256]{1,0:T(8,128)(2,1)S(1)}, f32[784,256]{1,0:T(8,128)S(1)}, f32[784,256]{1,0:T(8,128)S(1)}, s32[8,5,16,512]{3,2,1,0:T(8,128)S(1)}, bf16[8,128,512]{2,1,0:T(8,128)(2,1)S(1)}) custom-call(bf16[128,256]{1,0:T(8,128)(2,1)} %bitcast.11, s32[5,8,256]{2,1,0:T(8,128)} %bitcast.12, bf16[256,256]{1,0:T(8,128)(2,1)} %bitcast.10, ...), custom_call_target="tpu_custom_call" | custom-call | flops 1000000 | bytes 1000000 | tf_op jit(solution)/shard_map/pallas_call | solution.py:320
  4.2 2.6 %collective-permute-start = (bf16[256,256]{1,0:T(8,128)(2,1)S(1)}, bf16[256,256]{1,0:T(8,128)(2,1)S(1)}, u32[]{:S(2)}, u32[]{:S(2)}) collective-permute-start(bf16[256,256]{1,0:T(8,128)(2,1)S(1)} %get-tuple-element.30.refs_2_.refs_0_), channel_id=1, source_target_pairs={{0,8},{4,12},{8,0},{12,4},{16,24},{20,28},{24,16},{28,20},{1,9},{5... | collective-permute-start | bytes 393224 | tf_op jit(solution)/shard_map/ppermute | solution.py:350
  6.8 1.5 %collective-permute-start.1 = (bf16[256,256]{1,0:T(8,128)(2,1)S(1)}, bf16[256,256]{1,0:T(8,128)(2,1)S(1)}, u32[]{:S(2)}, u32[]{:S(2)}) collective-permute-start(bf16[256,256]{1,0:T(8,128)(2,1)S(1)} %get-tuple-element.30.refs_2_.refs_0_), channel_id=1, source_target_pairs={{0,16},{4,20},{8,24},{12,28},{16,0},{20,4},{24,8},{28,12},{1,17},{... | collective-permute-start | bytes 393224 | tf_op jit(solution)/shard_map/ppermute | solution.py:350
  8.3 2.7 %collective-permute-done.refs_3_.refs_1_ = bf16[256,256]{1,0:T(8,128)(2,1)S(1)} collective-permute-done((bf16[256,256]{1,0:T(8,128)(2,1)S(1)}, bf16[256,256]{1,0:T(8,128)(2,1)S(1)}, u32[]{:S(2)}, u32[]{:S(2)}) %collective-permute-start) | collective-permute-done | bytes 131104 | tf_op jit(solution)/shard_map/ppermute | solution.py:350
  11.0 2.6 %shard_map.94.refs_0_ = bf16[768,1280]{1,0:T(8,128)(2,1)S(1)} custom-call(bf16[8,128,512]{2,1,0:T(8,128)(2,1)S(1)} %get-tuple-element.28.column_ref, s32[8,5,16,512]{3,2,1,0:T(8,128)S(1)} %get-tuple-element.29.word_ref), custom_call_target="tpu_custom_call" | custom-call | flops 3000000000 | bytes 1000000 | tf_op jit(solution)/shard_map/pallas_call | solution.py:339
  13.7 1.5 %collective-permute-done.1.refs_4_.refs_2_ = bf16[256,256]{1,0:T(8,128)(2,1)S(1)} collective-permute-done((bf16[256,256]{1,0:T(8,128)(2,1)S(1)}, bf16[256,256]{1,0:T(8,128)(2,1)S(1)}, u32[]{:S(2)}, u32[]{:S(2)}) %collective-permute-start.1) | collective-permute-done | bytes 131104 | tf_op jit(solution)/shard_map/ppermute | solution.py:350
  15.8 1.6 %collective-permute-start.14 = (bf16[208,256]{1,0:T(8,128)(2,1)S(1)}, bf16[208,256]{1,0:T(8,128)(2,1)S(1)}, u32[]{:S(2)}, u32[]{:S(2)}) collective-permute-start(bf16[208,256]{1,0:T(8,128)(2,1)S(1)} %get-tuple-element.38), channel_id=1, source_target_pairs={{0,1},{1,0},{2,3},{3,2},{4,5},{5,4},{6,7},{7,6},{8,9},{9,8},{10,11... | collective-permute-start | bytes 319496 | tf_op jit(solution)/shard_map/ppermute | solution.py:367
  17.5 2.6 %collective-permute-start.15 = (bf16[208,256]{1,0:T(8,128)(2,1)S(1)}, bf16[208,256]{1,0:T(8,128)(2,1)S(1)}, u32[]{:S(2)}, u32[]{:S(2)}) collective-permute-start(bf16[208,256]{1,0:T(8,128)(2,1)S(1)} %get-tuple-element.39), channel_id=1, source_target_pairs={{0,2},{1,3},{2,0},{3,1},{4,6},{5,7},{6,4},{7,5},{8,10},{9,11},{10,... | collective-permute-start | bytes 319496 | tf_op jit(solution)/shard_map/ppermute | solution.py:367
  20.3 1.6 %shard_map.95.refs_1_ = bf16[768,768]{1,0:T(8,128)(2,1)S(1)} custom-call(bf16[8,128,512]{2,1,0:T(8,128)(2,1)S(1)} %get-tuple-element.28.column_ref, s32[8,5,16,512]{3,2,1,0:T(8,128)S(1)} %get-tuple-element.29.word_ref), custom_call_target="tpu_custom_call" | custom-call | flops 3000000000 | bytes 1000000 | tf_op jit(solution)/shard_map/pallas_call | solution.py:339
  21.9 1.1 %shard_map.96 = (f32[192,256]{1,0:T(8,128)S(1)}, bf16[192,256]{1,0:T(8,128)(2,1)S(1)}, bf16[192,256]{1,0:T(8,128)(2,1)S(1)}, bf16[192,256]{1,0:T(8,128)(2,1)S(1)}) custom-call(bf16[768,1280]{1,0:T(8,128)(2,1)S(1)} %shard_map.94.refs_0_, bf16[768,768]{1,0:T(8,128)(2,1)S(1)} %shard_map.95.refs_1_, bf16[256,256]{1,0:T(8,128)(2,1)S(1)} %get-tuple-element.30.refs_2_.refs_0_, ...), custom_call_target="tpu_custom_call" | custom-call | flops 1000000 | bytes 1000000 | tf_op jit(solution)/shard_map/pallas_call | solution.py:406
  23.1 0.7 %collective-permute-start.7 = (bf16[192,256]{1,0:T(8,128)(2,1)S(1)}, bf16[192,256]{1,0:T(8,128)(2,1)S(1)}, u32[]{:S(2)}, u32[]{:S(2)}) collective-permute-start(bf16[192,256]{1,0:T(8,128)(2,1)S(1)} %get-tuple-element.32), channel_id=1, source_target_pairs={{0,1},{1,0},{2,3},{3,2},{4,5},{5,4},{6,7},{7,6},{8,9},{9,8},{10,11... | collective-permute-start | bytes 294920 | tf_op jit(solution)/shard_map/ppermute | solution.py:367
  23.8 3.5 %collective-permute-start.8 = (bf16[192,256]{1,0:T(8,128)(2,1)S(1)}, bf16[192,256]{1,0:T(8,128)(2,1)S(1)}, u32[]{:S(2)}, u32[]{:S(2)}) collective-permute-start(bf16[192,256]{1,0:T(8,128)(2,1)S(1)} %get-tuple-element.33), channel_id=1, source_target_pairs={{0,2},{1,3},{2,0},{3,1},{4,6},{5,7},{6,4},{7,5},{8,10},{9,11},{10,... | collective-permute-start | bytes 294920 | tf_op jit(solution)/shard_map/ppermute | solution.py:367
  27.3 1.4 %collective-permute-done.15.refs_1_ = bf16[208,256]{1,0:T(8,128)(2,1)S(1)} collective-permute-done((bf16[208,256]{1,0:T(8,128)(2,1)S(1)}, bf16[208,256]{1,0:T(8,128)(2,1)S(1)}, u32[]{:S(2)}, u32[]{:S(2)}) %collective-permute-start.15) | collective-permute-done | bytes 106528 | tf_op jit(solution)/shard_map/ppermute | solution.py:367
  28.8 0.9 %collective-permute-start.17 = (bf16[64,256]{1,0:T(8,128)(2,1)S(1)}, bf16[64,256]{1,0:T(8,128)(2,1)S(1)}, u32[]{:S(2)}, u32[]{:S(2)}) collective-permute-start(bf16[64,256]{1,0:T(8,128)(2,1)S(1)} %get-tuple-element.42), channel_id=1, source_target_pairs={{0,8},{4,12},{8,0},{12,4},{16,24},{20,28},{24,16},{28,20},{1,9},{5... | collective-permute-start | bytes 98312 | tf_op jit(solution)/shard_map/ppermute | solution.py:350
  29.8 2.7 %collective-permute-start.9 = (bf16[192,256]{1,0:T(8,128)(2,1)S(1)}, bf16[192,256]{1,0:T(8,128)(2,1)S(1)}, u32[]{:S(2)}, u32[]{:S(2)}) collective-permute-start(bf16[192,256]{1,0:T(8,128)(2,1)S(1)} %get-tuple-element.34), channel_id=1, source_target_pairs={{0,3},{1,2},{2,1},{3,0},{4,7},{5,6},{6,5},{7,4},{8,11},{9,10},{10,... | collective-permute-start | bytes 294920 | tf_op jit(solution)/shard_map/ppermute | solution.py:367
  32.4 1.6 %collective-permute-start.18 = (bf16[64,256]{1,0:T(8,128)(2,1)S(1)}, bf16[64,256]{1,0:T(8,128)(2,1)S(1)}, u32[]{:S(2)}, u32[]{:S(2)}) collective-permute-start(bf16[64,256]{1,0:T(8,128)(2,1)S(1)} %get-tuple-element.43), channel_id=1, source_target_pairs={{0,16},{4,20},{8,24},{12,28},{16,0},{20,4},{24,8},{28,12},{1,17},{... | collective-permute-start | bytes 98312 | tf_op jit(solution)/shard_map/ppermute | solution.py:350
  34.0 1.8 %collective-permute-start.19 = (bf16[64,256]{1,0:T(8,128)(2,1)S(1)}, bf16[64,256]{1,0:T(8,128)(2,1)S(1)}, u32[]{:S(2)}, u32[]{:S(2)}) collective-permute-start(bf16[64,256]{1,0:T(8,128)(2,1)S(1)} %get-tuple-element.44), channel_id=1, source_target_pairs={{0,24},{4,28},{8,16},{12,20},{16,8},{20,12},{24,0},{28,4},{1,25},{... | collective-permute-start | bytes 98312 | tf_op jit(solution)/shard_map/ppermute | solution.py:350
  36.4 2.5 %collective-permute-done.19.refs_10_ = bf16[64,256]{1,0:T(8,128)(2,1)S(1)} collective-permute-done((bf16[64,256]{1,0:T(8,128)(2,1)S(1)}, bf16[64,256]{1,0:T(8,128)(2,1)S(1)}, u32[]{:S(2)}, u32[]{:S(2)}) %collective-permute-start.19) | collective-permute-done | bytes 32800 | tf_op jit(solution)/shard_map/ppermute | solution.py:350
  39.0 4.9 %collective-permute-start.20 = (bf16[64,256]{1,0:T(8,128)(2,1)S(1)}, bf16[64,256]{1,0:T(8,128)(2,1)S(1)}, u32[]{:S(2)}, u32[]{:S(2)}) collective-permute-start(bf16[64,256]{1,0:T(8,128)(2,1)S(1)} %get-tuple-element.45.refs_0_), channel_id=1, source_target_pairs={{0,1},{1,0},{2,3},{3,2},{4,5},{5,4},{6,7},{7,6},{8,9},{9,8},{10,11... | collective-permute-start | bytes 98312 | tf_op jit(solution)/shard_map/ppermute | solution.py:367
  43.9 0.9 %collective-permute-start.21 = (bf16[64,256]{1,0:T(8,128)(2,1)S(1)}, bf16[64,256]{1,0:T(8,128)(2,1)S(1)}, u32[]{:S(2)}, u32[]{:S(2)}) collective-permute-start(bf16[64,256]{1,0:T(8,128)(2,1)S(1)} %get-tuple-element.45.refs_0_), channel_id=1, source_target_pairs={{0,2},{1,3},{2,0},{3,1},{4,6},{5,7},{6,4},{7,5},{8,10},{9,11},{10,... | collective-permute-start | bytes 98312 | tf_op jit(solution)/shard_map/ppermute | solution.py:367
  44.9 1.5 %collective-permute-start.22 = (bf16[64,256]{1,0:T(8,128)(2,1)S(1)}, bf16[64,256]{1,0:T(8,128)(2,1)S(1)}, u32[]{:S(2)}, u32[]{:S(2)}) collective-permute-start(bf16[64,256]{1,0:T(8,128)(2,1)S(1)} %get-tuple-element.45.refs_0_), channel_id=1, source_target_pairs={{0,3},{1,2},{2,1},{3,0},{4,7},{5,6},{6,5},{7,4},{8,11},{9,10},{10,... | collective-permute-start | bytes 98312 | tf_op jit(solution)/shard_map/ppermute | solution.py:367
  46.4 1.1 %collective-permute-start.10 = (bf16[192,256]{1,0:T(8,128)(2,1)S(1)}, bf16[192,256]{1,0:T(8,128)(2,1)S(1)}, u32[]{:S(2)}, u32[]{:S(2)}) collective-permute-start(bf16[192,256]{1,0:T(8,128)(2,1)S(1)} %shard_map.97.refs_0_), channel_id=1, source_target_pairs={{0,1},{1,0},{2,3},{3,2},{4,5},{5,4},{6,7},{7,6},{8,9},{9,8},{10,11... | collective-permute-start | bytes 294920 | tf_op jit(solution)/shard_map/ppermute | solution.py:367
  47.5 1.8 %collective-permute-start.11 = (bf16[192,256]{1,0:T(8,128)(2,1)S(1)}, bf16[192,256]{1,0:T(8,128)(2,1)S(1)}, u32[]{:S(2)}, u32[]{:S(2)}) collective-permute-start(bf16[192,256]{1,0:T(8,128)(2,1)S(1)} %shard_map.97.refs_0_), channel_id=1, source_target_pairs={{0,2},{1,3},{2,0},{3,1},{4,6},{5,7},{6,4},{7,5},{8,10},{9,11},{10,... | collective-permute-start | bytes 294920 | tf_op jit(solution)/shard_map/ppermute | solution.py:367
  49.4 1.3 %collective-permute-done.22.refs_3_ = bf16[64,256]{1,0:T(8,128)(2,1)S(1)} collective-permute-done((bf16[64,256]{1,0:T(8,128)(2,1)S(1)}, bf16[64,256]{1,0:T(8,128)(2,1)S(1)}, u32[]{:S(2)}, u32[]{:S(2)}) %collective-permute-start.22) | collective-permute-done | bytes 32800 | tf_op jit(solution)/shard_map/ppermute | solution.py:367
  50.7 1.1 %collective-permute-start.23 = (bf16[4,48,256]{2,1,0:T(8,128)(2,1)S(1)}, bf16[4,48,256]{2,1,0:T(8,128)(2,1)S(1)}, u32[]{:S(2)}, u32[]{:S(2)}) collective-permute-start(bf16[4,48,256]{2,1,0:T(8,128)(2,1)S(1)} %get-tuple-element.46.refs_0_), channel_id=1, source_target_pairs={{0,8},{4,12},{8,0},{12,4},{16,24},{20,28},{24,16},{28,20},{1,9},{5... | collective-permute-start | bytes 294920 | tf_op jit(solution)/shard_map/ppermute | solution.py:350
  51.8 1.5 %collective-permute-start.24 = (bf16[4,48,256]{2,1,0:T(8,128)(2,1)S(1)}, bf16[4,48,256]{2,1,0:T(8,128)(2,1)S(1)}, u32[]{:S(2)}, u32[]{:S(2)}) collective-permute-start(bf16[4,48,256]{2,1,0:T(8,128)(2,1)S(1)} %get-tuple-element.46.refs_0_), channel_id=1, source_target_pairs={{0,16},{4,20},{8,24},{12,28},{16,0},{20,4},{24,8},{28,12},{1,17},{... | collective-permute-start | bytes 294920 | tf_op jit(solution)/shard_map/ppermute | solution.py:350
  53.4 0.9 %collective-permute-start.25 = (bf16[4,48,256]{2,1,0:T(8,128)(2,1)S(1)}, bf16[4,48,256]{2,1,0:T(8,128)(2,1)S(1)}, u32[]{:S(2)}, u32[]{:S(2)}) collective-permute-start(bf16[4,48,256]{2,1,0:T(8,128)(2,1)S(1)} %get-tuple-element.46.refs_0_), channel_id=1, source_target_pairs={{0,24},{4,28},{8,16},{12,20},{16,8},{20,12},{24,0},{28,4},{1,25},{... | collective-permute-start | bytes 294920 | tf_op jit(solution)/shard_map/ppermute | solution.py:350
  54.3 1.4 %collective-permute-start.12 = (bf16[192,256]{1,0:T(8,128)(2,1)S(1)}, bf16[192,256]{1,0:T(8,128)(2,1)S(1)}, u32[]{:S(2)}, u32[]{:S(2)}) collective-permute-start(bf16[192,256]{1,0:T(8,128)(2,1)S(1)} %shard_map.97.refs_0_), channel_id=1, source_target_pairs={{0,3},{1,2},{2,1},{3,0},{4,7},{5,6},{6,5},{7,4},{8,11},{9,10},{10,... | collective-permute-start | bytes 294920 | tf_op jit(solution)/shard_map/ppermute | solution.py:367
  56.5 2.4 %collective-permute-done.25.refs_3_ = bf16[4,48,256]{2,1,0:T(8,128)(2,1)S(1)} collective-permute-done((bf16[4,48,256]{2,1,0:T(8,128)(2,1)S(1)}, bf16[4,48,256]{2,1,0:T(8,128)(2,1)S(1)}, u32[]{:S(2)}, u32[]{:S(2)}) %collective-permute-start.25) | collective-permute-done | bytes 98336 | tf_op jit(solution)/shard_map/ppermute | solution.py:350
  58.9 1.8 %collective-permute-done.12.refs_3_ = bf16[192,256]{1,0:T(8,128)(2,1)S(1)} collective-permute-done((bf16[192,256]{1,0:T(8,128)(2,1)S(1)}, bf16[192,256]{1,0:T(8,128)(2,1)S(1)}, u32[]{:S(2)}, u32[]{:S(2)}) %collective-permute-start.12) | collective-permute-done | bytes 98336 | tf_op jit(solution)/shard_map/ppermute | solution.py:367
  60.7 0.9 %shard_map.98 = f32[4,192,256]{2,1,0:T(8,128)} custom-call(bf16[192,256]{1,0:T(8,128)(2,1)S(1)} %shard_map.97.refs_0_, bf16[192,256]{1,0:T(8,128)(2,1)S(1)} %collective-permute-done.10.refs_1_, bf16[192,256]{1,0:T(8,128)(2,1)S(1)} %collective-permute-done.11.refs_2_, bf16[192,256]{1,0:T(8,128)(2,1)S(1)} %collective-permute-done.12.refs_3_), custom_call_target="tpu_custom_call" | custom-call | flops 1000000 | bytes 1000000 | tf_op jit(solution)/shard_map/pallas_call | solution.py:438
  61.6 1.2 %shard_map.103 = (f32[2,4,4,48,256]{4,3,2,1,0:T(8,128)}, f32[256]{0:T(256)}, f32[256]{0:T(256)}) custom-call(bf16[4,48,256]{2,1,0:T(8,128)(2,1)S(1)} %get-tuple-element.46.refs_0_, bf16[4,48,256]{2,1,0:T(8,128)(2,1)S(1)} %collective-permute-done.23.refs_1_, bf16[4,48,256]{2,1,0:T(8,128)(2,1)S(1)} %collective-permute-done.24.refs_2_, ...), custom_call_target="tpu_custom_call" | custom-call | flops 1000000 | bytes 1000000 | tf_op jit(solution)/shard_map/pallas_call | solution.py:460
  (39 shorter events, 3.2 us)
Async XLA Ops:
  3.7 12.0 %collective-permute-start.13 = (f32[784,256]{1,0:T(8,128)S(1)}, f32[784,256]{1,0:T(8,128)S(1)}, u32[]{:S(2)}, u32[]{:S(2)}) collective-permute-start(f32[784,256]{1,0:T(8,128)S(1)} %get-tuple-element.36), channel_id=1, source_target_pairs={{0,4},{4,0},{8,12},{12,8},{16,20},{20,16},{24,28},{28,24},{1,5},{5... | collective-permute-start | bytes 2408456 | tf_op jit(solution)/shard_map/ppermute | solution.py:353
  4.2 6.8 %collective-permute-start = (bf16[256,256]{1,0:T(8,128)(2,1)S(1)}, bf16[256,256]{1,0:T(8,128)(2,1)S(1)}, u32[]{:S(2)}, u32[]{:S(2)}) collective-permute-start(bf16[256,256]{1,0:T(8,128)(2,1)S(1)} %get-tuple-element.30.refs_2_.refs_0_), channel_id=1, source_target_pairs={{0,8},{4,12},{8,0},{12,4},{16,24},{20,28},{24,16},{28,20},{1,9},{5... | collective-permute-start | bytes 393224 | tf_op jit(solution)/shard_map/ppermute | solution.py:350
  6.8 8.4 %collective-permute-start.1 = (bf16[256,256]{1,0:T(8,128)(2,1)S(1)}, bf16[256,256]{1,0:T(8,128)(2,1)S(1)}, u32[]{:S(2)}, u32[]{:S(2)}) collective-permute-start(bf16[256,256]{1,0:T(8,128)(2,1)S(1)} %get-tuple-element.30.refs_2_.refs_0_), channel_id=1, source_target_pairs={{0,16},{4,20},{8,24},{12,28},{16,0},{20,4},{24,8},{28,12},{1,17},{... | collective-permute-start | bytes 393224 | tf_op jit(solution)/shard_map/ppermute | solution.py:350
  8.3 6.8 %collective-permute-start.2 = (bf16[256,256]{1,0:T(8,128)(2,1)S(1)}, bf16[256,256]{1,0:T(8,128)(2,1)S(1)}, u32[]{:S(2)}, u32[]{:S(2)}) collective-permute-start(bf16[256,256]{1,0:T(8,128)(2,1)S(1)} %get-tuple-element.30.refs_2_.refs_0_), channel_id=1, source_target_pairs={{0,24},{4,28},{8,16},{12,20},{16,8},{20,12},{24,0},{28,4},{1,25},{... | collective-permute-start | bytes 393224 | tf_op jit(solution)/shard_map/ppermute | solution.py:350
  8.3 9.1 %collective-permute-start.3 = (bf16[256,256]{1,0:T(8,128)(2,1)S(1)}, bf16[256,256]{1,0:T(8,128)(2,1)S(1)}, u32[]{:S(2)}, u32[]{:S(2)}) collective-permute-start(bf16[256,256]{1,0:T(8,128)(2,1)S(1)} %get-tuple-element.30.refs_2_.refs_0_), channel_id=1, source_target_pairs={{0,4},{4,0},{8,12},{12,8},{16,20},{20,16},{24,28},{28,24},{1,5},{5... | collective-permute-start | bytes 393224 | tf_op jit(solution)/shard_map/ppermute | solution.py:353
  11.0 9.0 %collective-permute-start.4 = (bf16[256,256]{1,0:T(8,128)(2,1)S(1)}, bf16[256,256]{1,0:T(8,128)(2,1)S(1)}, u32[]{:S(2)}, u32[]{:S(2)}) collective-permute-start(bf16[256,256]{1,0:T(8,128)(2,1)S(1)} %collective-permute-done.refs_3_.refs_1_), channel_id=1, source_target_pairs={{0,4},{4,0},{8,12},{12,8},{16,20},{20,16},{24,28},{28,24},{1,5},{5... | collective-permute-start | bytes 393224 | tf_op jit(solution)/shard_map/ppermute | solution.py:353
  15.2 6.8 %collective-permute-start.5 = (bf16[256,256]{1,0:T(8,128)(2,1)S(1)}, bf16[256,256]{1,0:T(8,128)(2,1)S(1)}, u32[]{:S(2)}, u32[]{:S(2)}) collective-permute-start(bf16[256,256]{1,0:T(8,128)(2,1)S(1)} %collective-permute-done.1.refs_4_.refs_2_), channel_id=1, source_target_pairs={{0,4},{4,0},{8,12},{12,8},{16,20},{20,16},{24,28},{28,24},{1,5},{5... | collective-permute-start | bytes 393224 | tf_op jit(solution)/shard_map/ppermute | solution.py:353
  15.2 6.8 %collective-permute-start.6 = (bf16[256,256]{1,0:T(8,128)(2,1)S(1)}, bf16[256,256]{1,0:T(8,128)(2,1)S(1)}, u32[]{:S(2)}, u32[]{:S(2)}) collective-permute-start(bf16[256,256]{1,0:T(8,128)(2,1)S(1)} %collective-permute-done.2.refs_5_.refs_3_), channel_id=1, source_target_pairs={{0,4},{4,0},{8,12},{12,8},{16,20},{20,16},{24,28},{28,24},{1,5},{5... | collective-permute-start | bytes 393224 | tf_op jit(solution)/shard_map/ppermute | solution.py:353
  15.8 11.5 %collective-permute-start.14 = (bf16[208,256]{1,0:T(8,128)(2,1)S(1)}, bf16[208,256]{1,0:T(8,128)(2,1)S(1)}, u32[]{:S(2)}, u32[]{:S(2)}) collective-permute-start(bf16[208,256]{1,0:T(8,128)(2,1)S(1)} %get-tuple-element.38), channel_id=1, source_target_pairs={{0,1},{1,0},{2,3},{3,2},{4,5},{5,4},{6,7},{7,6},{8,9},{9,8},{10,11... | collective-permute-start | bytes 319496 | tf_op jit(solution)/shard_map/ppermute | solution.py:367
  17.5 11.3 %collective-permute-start.15 = (bf16[208,256]{1,0:T(8,128)(2,1)S(1)}, bf16[208,256]{1,0:T(8,128)(2,1)S(1)}, u32[]{:S(2)}, u32[]{:S(2)}) collective-permute-start(bf16[208,256]{1,0:T(8,128)(2,1)S(1)} %get-tuple-element.39), channel_id=1, source_target_pairs={{0,2},{1,3},{2,0},{3,1},{4,6},{5,7},{6,4},{7,5},{8,10},{9,11},{10,... | collective-permute-start | bytes 319496 | tf_op jit(solution)/shard_map/ppermute | solution.py:367
  20.0 8.7 %collective-permute-start.16 = (bf16[208,256]{1,0:T(8,128)(2,1)S(1)}, bf16[208,256]{1,0:T(8,128)(2,1)S(1)}, u32[]{:S(2)}, u32[]{:S(2)}) collective-permute-start(bf16[208,256]{1,0:T(8,128)(2,1)S(1)} %get-tuple-element.40), channel_id=1, source_target_pairs={{0,3},{1,2},{2,1},{3,0},{4,7},{5,6},{6,5},{7,4},{8,11},{9,10},{10,... | collective-permute-start | bytes 319496 | tf_op jit(solution)/shard_map/ppermute | solution.py:367
  23.1 21.8 %collective-permute-start.7 = (bf16[192,256]{1,0:T(8,128)(2,1)S(1)}, bf16[192,256]{1,0:T(8,128)(2,1)S(1)}, u32[]{:S(2)}, u32[]{:S(2)}) collective-permute-start(bf16[192,256]{1,0:T(8,128)(2,1)S(1)} %get-tuple-element.32), channel_id=1, source_target_pairs={{0,1},{1,0},{2,3},{3,2},{4,5},{5,4},{6,7},{7,6},{8,9},{9,8},{10,11... | collective-permute-start | bytes 294920 | tf_op jit(solution)/shard_map/ppermute | solution.py:367
  23.8 22.6 %collective-permute-start.8 = (bf16[192,256]{1,0:T(8,128)(2,1)S(1)}, bf16[192,256]{1,0:T(8,128)(2,1)S(1)}, u32[]{:S(2)}, u32[]{:S(2)}) collective-permute-start(bf16[192,256]{1,0:T(8,128)(2,1)S(1)} %get-tuple-element.33), channel_id=1, source_target_pairs={{0,2},{1,3},{2,0},{3,1},{4,6},{5,7},{6,4},{7,5},{8,10},{9,11},{10,... | collective-permute-start | bytes 294920 | tf_op jit(solution)/shard_map/ppermute | solution.py:367
  28.8 5.2 %collective-permute-start.17 = (bf16[64,256]{1,0:T(8,128)(2,1)S(1)}, bf16[64,256]{1,0:T(8,128)(2,1)S(1)}, u32[]{:S(2)}, u32[]{:S(2)}) collective-permute-start(bf16[64,256]{1,0:T(8,128)(2,1)S(1)} %get-tuple-element.42), channel_id=1, source_target_pairs={{0,8},{4,12},{8,0},{12,4},{16,24},{20,28},{24,16},{28,20},{1,9},{5... | collective-permute-start | bytes 98312 | tf_op jit(solution)/shard_map/ppermute | solution.py:350
  29.8 16.6 %collective-permute-start.9 = (bf16[192,256]{1,0:T(8,128)(2,1)S(1)}, bf16[192,256]{1,0:T(8,128)(2,1)S(1)}, u32[]{:S(2)}, u32[]{:S(2)}) collective-permute-start(bf16[192,256]{1,0:T(8,128)(2,1)S(1)} %get-tuple-element.34), channel_id=1, source_target_pairs={{0,3},{1,2},{2,1},{3,0},{4,7},{5,6},{6,5},{7,4},{8,11},{9,10},{10,... | collective-permute-start | bytes 294920 | tf_op jit(solution)/shard_map/ppermute | solution.py:367
  32.4 3.9 %collective-permute-start.18 = (bf16[64,256]{1,0:T(8,128)(2,1)S(1)}, bf16[64,256]{1,0:T(8,128)(2,1)S(1)}, u32[]{:S(2)}, u32[]{:S(2)}) collective-permute-start(bf16[64,256]{1,0:T(8,128)(2,1)S(1)} %get-tuple-element.43), channel_id=1, source_target_pairs={{0,16},{4,20},{8,24},{12,28},{16,0},{20,4},{24,8},{28,12},{1,17},{... | collective-permute-start | bytes 98312 | tf_op jit(solution)/shard_map/ppermute | solution.py:350
  34.0 4.8 %collective-permute-start.19 = (bf16[64,256]{1,0:T(8,128)(2,1)S(1)}, bf16[64,256]{1,0:T(8,128)(2,1)S(1)}, u32[]{:S(2)}, u32[]{:S(2)}) collective-permute-start(bf16[64,256]{1,0:T(8,128)(2,1)S(1)} %get-tuple-element.44), channel_id=1, source_target_pairs={{0,24},{4,28},{8,16},{12,20},{16,8},{20,12},{24,0},{28,4},{1,25},{... | collective-permute-start | bytes 98312 | tf_op jit(solution)/shard_map/ppermute | solution.py:350
  39.0 10.3 %collective-permute-start.20 = (bf16[64,256]{1,0:T(8,128)(2,1)S(1)}, bf16[64,256]{1,0:T(8,128)(2,1)S(1)}, u32[]{:S(2)}, u32[]{:S(2)}) collective-permute-start(bf16[64,256]{1,0:T(8,128)(2,1)S(1)} %get-tuple-element.45.refs_0_), channel_id=1, source_target_pairs={{0,1},{1,0},{2,3},{3,2},{4,5},{5,4},{6,7},{7,6},{8,9},{9,8},{10,11... | collective-permute-start | bytes 98312 | tf_op jit(solution)/shard_map/ppermute | solution.py:367
  43.9 5.5 %collective-permute-start.21 = (bf16[64,256]{1,0:T(8,128)(2,1)S(1)}, bf16[64,256]{1,0:T(8,128)(2,1)S(1)}, u32[]{:S(2)}, u32[]{:S(2)}) collective-permute-start(bf16[64,256]{1,0:T(8,128)(2,1)S(1)} %get-tuple-element.45.refs_0_), channel_id=1, source_target_pairs={{0,2},{1,3},{2,0},{3,1},{4,6},{5,7},{6,4},{7,5},{8,10},{9,11},{10,... | collective-permute-start | bytes 98312 | tf_op jit(solution)/shard_map/ppermute | solution.py:367
  44.9 5.8 %collective-permute-start.22 = (bf16[64,256]{1,0:T(8,128)(2,1)S(1)}, bf16[64,256]{1,0:T(8,128)(2,1)S(1)}, u32[]{:S(2)}, u32[]{:S(2)}) collective-permute-start(bf16[64,256]{1,0:T(8,128)(2,1)S(1)} %get-tuple-element.45.refs_0_), channel_id=1, source_target_pairs={{0,3},{1,2},{2,1},{3,0},{4,7},{5,6},{6,5},{7,4},{8,11},{9,10},{10,... | collective-permute-start | bytes 98312 | tf_op jit(solution)/shard_map/ppermute | solution.py:367
  46.4 7.8 %collective-permute-start.10 = (bf16[192,256]{1,0:T(8,128)(2,1)S(1)}, bf16[192,256]{1,0:T(8,128)(2,1)S(1)}, u32[]{:S(2)}, u32[]{:S(2)}) collective-permute-start(bf16[192,256]{1,0:T(8,128)(2,1)S(1)} %shard_map.97.refs_0_), channel_id=1, source_target_pairs={{0,1},{1,0},{2,3},{3,2},{4,5},{5,4},{6,7},{7,6},{8,9},{9,8},{10,11... | collective-permute-start | bytes 294920 | tf_op jit(solution)/shard_map/ppermute | solution.py:367
  47.5 8.2 %collective-permute-start.11 = (bf16[192,256]{1,0:T(8,128)(2,1)S(1)}, bf16[192,256]{1,0:T(8,128)(2,1)S(1)}, u32[]{:S(2)}, u32[]{:S(2)}) collective-permute-start(bf16[192,256]{1,0:T(8,128)(2,1)S(1)} %shard_map.97.refs_0_), channel_id=1, source_target_pairs={{0,2},{1,3},{2,0},{3,1},{4,6},{5,7},{6,4},{7,5},{8,10},{9,11},{10,... | collective-permute-start | bytes 294920 | tf_op jit(solution)/shard_map/ppermute | solution.py:367
  50.7 5.0 %collective-permute-start.23 = (bf16[4,48,256]{2,1,0:T(8,128)(2,1)S(1)}, bf16[4,48,256]{2,1,0:T(8,128)(2,1)S(1)}, u32[]{:S(2)}, u32[]{:S(2)}) collective-permute-start(bf16[4,48,256]{2,1,0:T(8,128)(2,1)S(1)} %get-tuple-element.46.refs_0_), channel_id=1, source_target_pairs={{0,8},{4,12},{8,0},{12,4},{16,24},{20,28},{24,16},{28,20},{1,9},{5... | collective-permute-start | bytes 294920 | tf_op jit(solution)/shard_map/ppermute | solution.py:350
  51.8 4.6 %collective-permute-start.24 = (bf16[4,48,256]{2,1,0:T(8,128)(2,1)S(1)}, bf16[4,48,256]{2,1,0:T(8,128)(2,1)S(1)}, u32[]{:S(2)}, u32[]{:S(2)}) collective-permute-start(bf16[4,48,256]{2,1,0:T(8,128)(2,1)S(1)} %get-tuple-element.46.refs_0_), channel_id=1, source_target_pairs={{0,16},{4,20},{8,24},{12,28},{16,0},{20,4},{24,8},{28,12},{1,17},{... | collective-permute-start | bytes 294920 | tf_op jit(solution)/shard_map/ppermute | solution.py:350
  53.4 5.5 %collective-permute-start.25 = (bf16[4,48,256]{2,1,0:T(8,128)(2,1)S(1)}, bf16[4,48,256]{2,1,0:T(8,128)(2,1)S(1)}, u32[]{:S(2)}, u32[]{:S(2)}) collective-permute-start(bf16[4,48,256]{2,1,0:T(8,128)(2,1)S(1)} %get-tuple-element.46.refs_0_), channel_id=1, source_target_pairs={{0,24},{4,28},{8,16},{12,20},{16,8},{20,12},{24,0},{28,4},{1,25},{... | collective-permute-start | bytes 294920 | tf_op jit(solution)/shard_map/ppermute | solution.py:350
  54.3 6.4 %collective-permute-start.12 = (bf16[192,256]{1,0:T(8,128)(2,1)S(1)}, bf16[192,256]{1,0:T(8,128)(2,1)S(1)}, u32[]{:S(2)}, u32[]{:S(2)}) collective-permute-start(bf16[192,256]{1,0:T(8,128)(2,1)S(1)} %shard_map.97.refs_0_), channel_id=1, source_target_pairs={{0,3},{1,2},{2,1},{3,0},{4,7},{5,6},{6,5},{7,4},{8,11},{9,10},{10,... | collective-permute-start | bytes 294920 | tf_op jit(solution)/shard_map/ppermute | solution.py:367
  55.7 5.9 %collective-permute-start.26 = (bf16[4,48,256]{2,1,0:T(8,128)(2,1)S(1)}, bf16[4,48,256]{2,1,0:T(8,128)(2,1)S(1)}, u32[]{:S(2)}, u32[]{:S(2)}) collective-permute-start(bf16[4,48,256]{2,1,0:T(8,128)(2,1)S(1)} %get-tuple-element.46.refs_0_), channel_id=1, source_target_pairs={{0,4},{4,0},{8,12},{12,8},{16,20},{20,16},{24,28},{28,24},{1,5},{5... | collective-permute-start | bytes 294920 | tf_op jit(solution)/shard_map/ppermute | solution.py:353
  55.7 5.9 %collective-permute-start.27 = (bf16[4,48,256]{2,1,0:T(8,128)(2,1)S(1)}, bf16[4,48,256]{2,1,0:T(8,128)(2,1)S(1)}, u32[]{:S(2)}, u32[]{:S(2)}) collective-permute-start(bf16[4,48,256]{2,1,0:T(8,128)(2,1)S(1)} %collective-permute-done.23.refs_1_), channel_id=1, source_target_pairs={{0,4},{4,0},{8,12},{12,8},{16,20},{20,16},{24,28},{28,24},{1,5},{5... | collective-permute-start | bytes 294920 | tf_op jit(solution)/shard_map/ppermute | solution.py:353
  56.4 5.2 %collective-permute-start.28 = (bf16[4,48,256]{2,1,0:T(8,128)(2,1)S(1)}, bf16[4,48,256]{2,1,0:T(8,128)(2,1)S(1)}, u32[]{:S(2)}, u32[]{:S(2)}) collective-permute-start(bf16[4,48,256]{2,1,0:T(8,128)(2,1)S(1)} %collective-permute-done.24.refs_2_), channel_id=1, source_target_pairs={{0,4},{4,0},{8,12},{12,8},{16,20},{20,16},{24,28},{28,24},{1,5},{5... | collective-permute-start | bytes 294920 | tf_op jit(solution)/shard_map/ppermute | solution.py:353
  58.9 2.8 %collective-permute-start.29 = (bf16[4,48,256]{2,1,0:T(8,128)(2,1)S(1)}, bf16[4,48,256]{2,1,0:T(8,128)(2,1)S(1)}, u32[]{:S(2)}, u32[]{:S(2)}) collective-permute-start(bf16[4,48,256]{2,1,0:T(8,128)(2,1)S(1)} %collective-permute-done.25.refs_3_), channel_id=1, source_target_pairs={{0,4},{4,0},{8,12},{12,8},{16,20},{20,16},{24,28},{28,24},{1,5},{5... | collective-permute-start | bytes 294920 | tf_op jit(solution)/shard_map/ppermute | solution.py:353

commit v4 on v3

--- a/solution.py
+++ b/solution.py
@@ -269,7 +269,17 @@
         copy.wait()
 
 
-def place_two_kernel(order, *refs):
+def place_blocks(blocks, order, out, held, sems):
+    copies = []
+    for n, (block, place) in enumerate(zip(blocks, order)):
+        core, chip = place()
+        held[n] = block[...].astype(F32)
+        copies.append(pltpu.make_async_copy(held.at[n], out.at[core, :, chip], sems.at[n]))
+        copies[-1].start()
+    return copies
+
+
+def place_first_kernel(order, *refs):
     blocks, (one_ref, two_ref) = refs[: len(order)], refs[len(order) : len(order) + 2]
     out, one_out, two_out, held, sems = refs[len(order) + 2 :]
     copies = [
@@ -278,12 +288,14 @@
     ]
     for copy in copies:
         copy.start()
-    for n, (block, place) in enumerate(zip(blocks, order)):
-        core, chip = place()
-        held[n] = block[...].astype(F32)
-        copies.append(pltpu.make_async_copy(held.at[n], out.at[core, :, chip], sems.at[n]))
-        copies[-1].start()
+    copies += place_blocks(blocks, order, out, held, sems)
     for copy in copies:
+        copy.wait()
+
+
+def place_rest_kernel(order, begun, *refs):
+    blocks, (out, held, sems) = refs[: len(order)], refs[len(order) :]
+    for copy in place_blocks(blocks, order, out, held, sems):
         copy.wait()
 
 
@@ -457,19 +469,30 @@
                         lax.bitwise_xor(chip_of(), jnp.int32(k)),
                     )
                 )
-        grad_w2, bias_one, bias_two = call(
-            functools.partial(place_two_kernel, places),
+        early = [n * chips for n in range(cores)]
+        late = [n for n in range(feat) if n not in early]
+        whole = jax.ShapeDtypeStruct((cores, reps, chips, piece, hidden_width), F32)
+        in_memory = pl.BlockSpec(memory_space=pltpu.HBM)
+        begun, bias_one, bias_two = call(
+            functools.partial(place_first_kernel, [places[n] for n in early]),
+            (whole,) + (jax.ShapeDtypeStruct((hidden_width,), F32),) * 2,
             (
-                jax.ShapeDtypeStruct((cores, reps, chips, piece, hidden_width), F32),
-                jax.ShapeDtypeStruct((hidden_width,), F32),
-                jax.ShapeDtypeStruct((hidden_width,), F32),
+                pltpu.VMEM((len(early), reps, piece, hidden_width), F32),
+                pltpu.SemaphoreType.DMA((len(early) + 2,)),
             ),
+            out_specs=[in_memory] * 3,
+        )(*[upper_all[n] for n in early], bias_one, bias_two)
+        grad_w2 = call(
+            functools.partial(place_rest_kernel, [places[n] for n in late]),
+            whole,
             (
-                pltpu.VMEM((feat, reps, piece, hidden_width), F32),
-                pltpu.SemaphoreType.DMA((feat + 2,)),
+                pltpu.VMEM((len(late), reps, piece, hidden_width), F32),
+                pltpu.SemaphoreType.DMA((len(late),)),
             ),
-            out_specs=[pl.BlockSpec(memory_space=pltpu.HBM)] * 3,
-        )(*upper_all, bias_one, bias_two)
+            in_specs=[in_memory] + [VMEM] * len(late),
+            out_specs=in_memory,
+            input_output_aliases={0: 0},
+        )(begun, *[upper_all[n] for n in late])
     else:
         grad_w2, bias_one, bias_two = upper, bias_one[0], bias_two[0]
     grad_w2 = grad_w2.reshape(sets, hidden_width, hidden_width)

time: 63 us -> 63.7 us (1.011)
  Pallas kernels: 11 us -> 11.7 us
    pallas_call x1 -> x2, Pallas kernels: 1.24 us -> 1.88 us  [the longest x1 1.08 us: on_device(): call(functools.partial(place_rest_kernel, [places[n] for n in late]), who...]
  transfers between devices with their start and end apart: 30 -> 30, of which waited for: 9 -> 9; matrix products, arithmetic and copies ran while one was open for 0% -> 0% of each run, Pallas kernels for 11% -> 12%
where the time goes in v4:
time: 63.7 us; the launch traced here: 63.5 us
  starting transfers between devices  36.6 us (57%)
  waiting for transfers between devices  14.5 us (23%)
  Pallas kernels  11.7 us (18%)
  between operations  0.77 us (1%)
    ppermute x12, starting transfers between devices, to_rep(): return lax.ppermute(value, 'rep', pairs)  23.1 us
    ppermute x9, starting transfers between devices, to_chip(): return lax.ppermute(value, 'feat', pairs)  11.9 us
    ppermute x9, waiting for transfers between devices, to_chip(): return lax.ppermute(value, 'feat', pairs)  9.79 us
    ppermute x12, waiting for transfers between devices, to_rep(): return lax.ppermute(value, 'rep', pairs)  4.66 us
    pallas_call x2, Pallas kernels, on_device(): call(functools.partial(gather_kernel, start, run), shape(sets * width, ru...  4.24 us
    pallas_call x1, Pallas kernels, on_device(): call(functools.partial(upper_kernel, factor, core_of if direct else lambd...  3.03 us
    ppermute x9, starting transfers between devices, to_core(): return lax.ppermute(value, 'feat', [(i, i ^ 1) for i in range(feat)])  1.59 us
  transfers between devices with their start and end apart: 30, of which 9 were waited for; matrix products, arithmetic and copies ran while one was open for 0% of the time, Pallas kernels for 12%

profile of v4, /device:TPU:0, one launch (start us, length us, event | category | flops | bytes accessed | tf_op | source)
XLA Modules:
  0.0 63.5 jit_solution(9338640187162271338)
XLA Ops:
  0.6 3.0 %shard_map.93 = (bf16[256,256]{1,0:T(8,128)(2,1)S(1)}, f32[784,256]{1,0:T(8,128)S(1)}, f32[784,256]{1,0:T(8,128)S(1)}, s32[8,5,16,512]{3,2,1,0:T(8,128)S(1)}, bf16[8,128,512]{2,1,0:T(8,128)(2,1)S(1)}) custom-call(bf16[128,256]{1,0:T(8,128)(2,1)} %bitcast.12, s32[5,8,256]{2,1,0:T(8,128)} %bitcast.13, bf16[256,256]{1,0:T(8,128)(2,1)} %bitcast.11, ...), custom_call_target="tpu_custom_call" | custom-call | flops 1000000 | bytes 1000000 | tf_op jit(solution)/shard_map/pallas_call | solution.py:332
  4.2 2.6 %collective-permute-start = (bf16[256,256]{1,0:T(8,128)(2,1)S(1)}, bf16[256,256]{1,0:T(8,128)(2,1)S(1)}, u32[]{:S(2)}, u32[]{:S(2)}) collective-permute-start(bf16[256,256]{1,0:T(8,128)(2,1)S(1)} %get-tuple-element.30.refs_2_.refs_0_), channel_id=1, source_target_pairs={{0,8},{4,12},{8,0},{12,4},{16,24},{20,28},{24,16},{28,20},{1,9},{5... | collective-permute-start | bytes 393224 | tf_op jit(solution)/shard_map/ppermute | solution.py:362
  6.8 1.5 %collective-permute-start.1 = (bf16[256,256]{1,0:T(8,128)(2,1)S(1)}, bf16[256,256]{1,0:T(8,128)(2,1)S(1)}, u32[]{:S(2)}, u32[]{:S(2)}) collective-permute-start(bf16[256,256]{1,0:T(8,128)(2,1)S(1)} %get-tuple-element.30.refs_2_.refs_0_), channel_id=1, source_target_pairs={{0,16},{4,20},{8,24},{12,28},{16,0},{20,4},{24,8},{28,12},{1,17},{... | collective-permute-start | bytes 393224 | tf_op jit(solution)/shard_map/ppermute | solution.py:362
  8.3 2.7 %collective-permute-done.refs_3_.refs_1_ = bf16[256,256]{1,0:T(8,128)(2,1)S(1)} collective-permute-done((bf16[256,256]{1,0:T(8,128)(2,1)S(1)}, bf16[256,256]{1,0:T(8,128)(2,1)S(1)}, u32[]{:S(2)}, u32[]{:S(2)}) %collective-permute-start) | collective-permute-done | bytes 131104 | tf_op jit(solution)/shard_map/ppermute | solution.py:362
  11.0 2.6 %shard_map.94.refs_0_ = bf16[768,1280]{1,0:T(8,128)(2,1)S(1)} custom-call(bf16[8,128,512]{2,1,0:T(8,128)(2,1)S(1)} %get-tuple-element.28.column_ref, s32[8,5,16,512]{3,2,1,0:T(8,128)S(1)} %get-tuple-element.29.word_ref), custom_call_target="tpu_custom_call" | custom-call | flops 3000000000 | bytes 1000000 | tf_op jit(solution)/shard_map/pallas_call | solution.py:351
  13.7 1.5 %collective-permute-done.1.refs_4_.refs_2_ = bf16[256,256]{1,0:T(8,128)(2,1)S(1)} collective-permute-done((bf16[256,256]{1,0:T(8,128)(2,1)S(1)}, bf16[256,256]{1,0:T(8,128)(2,1)S(1)}, u32[]{:S(2)}, u32[]{:S(2)}) %collective-permute-start.1) | collective-permute-done | bytes 131104 | tf_op jit(solution)/shard_map/ppermute | solution.py:362
  15.8 1.6 %collective-permute-start.14 = (bf16[208,256]{1,0:T(8,128)(2,1)S(1)}, bf16[208,256]{1,0:T(8,128)(2,1)S(1)}, u32[]{:S(2)}, u32[]{:S(2)}) collective-permute-start(bf16[208,256]{1,0:T(8,128)(2,1)S(1)} %get-tuple-element.38), channel_id=1, source_target_pairs={{0,1},{1,0},{2,3},{3,2},{4,5},{5,4},{6,7},{7,6},{8,9},{9,8},{10,11... | collective-permute-start | bytes 319496 | tf_op jit(solution)/shard_map/ppermute | solution.py:379
  17.5 2.6 %collective-permute-start.15 = (bf16[208,256]{1,0:T(8,128)(2,1)S(1)}, bf16[208,256]{1,0:T(8,128)(2,1)S(1)}, u32[]{:S(2)}, u32[]{:S(2)}) collective-permute-start(bf16[208,256]{1,0:T(8,128)(2,1)S(1)} %get-tuple-element.39), channel_id=1, source_target_pairs={{0,2},{1,3},{2,0},{3,1},{4,6},{5,7},{6,4},{7,5},{8,10},{9,11},{10,... | collective-permute-start | bytes 319496 | tf_op jit(solution)/shard_map/ppermute | solution.py:379
  20.3 1.6 %shard_map.95.refs_1_ = bf16[768,768]{1,0:T(8,128)(2,1)S(1)} custom-call(bf16[8,128,512]{2,1,0:T(8,128)(2,1)S(1)} %get-tuple-element.28.column_ref, s32[8,5,16,512]{3,2,1,0:T(8,128)S(1)} %get-tuple-element.29.word_ref), custom_call_target="tpu_custom_call" | custom-call | flops 3000000000 | bytes 1000000 | tf_op jit(solution)/shard_map/pallas_call | solution.py:351
  21.9 1.1 %shard_map.96 = (f32[192,256]{1,0:T(8,128)S(1)}, bf16[192,256]{1,0:T(8,128)(2,1)S(1)}, bf16[192,256]{1,0:T(8,128)(2,1)S(1)}, bf16[192,256]{1,0:T(8,128)(2,1)S(1)}) custom-call(bf16[768,1280]{1,0:T(8,128)(2,1)S(1)} %shard_map.94.refs_0_, bf16[768,768]{1,0:T(8,128)(2,1)S(1)} %shard_map.95.refs_1_, bf16[256,256]{1,0:T(8,128)(2,1)S(1)} %get-tuple-element.30.refs_2_.refs_0_, ...), custom_call_target="tpu_custom_call" | custom-call | flops 1000000 | bytes 1000000 | tf_op jit(solution)/shard_map/pallas_call | solution.py:418
  23.8 3.5 %collective-permute-start.8 = (bf16[192,256]{1,0:T(8,128)(2,1)S(1)}, bf16[192,256]{1,0:T(8,128)(2,1)S(1)}, u32[]{:S(2)}, u32[]{:S(2)}) collective-permute-start(bf16[192,256]{1,0:T(8,128)(2,1)S(1)} %get-tuple-element.33), channel_id=1, source_target_pairs={{0,2},{1,3},{2,0},{3,1},{4,6},{5,7},{6,4},{7,5},{8,10},{9,11},{10,... | collective-permute-start | bytes 294920 | tf_op jit(solution)/shard_map/ppermute | solution.py:379
  27.3 1.4 %collective-permute-done.15.refs_1_ = bf16[208,256]{1,0:T(8,128)(2,1)S(1)} collective-permute-done((bf16[208,256]{1,0:T(8,128)(2,1)S(1)}, bf16[208,256]{1,0:T(8,128)(2,1)S(1)}, u32[]{:S(2)}, u32[]{:S(2)}) %collective-permute-start.15) | collective-permute-done | bytes 106528 | tf_op jit(solution)/shard_map/ppermute | solution.py:379
  28.8 0.9 %collective-permute-start.17 = (bf16[64,256]{1,0:T(8,128)(2,1)S(1)}, bf16[64,256]{1,0:T(8,128)(2,1)S(1)}, u32[]{:S(2)}, u32[]{:S(2)}) collective-permute-start(bf16[64,256]{1,0:T(8,128)(2,1)S(1)} %get-tuple-element.42), channel_id=1, source_target_pairs={{0,8},{4,12},{8,0},{12,4},{16,24},{20,28},{24,16},{28,20},{1,9},{5... | collective-permute-start | bytes 98312 | tf_op jit(solution)/shard_map/ppermute | solution.py:362
  29.8 2.7 %collective-permute-start.9 = (bf16[192,256]{1,0:T(8,128)(2,1)S(1)}, bf16[192,256]{1,0:T(8,128)(2,1)S(1)}, u32[]{:S(2)}, u32[]{:S(2)}) collective-permute-start(bf16[192,256]{1,0:T(8,128)(2,1)S(1)} %get-tuple-element.34), channel_id=1, source_target_pairs={{0,3},{1,2},{2,1},{3,0},{4,7},{5,6},{6,5},{7,4},{8,11},{9,10},{10,... | collective-permute-start | bytes 294920 | tf_op jit(solution)/shard_map/ppermute | solution.py:379
  32.4 1.5 %collective-permute-start.18 = (bf16[64,256]{1,0:T(8,128)(2,1)S(1)}, bf16[64,256]{1,0:T(8,128)(2,1)S(1)}, u32[]{:S(2)}, u32[]{:S(2)}) collective-permute-start(bf16[64,256]{1,0:T(8,128)(2,1)S(1)} %get-tuple-element.43), channel_id=1, source_target_pairs={{0,16},{4,20},{8,24},{12,28},{16,0},{20,4},{24,8},{28,12},{1,17},{... | collective-permute-start | bytes 98312 | tf_op jit(solution)/shard_map/ppermute | solution.py:362
  34.0 1.8 %collective-permute-start.19 = (bf16[64,256]{1,0:T(8,128)(2,1)S(1)}, bf16[64,256]{1,0:T(8,128)(2,1)S(1)}, u32[]{:S(2)}, u32[]{:S(2)}) collective-permute-start(bf16[64,256]{1,0:T(8,128)(2,1)S(1)} %get-tuple-element.44), channel_id=1, source_target_pairs={{0,24},{4,28},{8,16},{12,20},{16,8},{20,12},{24,0},{28,4},{1,25},{... | collective-permute-start | bytes 98312 | tf_op jit(solution)/shard_map/ppermute | solution.py:362
  36.4 2.4 %collective-permute-done.19.refs_10_ = bf16[64,256]{1,0:T(8,128)(2,1)S(1)} collective-permute-done((bf16[64,256]{1,0:T(8,128)(2,1)S(1)}, bf16[64,256]{1,0:T(8,128)(2,1)S(1)}, u32[]{:S(2)}, u32[]{:S(2)}) %collective-permute-start.19) | collective-permute-done | bytes 32800 | tf_op jit(solution)/shard_map/ppermute | solution.py:362
  39.0 4.9 %collective-permute-start.20 = (bf16[64,256]{1,0:T(8,128)(2,1)S(1)}, bf16[64,256]{1,0:T(8,128)(2,1)S(1)}, u32[]{:S(2)}, u32[]{:S(2)}) collective-permute-start(bf16[64,256]{1,0:T(8,128)(2,1)S(1)} %get-tuple-element.45.refs_0_), channel_id=1, source_target_pairs={{0,1},{1,0},{2,3},{3,2},{4,5},{5,4},{6,7},{7,6},{8,9},{9,8},{10,11... | collective-permute-start | bytes 98312 | tf_op jit(solution)/shard_map/ppermute | solution.py:379
  43.9 0.9 %collective-permute-start.21 = (bf16[64,256]{1,0:T(8,128)(2,1)S(1)}, bf16[64,256]{1,0:T(8,128)(2,1)S(1)}, u32[]{:S(2)}, u32[]{:S(2)}) collective-permute-start(bf16[64,256]{1,0:T(8,128)(2,1)S(1)} %get-tuple-element.45.refs_0_), channel_id=1, source_target_pairs={{0,2},{1,3},{2,0},{3,1},{4,6},{5,7},{6,4},{7,5},{8,10},{9,11},{10,... | collective-permute-start | bytes 98312 | tf_op jit(solution)/shard_map/ppermute | solution.py:379
  44.9 1.5 %collective-permute-start.22 = (bf16[64,256]{1,0:T(8,128)(2,1)S(1)}, bf16[64,256]{1,0:T(8,128)(2,1)S(1)}, u32[]{:S(2)}, u32[]{:S(2)}) collective-permute-start(bf16[64,256]{1,0:T(8,128)(2,1)S(1)} %get-tuple-element.45.refs_0_), channel_id=1, source_target_pairs={{0,3},{1,2},{2,1},{3,0},{4,7},{5,6},{6,5},{7,4},{8,11},{9,10},{10,... | collective-permute-start | bytes 98312 | tf_op jit(solution)/shard_map/ppermute | solution.py:379
  46.4 1.1 %collective-permute-start.10 = (bf16[192,256]{1,0:T(8,128)(2,1)S(1)}, bf16[192,256]{1,0:T(8,128)(2,1)S(1)}, u32[]{:S(2)}, u32[]{:S(2)}) collective-permute-start(bf16[192,256]{1,0:T(8,128)(2,1)S(1)} %shard_map.97.refs_0_), channel_id=1, source_target_pairs={{0,1},{1,0},{2,3},{3,2},{4,5},{5,4},{6,7},{7,6},{8,9},{9,8},{10,11... | collective-permute-start | bytes 294920 | tf_op jit(solution)/shard_map/ppermute | solution.py:379
  47.5 1.8 %collective-permute-start.11 = (bf16[192,256]{1,0:T(8,128)(2,1)S(1)}, bf16[192,256]{1,0:T(8,128)(2,1)S(1)}, u32[]{:S(2)}, u32[]{:S(2)}) collective-permute-start(bf16[192,256]{1,0:T(8,128)(2,1)S(1)} %shard_map.97.refs_0_), channel_id=1, source_target_pairs={{0,2},{1,3},{2,0},{3,1},{4,6},{5,7},{6,4},{7,5},{8,10},{9,11},{10,... | collective-permute-start | bytes 294920 | tf_op jit(solution)/shard_map/ppermute | solution.py:379
  49.4 1.3 %collective-permute-done.22.refs_3_ = bf16[64,256]{1,0:T(8,128)(2,1)S(1)} collective-permute-done((bf16[64,256]{1,0:T(8,128)(2,1)S(1)}, bf16[64,256]{1,0:T(8,128)(2,1)S(1)}, u32[]{:S(2)}, u32[]{:S(2)}) %collective-permute-start.22) | collective-permute-done | bytes 32800 | tf_op jit(solution)/shard_map/ppermute | solution.py:379
  50.7 1.1 %collective-permute-start.24 = (bf16[4,48,256]{2,1,0:T(8,128)(2,1)S(1)}, bf16[4,48,256]{2,1,0:T(8,128)(2,1)S(1)}, u32[]{:S(2)}, u32[]{:S(2)}) collective-permute-start(bf16[4,48,256]{2,1,0:T(8,128)(2,1)S(1)} %get-tuple-element.46.refs_0_), channel_id=1, source_target_pairs={{0,8},{4,12},{8,0},{12,4},{16,24},{20,28},{24,16},{28,20},{1,9},{5... | collective-permute-start | bytes 294920 | tf_op jit(solution)/shard_map/ppermute | solution.py:362
  51.8 1.4 %collective-permute-start.25 = (bf16[4,48,256]{2,1,0:T(8,128)(2,1)S(1)}, bf16[4,48,256]{2,1,0:T(8,128)(2,1)S(1)}, u32[]{:S(2)}, u32[]{:S(2)}) collective-permute-start(bf16[4,48,256]{2,1,0:T(8,128)(2,1)S(1)} %get-tuple-element.46.refs_0_), channel_id=1, source_target_pairs={{0,16},{4,20},{8,24},{12,28},{16,0},{20,4},{24,8},{28,12},{1,17},{... | collective-permute-start | bytes 294920 | tf_op jit(solution)/shard_map/ppermute | solution.py:362
  53.3 1.0 %collective-permute-start.26 = (bf16[4,48,256]{2,1,0:T(8,128)(2,1)S(1)}, bf16[4,48,256]{2,1,0:T(8,128)(2,1)S(1)}, u32[]{:S(2)}, u32[]{:S(2)}) collective-permute-start(bf16[4,48,256]{2,1,0:T(8,128)(2,1)S(1)} %get-tuple-element.46.refs_0_), channel_id=1, source_target_pairs={{0,24},{4,28},{8,16},{12,20},{16,8},{20,12},{24,0},{28,4},{1,25},{... | collective-permute-start | bytes 294920 | tf_op jit(solution)/shard_map/ppermute | solution.py:362
  54.3 1.4 %collective-permute-start.12 = (bf16[192,256]{1,0:T(8,128)(2,1)S(1)}, bf16[192,256]{1,0:T(8,128)(2,1)S(1)}, u32[]{:S(2)}, u32[]{:S(2)}) collective-permute-start(bf16[192,256]{1,0:T(8,128)(2,1)S(1)} %shard_map.97.refs_0_), channel_id=1, source_target_pairs={{0,3},{1,2},{2,1},{3,0},{4,7},{5,6},{6,5},{7,4},{8,11},{9,10},{10,... | collective-permute-start | bytes 294920 | tf_op jit(solution)/shard_map/ppermute | solution.py:379
  56.5 2.3 %collective-permute-done.26.refs_2_ = bf16[4,48,256]{2,1,0:T(8,128)(2,1)S(1)} collective-permute-done((bf16[4,48,256]{2,1,0:T(8,128)(2,1)S(1)}, bf16[4,48,256]{2,1,0:T(8,128)(2,1)S(1)}, u32[]{:S(2)}, u32[]{:S(2)}) %collective-permute-start.26) | collective-permute-done | bytes 98336 | tf_op jit(solution)/shard_map/ppermute | solution.py:362
  58.8 1.9 %collective-permute-done.12.refs_3_ = bf16[192,256]{1,0:T(8,128)(2,1)S(1)} collective-permute-done((bf16[192,256]{1,0:T(8,128)(2,1)S(1)}, bf16[192,256]{1,0:T(8,128)(2,1)S(1)}, u32[]{:S(2)}, u32[]{:S(2)}) %collective-permute-start.12) | collective-permute-done | bytes 98336 | tf_op jit(solution)/shard_map/ppermute | solution.py:379
  60.7 0.9 %shard_map.98 = f32[4,192,256]{2,1,0:T(8,128)} custom-call(bf16[192,256]{1,0:T(8,128)(2,1)S(1)} %shard_map.97.refs_0_, bf16[192,256]{1,0:T(8,128)(2,1)S(1)} %collective-permute-done.10.refs_1_, bf16[192,256]{1,0:T(8,128)(2,1)S(1)} %collective-permute-done.11.refs_2_, bf16[192,256]{1,0:T(8,128)(2,1)S(1)} %collective-permute-done.12.refs_3_), custom_call_target="tpu_custom_call" | custom-call | flops 1000000 | bytes 1000000 | tf_op jit(solution)/shard_map/pallas_call | solution.py:450
  61.6 0.8 %shard_map.103 = (f32[2,4,4,48,256]{4,3,2,1,0:T(8,128)}, f32[256]{0:T(256)}, f32[256]{0:T(256)}) custom-call(bf16[4,48,256]{2,1,0:T(8,128)(2,1)S(1)} %get-tuple-element.46.refs_0_, bf16[4,48,256]{2,1,0:T(8,128)(2,1)S(1)} %collective-permute-done.23.refs_1_, f32[8,256]{1,0:T(8,128)S(1)} %get-tuple-element.47.refs_2_, f32[8,256]{1,0:T(8,128)S(1)} %get-tuple-element.48.refs_3_), custom_call_target="tpu_custom_call" | custom-call | flops 1000000 | bytes 1000000 | tf_op jit(solution)/shard_map/pallas_call | solution.py:476
  62.5 1.1 %shard_map.104 = f32[2,4,4,48,256]{4,3,2,1,0:T(8,128)} custom-call(f32[2,4,4,48,256]{4,3,2,1,0:T(8,128)} %get-tuple-element.50.begun, bf16[4,48,256]{2,1,0:T(8,128)(2,1)S(1)} %collective-permute-done.24.refs_0_, bf16[4,48,256]{2,1,0:T(8,128)(2,1)S(1)} %collective-permute-done.25.refs_1_, ...), custom_call_target="tpu_custom_call", output_to_operand_aliasing={{}: (0, {})} | custom-call | flops 1000000 | bytes 1000000 | tf_op jit(solution)/shard_map/pallas_call | solution.py:485
  (40 shorter events, 3.9 us)
Async XLA Ops:
  3.7 12.0 %collective-permute-start.13 = (f32[784,256]{1,0:T(8,128)S(1)}, f32[784,256]{1,0:T(8,128)S(1)}, u32[]{:S(2)}, u32[]{:S(2)}) collective-permute-start(f32[784,256]{1,0:T(8,128)S(1)} %get-tuple-element.36), channel_id=1, source_target_pairs={{0,4},{4,0},{8,12},{12,8},{16,20},{20,16},{24,28},{28,24},{1,5},{5... | collective-permute-start | bytes 2408456 | tf_op jit(solution)/shard_map/ppermute | solution.py:365
  4.2 6.8 %collective-permute-start = (bf16[256,256]{1,0:T(8,128)(2,1)S(1)}, bf16[256,256]{1,0:T(8,128)(2,1)S(1)}, u32[]{:S(2)}, u32[]{:S(2)}) collective-permute-start(bf16[256,256]{1,0:T(8,128)(2,1)S(1)} %get-tuple-element.30.refs_2_.refs_0_), channel_id=1, source_target_pairs={{0,8},{4,12},{8,0},{12,4},{16,24},{20,28},{24,16},{28,20},{1,9},{5... | collective-permute-start | bytes 393224 | tf_op jit(solution)/shard_map/ppermute | solution.py:362
  6.8 8.4 %collective-permute-start.1 = (bf16[256,256]{1,0:T(8,128)(2,1)S(1)}, bf16[256,256]{1,0:T(8,128)(2,1)S(1)}, u32[]{:S(2)}, u32[]{:S(2)}) collective-permute-start(bf16[256,256]{1,0:T(8,128)(2,1)S(1)} %get-tuple-element.30.refs_2_.refs_0_), channel_id=1, source_target_pairs={{0,16},{4,20},{8,24},{12,28},{16,0},{20,4},{24,8},{28,12},{1,17},{... | collective-permute-start | bytes 393224 | tf_op jit(solution)/shard_map/ppermute | solution.py:362
  8.3 6.8 %collective-permute-start.2 = (bf16[256,256]{1,0:T(8,128)(2,1)S(1)}, bf16[256,256]{1,0:T(8,128)(2,1)S(1)}, u32[]{:S(2)}, u32[]{:S(2)}) collective-permute-start(bf16[256,256]{1,0:T(8,128)(2,1)S(1)} %get-tuple-element.30.refs_2_.refs_0_), channel_id=1, source_target_pairs={{0,24},{4,28},{8,16},{12,20},{16,8},{20,12},{24,0},{28,4},{1,25},{... | collective-permute-start | bytes 393224 | tf_op jit(solution)/shard_map/ppermute | solution.py:362
  8.3 9.1 %collective-permute-start.3 = (bf16[256,256]{1,0:T(8,128)(2,1)S(1)}, bf16[256,256]{1,0:T(8,128)(2,1)S(1)}, u32[]{:S(2)}, u32[]{:S(2)}) collective-permute-start(bf16[256,256]{1,0:T(8,128)(2,1)S(1)} %get-tuple-element.30.refs_2_.refs_0_), channel_id=1, source_target_pairs={{0,4},{4,0},{8,12},{12,8},{16,20},{20,16},{24,28},{28,24},{1,5},{5... | collective-permute-start | bytes 393224 | tf_op jit(solution)/shard_map/ppermute | solution.py:365
  11.0 9.0 %collective-permute-start.4 = (bf16[256,256]{1,0:T(8,128)(2,1)S(1)}, bf16[256,256]{1,0:T(8,128)(2,1)S(1)}, u32[]{:S(2)}, u32[]{:S(2)}) collective-permute-start(bf16[256,256]{1,0:T(8,128)(2,1)S(1)} %collective-permute-done.refs_3_.refs_1_), channel_id=1, source_target_pairs={{0,4},{4,0},{8,12},{12,8},{16,20},{20,16},{24,28},{28,24},{1,5},{5... | collective-permute-start | bytes 393224 | tf_op jit(solution)/shard_map/ppermute | solution.py:365
  15.2 6.8 %collective-permute-start.5 = (bf16[256,256]{1,0:T(8,128)(2,1)S(1)}, bf16[256,256]{1,0:T(8,128)(2,1)S(1)}, u32[]{:S(2)}, u32[]{:S(2)}) collective-permute-start(bf16[256,256]{1,0:T(8,128)(2,1)S(1)} %collective-permute-done.1.refs_4_.refs_2_), channel_id=1, source_target_pairs={{0,4},{4,0},{8,12},{12,8},{16,20},{20,16},{24,28},{28,24},{1,5},{5... | collective-permute-start | bytes 393224 | tf_op jit(solution)/shard_map/ppermute | solution.py:365
  15.2 6.8 %collective-permute-start.6 = (bf16[256,256]{1,0:T(8,128)(2,1)S(1)}, bf16[256,256]{1,0:T(8,128)(2,1)S(1)}, u32[]{:S(2)}, u32[]{:S(2)}) collective-permute-start(bf16[256,256]{1,0:T(8,128)(2,1)S(1)} %collective-permute-done.2.refs_5_.refs_3_), channel_id=1, source_target_pairs={{0,4},{4,0},{8,12},{12,8},{16,20},{20,16},{24,28},{28,24},{1,5},{5... | collective-permute-start | bytes 393224 | tf_op jit(solution)/shard_map/ppermute | solution.py:365
  15.8 11.5 %collective-permute-start.14 = (bf16[208,256]{1,0:T(8,128)(2,1)S(1)}, bf16[208,256]{1,0:T(8,128)(2,1)S(1)}, u32[]{:S(2)}, u32[]{:S(2)}) collective-permute-start(bf16[208,256]{1,0:T(8,128)(2,1)S(1)} %get-tuple-element.38), channel_id=1, source_target_pairs={{0,1},{1,0},{2,3},{3,2},{4,5},{5,4},{6,7},{7,6},{8,9},{9,8},{10,11... | collective-permute-start | bytes 319496 | tf_op jit(solution)/shard_map/ppermute | solution.py:379
  17.5 11.3 %collective-permute-start.15 = (bf16[208,256]{1,0:T(8,128)(2,1)S(1)}, bf16[208,256]{1,0:T(8,128)(2,1)S(1)}, u32[]{:S(2)}, u32[]{:S(2)}) collective-permute-start(bf16[208,256]{1,0:T(8,128)(2,1)S(1)} %get-tuple-element.39), channel_id=1, source_target_pairs={{0,2},{1,3},{2,0},{3,1},{4,6},{5,7},{6,4},{7,5},{8,10},{9,11},{10,... | collective-permute-start | bytes 319496 | tf_op jit(solution)/shard_map/ppermute | solution.py:379
  20.0 8.7 %collective-permute-start.16 = (bf16[208,256]{1,0:T(8,128)(2,1)S(1)}, bf16[208,256]{1,0:T(8,128)(2,1)S(1)}, u32[]{:S(2)}, u32[]{:S(2)}) collective-permute-start(bf16[208,256]{1,0:T(8,128)(2,1)S(1)} %get-tuple-element.40), channel_id=1, source_target_pairs={{0,3},{1,2},{2,1},{3,0},{4,7},{5,6},{6,5},{7,4},{8,11},{9,10},{10,... | collective-permute-start | bytes 319496 | tf_op jit(solution)/shard_map/ppermute | solution.py:379
  23.1 21.8 %collective-permute-start.7 = (bf16[192,256]{1,0:T(8,128)(2,1)S(1)}, bf16[192,256]{1,0:T(8,128)(2,1)S(1)}, u32[]{:S(2)}, u32[]{:S(2)}) collective-permute-start(bf16[192,256]{1,0:T(8,128)(2,1)S(1)} %get-tuple-element.32), channel_id=1, source_target_pairs={{0,1},{1,0},{2,3},{3,2},{4,5},{5,4},{6,7},{7,6},{8,9},{9,8},{10,11... | collective-permute-start | bytes 294920 | tf_op jit(solution)/shard_map/ppermute | solution.py:379
  23.8 22.6 %collective-permute-start.8 = (bf16[192,256]{1,0:T(8,128)(2,1)S(1)}, bf16[192,256]{1,0:T(8,128)(2,1)S(1)}, u32[]{:S(2)}, u32[]{:S(2)}) collective-permute-start(bf16[192,256]{1,0:T(8,128)(2,1)S(1)} %get-tuple-element.33), channel_id=1, source_target_pairs={{0,2},{1,3},{2,0},{3,1},{4,6},{5,7},{6,4},{7,5},{8,10},{9,11},{10,... | collective-permute-start | bytes 294920 | tf_op jit(solution)/shard_map/ppermute | solution.py:379
  28.8 5.2 %collective-permute-start.17 = (bf16[64,256]{1,0:T(8,128)(2,1)S(1)}, bf16[64,256]{1,0:T(8,128)(2,1)S(1)}, u32[]{:S(2)}, u32[]{:S(2)}) collective-permute-start(bf16[64,256]{1,0:T(8,128)(2,1)S(1)} %get-tuple-element.42), channel_id=1, source_target_pairs={{0,8},{4,12},{8,0},{12,4},{16,24},{20,28},{24,16},{28,20},{1,9},{5... | collective-permute-start | bytes 98312 | tf_op jit(solution)/shard_map/ppermute | solution.py:362
  29.8 16.6 %collective-permute-start.9 = (bf16[192,256]{1,0:T(8,128)(2,1)S(1)}, bf16[192,256]{1,0:T(8,128)(2,1)S(1)}, u32[]{:S(2)}, u32[]{:S(2)}) collective-permute-start(bf16[192,256]{1,0:T(8,128)(2,1)S(1)} %get-tuple-element.34), channel_id=1, source_target_pairs={{0,3},{1,2},{2,1},{3,0},{4,7},{5,6},{6,5},{7,4},{8,11},{9,10},{10,... | collective-permute-start | bytes 294920 | tf_op jit(solution)/shard_map/ppermute | solution.py:379
  32.4 3.9 %collective-permute-start.18 = (bf16[64,256]{1,0:T(8,128)(2,1)S(1)}, bf16[64,256]{1,0:T(8,128)(2,1)S(1)}, u32[]{:S(2)}, u32[]{:S(2)}) collective-permute-start(bf16[64,256]{1,0:T(8,128)(2,1)S(1)} %get-tuple-element.43), channel_id=1, source_target_pairs={{0,16},{4,20},{8,24},{12,28},{16,0},{20,4},{24,8},{28,12},{1,17},{... | collective-permute-start | bytes 98312 | tf_op jit(solution)/shard_map/ppermute | solution.py:362
  34.0 4.8 %collective-permute-start.19 = (bf16[64,256]{1,0:T(8,128)(2,1)S(1)}, bf16[64,256]{1,0:T(8,128)(2,1)S(1)}, u32[]{:S(2)}, u32[]{:S(2)}) collective-permute-start(bf16[64,256]{1,0:T(8,128)(2,1)S(1)} %get-tuple-element.44), channel_id=1, source_target_pairs={{0,24},{4,28},{8,16},{12,20},{16,8},{20,12},{24,0},{28,4},{1,25},{... | collective-permute-start | bytes 98312 | tf_op jit(solution)/shard_map/ppermute | solution.py:362
  39.0 10.4 %collective-permute-start.20 = (bf16[64,256]{1,0:T(8,128)(2,1)S(1)}, bf16[64,256]{1,0:T(8,128)(2,1)S(1)}, u32[]{:S(2)}, u32[]{:S(2)}) collective-permute-start(bf16[64,256]{1,0:T(8,128)(2,1)S(1)} %get-tuple-element.45.refs_0_), channel_id=1, source_target_pairs={{0,1},{1,0},{2,3},{3,2},{4,5},{5,4},{6,7},{7,6},{8,9},{9,8},{10,11... | collective-permute-start | bytes 98312 | tf_op jit(solution)/shard_map/ppermute | solution.py:379
  43.9 5.5 %collective-permute-start.21 = (bf16[64,256]{1,0:T(8,128)(2,1)S(1)}, bf16[64,256]{1,0:T(8,128)(2,1)S(1)}, u32[]{:S(2)}, u32[]{:S(2)}) collective-permute-start(bf16[64,256]{1,0:T(8,128)(2,1)S(1)} %get-tuple-element.45.refs_0_), channel_id=1, source_target_pairs={{0,2},{1,3},{2,0},{3,1},{4,6},{5,7},{6,4},{7,5},{8,10},{9,11},{10,... | collective-permute-start | bytes 98312 | tf_op jit(solution)/shard_map/ppermute | solution.py:379
  44.9 5.8 %collective-permute-start.22 = (bf16[64,256]{1,0:T(8,128)(2,1)S(1)}, bf16[64,256]{1,0:T(8,128)(2,1)S(1)}, u32[]{:S(2)}, u32[]{:S(2)}) collective-permute-start(bf16[64,256]{1,0:T(8,128)(2,1)S(1)} %get-tuple-element.45.refs_0_), channel_id=1, source_target_pairs={{0,3},{1,2},{2,1},{3,0},{4,7},{5,6},{6,5},{7,4},{8,11},{9,10},{10,... | collective-permute-start | bytes 98312 | tf_op jit(solution)/shard_map/ppermute | solution.py:379
  46.4 7.8 %collective-permute-start.10 = (bf16[192,256]{1,0:T(8,128)(2,1)S(1)}, bf16[192,256]{1,0:T(8,128)(2,1)S(1)}, u32[]{:S(2)}, u32[]{:S(2)}) collective-permute-start(bf16[192,256]{1,0:T(8,128)(2,1)S(1)} %shard_map.97.refs_0_), channel_id=1, source_target_pairs={{0,1},{1,0},{2,3},{3,2},{4,5},{5,4},{6,7},{7,6},{8,9},{9,8},{10,11... | collective-permute-start | bytes 294920 | tf_op jit(solution)/shard_map/ppermute | solution.py:379
  47.5 8.2 %collective-permute-start.11 = (bf16[192,256]{1,0:T(8,128)(2,1)S(1)}, bf16[192,256]{1,0:T(8,128)(2,1)S(1)}, u32[]{:S(2)}, u32[]{:S(2)}) collective-permute-start(bf16[192,256]{1,0:T(8,128)(2,1)S(1)} %shard_map.97.refs_0_), channel_id=1, source_target_pairs={{0,2},{1,3},{2,0},{3,1},{4,6},{5,7},{6,4},{7,5},{8,10},{9,11},{10,... | collective-permute-start | bytes 294920 | tf_op jit(solution)/shard_map/ppermute | solution.py:379
  50.7 5.0 %collective-permute-start.24 = (bf16[4,48,256]{2,1,0:T(8,128)(2,1)S(1)}, bf16[4,48,256]{2,1,0:T(8,128)(2,1)S(1)}, u32[]{:S(2)}, u32[]{:S(2)}) collective-permute-start(bf16[4,48,256]{2,1,0:T(8,128)(2,1)S(1)} %get-tuple-element.46.refs_0_), channel_id=1, source_target_pairs={{0,8},{4,12},{8,0},{12,4},{16,24},{20,28},{24,16},{28,20},{1,9},{5... | collective-permute-start | bytes 294920 | tf_op jit(solution)/shard_map/ppermute | solution.py:362
  51.8 4.6 %collective-permute-start.25 = (bf16[4,48,256]{2,1,0:T(8,128)(2,1)S(1)}, bf16[4,48,256]{2,1,0:T(8,128)(2,1)S(1)}, u32[]{:S(2)}, u32[]{:S(2)}) collective-permute-start(bf16[4,48,256]{2,1,0:T(8,128)(2,1)S(1)} %get-tuple-element.46.refs_0_), channel_id=1, source_target_pairs={{0,16},{4,20},{8,24},{12,28},{16,0},{20,4},{24,8},{28,12},{1,17},{... | collective-permute-start | bytes 294920 | tf_op jit(solution)/shard_map/ppermute | solution.py:362
  53.3 5.5 %collective-permute-start.26 = (bf16[4,48,256]{2,1,0:T(8,128)(2,1)S(1)}, bf16[4,48,256]{2,1,0:T(8,128)(2,1)S(1)}, u32[]{:S(2)}, u32[]{:S(2)}) collective-permute-start(bf16[4,48,256]{2,1,0:T(8,128)(2,1)S(1)} %get-tuple-element.46.refs_0_), channel_id=1, source_target_pairs={{0,24},{4,28},{8,16},{12,20},{16,8},{20,12},{24,0},{28,4},{1,25},{... | collective-permute-start | bytes 294920 | tf_op jit(solution)/shard_map/ppermute | solution.py:362
  54.3 6.4 %collective-permute-start.12 = (bf16[192,256]{1,0:T(8,128)(2,1)S(1)}, bf16[192,256]{1,0:T(8,128)(2,1)S(1)}, u32[]{:S(2)}, u32[]{:S(2)}) collective-permute-start(bf16[192,256]{1,0:T(8,128)(2,1)S(1)} %shard_map.97.refs_0_), channel_id=1, source_target_pairs={{0,3},{1,2},{2,1},{3,0},{4,7},{5,6},{6,5},{7,4},{8,11},{9,10},{10,... | collective-permute-start | bytes 294920 | tf_op jit(solution)/shard_map/ppermute | solution.py:379
  55.7 5.9 %collective-permute-start.23 = (bf16[4,48,256]{2,1,0:T(8,128)(2,1)S(1)}, bf16[4,48,256]{2,1,0:T(8,128)(2,1)S(1)}, u32[]{:S(2)}, u32[]{:S(2)}) collective-permute-start(bf16[4,48,256]{2,1,0:T(8,128)(2,1)S(1)} %get-tuple-element.46.refs_0_), channel_id=1, source_target_pairs={{0,4},{4,0},{8,12},{12,8},{16,20},{20,16},{24,28},{28,24},{1,5},{5... | collective-permute-start | bytes 294920 | tf_op jit(solution)/shard_map/ppermute | solution.py:365
  55.7 6.7 %collective-permute-start.27 = (bf16[4,48,256]{2,1,0:T(8,128)(2,1)S(1)}, bf16[4,48,256]{2,1,0:T(8,128)(2,1)S(1)}, u32[]{:S(2)}, u32[]{:S(2)}) collective-permute-start(bf16[4,48,256]{2,1,0:T(8,128)(2,1)S(1)} %collective-permute-done.24.refs_0_), channel_id=1, source_target_pairs={{0,4},{4,0},{8,12},{12,8},{16,20},{20,16},{24,28},{28,24},{1,5},{5... | collective-permute-start | bytes 294920 | tf_op jit(solution)/shard_map/ppermute | solution.py:365
  56.5 6.0 %collective-permute-start.28 = (bf16[4,48,256]{2,1,0:T(8,128)(2,1)S(1)}, bf16[4,48,256]{2,1,0:T(8,128)(2,1)S(1)}, u32[]{:S(2)}, u32[]{:S(2)}) collective-permute-start(bf16[4,48,256]{2,1,0:T(8,128)(2,1)S(1)} %collective-permute-done.25.refs_1_), channel_id=1, source_target_pairs={{0,4},{4,0},{8,12},{12,8},{16,20},{20,16},{24,28},{28,24},{1,5},{5... | collective-permute-start | bytes 294920 | tf_op jit(solution)/shard_map/ppermute | solution.py:365
  58.8 3.7 %collective-permute-start.29 = (bf16[4,48,256]{2,1,0:T(8,128)(2,1)S(1)}, bf16[4,48,256]{2,1,0:T(8,128)(2,1)S(1)}, u32[]{:S(2)}, u32[]{:S(2)}) collective-permute-start(bf16[4,48,256]{2,1,0:T(8,128)(2,1)S(1)} %collective-permute-done.26.refs_2_), channel_id=1, source_target_pairs={{0,4},{4,0},{8,12},{12,8},{16,20},{20,16},{24,28},{28,24},{1,5},{5... | collective-permute-start | bytes 294920 | tf_op jit(solution)/shard_map/ppermute | solution.py:365
